TPU v7x, 128 devices: a whole 4x4x4 slice. The times are simulated.
128 devices in a mesh: fsdp: 32 (over z, y, x_hi), sp: 4 (over x_lo, core).
Axes of the slice: x: 4 (x_hi: 2, x_lo: 2; x = x_hi * 2 + x_lo), y: 4, z: 4, core: 2. Of those that a mesh axis runs over, the one named last changes fastest.
Arguments:
- tokens: bfloat16 [32, 512, 1536], P('fsdp', 'sp'), may hold values from -6 to 6
- modulation: float32 [32, 1, 6, 1536], P('fsdp'), may hold values from -4 to 4
- w_qkv: bfloat16 [1, 1536, 3, 1536], P(None, 'fsdp', None, 'sp'), may hold values from -0.15625 to 0.15625
- w_out: bfloat16 [1, 1536, 1536], P(None, 'sp', 'fsdp'), may hold values from -0.15625 to 0.15625
- w_in: bfloat16 [1, 1536, 6144], P(None, 'fsdp', 'sp'), may hold values from -0.15625 to 0.15625
- w_back: bfloat16 [1, 6144, 1536], P(None, 'sp', 'fsdp'), may hold values from -0.078125 to 0.078125
- out_grad: bfloat16 [32, 512, 1536], P('fsdp', 'sp'), may hold values from -6 to 6
Outputs:
- final_out: bfloat16 [32, 512, 1536], P('fsdp', 'sp')
- input_grad: float32 [32, 512, 1536], P('fsdp', 'sp')
- grad_qkv: float32 [1, 1536, 3, 1536], P(None, 'fsdp', None, 'sp')
- grad_out: float32 [1, 1536, 1536], P(None, 'sp', 'fsdp')
- grad_in: float32 [1, 1536, 6144], P(None, 'fsdp', 'sp')
- grad_back: float32 [1, 6144, 1536], P(None, 'sp', 'fsdp')
All inputs are finite; a program needn't handle non-finite values.
Results may differ from a plain program's by a relative error of at most 0.03.
Values may be sent and summed in bfloat16 or wider, within the bound.
A program may use at most 128 MiB of HBM per device.

v0:
```python
import math

import jax
import jax.numpy as jnp
from jax import lax
from jax.sharding import Mesh
from jax.sharding import PartitionSpec as P

HEAD_DIM = 128
SP = ("sp_0", "sp_1")


ln_eps = 1e-06
temper = 2.5
block_limit = 512


def laid_out(blocks, dim):
    blocks = jnp.moveaxis(blocks, 0, dim)
    lengths = blocks.shape
    return blocks.reshape(*lengths[:dim], lengths[dim] * lengths[dim + 1], *lengths[dim + 2 :])


def one_gather(arrays, axis, dims):
    ravelled = jnp.concatenate([a.reshape(-1) for a in arrays])
    lines, at, gathered = lax.all_gather(ravelled, axis), 0, []
    for a, dim in zip(arrays, dims):
        blocks = lines[:, at : at + a.size].reshape(-1, *a.shape)
        gathered.append(laid_out(blocks, dim))
        at += a.size
    return tuple(gathered)


def own_block(blocks, axes, turns):
    inside = blocks.shape[1:]
    blocks = blocks.reshape(*(lax.axis_size(a) for a in axes), *inside)
    blocks = jnp.moveaxis(blocks, turns, range(len(axes))).reshape(-1, *inside)
    for k in turns:
        blocks = lax.psum_scatter(blocks, axes[k], scatter_dimension=0, tiled=True)
    return blocks[0]


def cut_along(value, dim, count):
    return jnp.stack(jnp.split(value, count, axis=dim))


def sum_by_axis(value, axes, turns, dim):
    count = lax.axis_size(axes)
    return own_block(cut_along(value, dim, count), axes, turns)


def sum_packed(arrays, axis, dims):
    count = lax.axis_size(axis)
    blocks = [cut_along(a, dim, count) for a, dim in zip(arrays, dims)]
    lines = jnp.concatenate([b.reshape(count, -1) for b in blocks], axis=1)
    ravelled, at, gathered = lax.psum_scatter(lines, axis, tiled=True)[0], 0, []
    for b in blocks:
        part = b[0]
        gathered.append(ravelled[at : at + part.size].reshape(part.shape))
        at += part.size
    return tuple(gathered)


def normalize(stream):
    mean_part = jnp.mean(stream, axis=-1, keepdims=True)
    centred = stream - mean_part
    rstd = lax.rsqrt(jnp.mean(centred * centred, axis=-1, keepdims=True) + ln_eps)
    return (centred * rstd, rstd)


def norm_back(normed, rstd, incoming):
    first = jnp.mean(incoming, axis=-1, keepdims=True)
    second = jnp.mean(incoming * normed, axis=-1, keepdims=True)
    return rstd * (incoming - first - normed * second)


def gelu_tanh(hidden):
    return jax.nn.gelu(hidden, approximate=True)


def project(left, weight):
    flat_rows = left.reshape(-1, left.shape[-1])
    result = jnp.dot(flat_rows, weight, preferred_element_type=jnp.float32)
    return result.reshape(left.shape[:-1] + (weight.shape[1],))


def project_back(left, weight):
    flat_rows = left.reshape(-1, left.shape[-1])
    result = lax.dot_general(
        flat_rows, weight, (((1,), (1,)), ((), ())), preferred_element_type=jnp.float32
    )
    return result.reshape(left.shape[:-1] + (weight.shape[0],))


def weight_term(left, right, grad_scale):
    left_rows = left.reshape(-1, left.shape[-1])
    right_rows = right.reshape(-1, right.shape[-1])

    def term_rows(start, count):
        column_part = lax.dynamic_slice_in_dim(left_rows, start, count, 1)
        product = lax.dot_general(
            column_part, right_rows, (((0,), (0,)), ((), ())), preferred_element_type=jnp.float32
        )
        return product * grad_scale

    return term_rows


def split_heads(packed, head_count):
    return packed.reshape(packed.shape[:-1] + (head_count, packed.shape[-1] // head_count))


def heads_major(tensor):
    videos, seq_len, head_count, head_width = tensor.shape
    return tensor.transpose(0, 2, 1, 3).reshape(videos * head_count, seq_len, head_width)


def heads_minor(tensor, videos):
    merged, seq_len, head_width = tensor.shape
    return tensor.reshape(videos, merged // videos, seq_len, head_width).transpose(0, 2, 1, 3)


def attend_head(triple):
    queries, key_rows, values = triple
    seq_len, head_width = queries.shape
    block_size = min(block_limit, seq_len)
    score_factor = temper / math.sqrt(head_width)
    values_wide = values.astype(jnp.float32)

    def one_block(query_rows):
        scores = jnp.dot(query_rows, key_rows.T, preferred_element_type=jnp.float32) * score_factor
        softmaxed = jax.nn.softmax(scores, axis=-1)
        return jnp.dot(softmaxed, values_wide, precision=lax.Precision.DEFAULT).astype(jnp.bfloat16)

    attended = lax.map(one_block, queries.reshape(seq_len // block_size, block_size, head_width))
    return attended.reshape(seq_len, head_width)


def attend_back(quadruple):
    queries, key_rows, values, upstream = quadruple
    seq_len, head_width = queries.shape
    block_size = min(block_limit, seq_len)
    score_factor = temper / math.sqrt(head_width)
    keys_wide = key_rows.astype(jnp.float32)

    def one_block(running, block_pair):
        query_rows, grad_rows = block_pair
        scores = jnp.dot(query_rows, key_rows.T, preferred_element_type=jnp.float32) * score_factor
        softmaxed = jax.nn.softmax(scores, axis=-1)
        dprobs = jnp.dot(grad_rows, values.T, preferred_element_type=jnp.float32)
        dscores = (
            softmaxed
            * (dprobs - jnp.sum(softmaxed * dprobs, axis=-1, keepdims=True))
            * score_factor
        )
        dquery = jnp.dot(dscores, keys_wide, precision=lax.Precision.DEFAULT)
        grad_keys = running[0] + jnp.dot(
            dscores.T, query_rows.astype(jnp.float32), precision=lax.Precision.DEFAULT
        )
        dvalues = running[1] + jnp.dot(
            softmaxed.T, grad_rows.astype(jnp.float32), precision=lax.Precision.DEFAULT
        )
        return ((grad_keys, dvalues), dquery)

    zero_rows = jnp.zeros((seq_len, head_width), jnp.float32)
    count = seq_len // block_size
    blocks = (
        queries.reshape(count, block_size, head_width),
        upstream.reshape(count, block_size, head_width),
    )
    (grad_keys, dvalues), dquery = lax.scan(one_block, (zero_rows, zero_rows), blocks)
    return (
        dquery.reshape(seq_len, head_width).astype(jnp.bfloat16),
        grad_keys.astype(jnp.bfloat16),
        dvalues.astype(jnp.bfloat16),
    )


def attend_all(queries, key_rows, values):
    attended = lax.map(
        attend_head, (heads_major(queries), heads_major(key_rows), heads_major(values))
    )
    return heads_minor(attended, queries.shape[0])


def attend_all_back(queries, key_rows, values, upstream):
    grad_heads = lax.map(
        attend_back,
        (heads_major(queries), heads_major(key_rows), heads_major(values), heads_major(upstream)),
    )
    return tuple((heads_minor(grad_piece, queries.shape[0]) for grad_piece in grad_heads))


def body(tokens, modulation, w_qkv, w_out, w_in, w_back, out_grad):
    videos, local_seq, model_width = tokens.shape
    layers = w_qkv.shape[0]
    own_width = w_qkv.shape[3]
    own_heads = own_width // HEAD_DIM
    grad_scale = 1.0 / math.sqrt(videos * local_seq * lax.axis_size("fsdp") * lax.axis_size(SP))
    stream = tokens.astype(jnp.float32)
    stored = []
    fetched = []
    for layer_index in range(layers):
        weights = one_gather(
            (w_qkv[layer_index], w_out[layer_index], w_in[layer_index], w_back[layer_index]),
            "fsdp",
            (0, 1, 0, 1),
        )
        fetched.append(weights)
        whole_qkv, whole_out, whole_in, whole_back = weights
        joint = whole_qkv.reshape(model_width, 3 * own_width)
        layer_mod = modulation[:, layer_index][:, :, None, :]
        normed_first, rstd_first = normalize(stream)
        input_first = (normed_first * (1.0 + layer_mod[:, 1]) + layer_mod[:, 0]).astype(
            jnp.bfloat16
        )
        first_rows = lax.all_gather(input_first, SP, axis=1, tiled=True)
        packed = project(first_rows, joint).astype(jnp.bfloat16)
        queries = split_heads(packed[..., :own_width], own_heads)
        key_rows = split_heads(packed[..., own_width : 2 * own_width], own_heads)
        values = split_heads(packed[..., 2 * own_width :], own_heads)
        attended = attend_all(queries, key_rows, values).reshape(videos, -1, own_width)
        attn_part = sum_by_axis(
            project(attended, whole_out).astype(jnp.bfloat16), SP, (1, 0), 1
        ).astype(jnp.float32)
        middle = stream + layer_mod[:, 2] * attn_part
        normed_second, rstd_second = normalize(middle)
        input_second = (normed_second * (1.0 + layer_mod[:, 4]) + layer_mod[:, 3]).astype(
            jnp.bfloat16
        )
        second_rows = lax.all_gather(input_second, SP, axis=1, tiled=True)
        hidden = project(second_rows, whole_in)
        activated = gelu_tanh(hidden).astype(jnp.bfloat16)
        ffn_part = sum_by_axis(
            project(activated, whole_back).astype(jnp.bfloat16), SP, (1, 0), 1
        ).astype(jnp.float32)
        stream = middle + layer_mod[:, 5] * ffn_part
        stored.append(
            (
                normed_first,
                rstd_first,
                first_rows,
                queries,
                key_rows,
                values,
                attended,
                normed_second,
                rstd_second,
                second_rows,
                hidden,
                activated,
            )
        )
    final_out = stream.astype(jnp.bfloat16)
    stream_grad = out_grad.astype(jnp.float32)
    results = [None] * layers
    for layer_index in range(layers - 1, -1, -1):
        (
            normed_first,
            rstd_first,
            first_rows,
            queries,
            key_rows,
            values,
            attended,
            normed_second,
            rstd_second,
            second_rows,
            hidden,
            activated,
        ) = stored[layer_index]
        whole_qkv, whole_out, whole_in, whole_back = fetched[layer_index]
        joint = whole_qkv.reshape(model_width, 3 * own_width)
        layer_mod = modulation[:, layer_index][:, :, None, :]
        down_grad = (layer_mod[:, 5] * stream_grad).astype(jnp.bfloat16)
        down_rows = lax.all_gather(down_grad, SP, axis=1, tiled=True)
        back_hidden = project_back(down_rows, whole_back)
        unused, pullback = jax.vjp(gelu_tanh, hidden)
        up_grad = pullback(back_hidden)[0].astype(jnp.bfloat16)
        back_second = sum_by_axis(
            project_back(up_grad, whole_in).astype(jnp.bfloat16), SP, (1, 0), 1
        ).astype(jnp.float32)
        stream_grad = stream_grad + norm_back(
            normed_second, rstd_second, back_second * (1.0 + layer_mod[:, 4])
        )
        attn_grad = (layer_mod[:, 2] * stream_grad).astype(jnp.bfloat16)
        attn_rows = lax.all_gather(attn_grad, SP, axis=1, tiled=True)
        mixed_grad = split_heads(project_back(attn_rows, whole_out).astype(jnp.bfloat16), own_heads)
        grad_query, grad_keys, grad_values = attend_all_back(queries, key_rows, values, mixed_grad)
        packed_grad = jnp.concatenate(
            [
                grad_query.reshape(videos, -1, own_width),
                grad_keys.reshape(videos, -1, own_width),
                grad_values.reshape(videos, -1, own_width),
            ],
            axis=-1,
        )
        back_first = lax.psum_scatter(
            project_back(packed_grad, joint).astype(jnp.bfloat16),
            SP,
            scatter_dimension=1,
            tiled=True,
        ).astype(jnp.float32)
        stream_grad = stream_grad + norm_back(
            normed_first, rstd_first, back_first * (1.0 + layer_mod[:, 1])
        )
        term_qkv = weight_term(first_rows, packed_grad, grad_scale)
        term_out = weight_term(attn_rows, attended, grad_scale)
        term_in = weight_term(second_rows, up_grad, grad_scale)
        term_back = weight_term(down_rows, activated, grad_scale)
        full_terms = (
            term_qkv(0, model_width),
            term_out(0, model_width),
            term_in(0, model_width),
            term_back(0, model_width),
        )
        sum_qkv, sum_out, sum_in, sum_back = tuple(
            (
                part.astype(jnp.float32)
                for part in sum_packed(
                    (
                        full_terms[0].astype(jnp.bfloat16),
                        full_terms[1].astype(jnp.bfloat16),
                        full_terms[2].astype(jnp.bfloat16),
                        full_terms[3].astype(jnp.bfloat16),
                    ),
                    "fsdp",
                    (0, 0, 0, 0),
                )
            )
        )
        results[layer_index] = (
            sum_qkv.reshape(sum_qkv.shape[0], 3, own_width),
            sum_out.T,
            sum_in,
            sum_back.T,
        )
    grad_qkv = jnp.stack([results[index][0] for index in range(layers)])
    grad_out = jnp.stack([results[index][1] for index in range(layers)])
    grad_in = jnp.stack([results[index][2] for index in range(layers)])
    grad_back = jnp.stack([results[index][3] for index in range(layers)])
    return (final_out, stream_grad, grad_qkv, grad_out, grad_in, grad_back)


def solution(mesh):
    torus = Mesh(mesh.devices.reshape(mesh.shape["fsdp"], 2, 2), ("fsdp", "sp_0", "sp_1"))
    return jax.shard_map(
        body,
        mesh=torus,
        in_specs=(
            P("fsdp", SP, None),
            P("fsdp", None, None, None),
            P(None, "fsdp", None, SP),
            P(None, SP, "fsdp"),
            P(None, "fsdp", SP),
            P(None, SP, "fsdp"),
            P("fsdp", SP, None),
        ),
        out_specs=(
            P("fsdp", SP, None),
            P("fsdp", SP, None),
            P(None, "fsdp", None, SP),
            P(None, SP, "fsdp"),
            P(None, "fsdp", SP),
            P(None, SP, "fsdp"),
        ),
        check_vma=False,
    )
```

profile of v0, /device:TPU:0, one launch (start us, length us, event | category | flops | bytes accessed | tf_op | source)
XLA Modules:
  0.0 1303.5 jit_solution(8247963021903286426)
XLA Ops:
  15.2 139.5 %all-gather.15.cloned.1.call-done = bf16[7077888]{0:T(1024)(128)(2,1)} async-done(((bf16[221184]{0:T(1024)(128)(2,1)}), bf16[7077888]{0:T(1024)(128)(2,1)}) %all-gather.15.cloned.1.call-update) | async-done | bytes 14155792 | tf_op jit(solution)/shard_map/all_gather | solution.py:26
  154.7 12.9 reshape.778
  167.6 2.0 slice-done
  169.6 3.1 reshape_reshape_reshape.4
  172.7 6.6 all-gather.7.cloned.1.call-done
  179.3 4.7 fusion.57
  184.3 3.2 while.24
  187.6 4.2 reshape.748
  191.8 3.2 copy.33
  196.5 1.3 copy.34
  197.8 13.1 %reduce-scatter.8.cloned.1.call-done = bf16[2,1,128,1536]{3,2,1,0:T(8,128)(2,1)} async-done(((bf16[4,1,128,1536]{3,2,1,0:T(8,128)(2,1)}), bf16[2,1,128,1536]{3,2,1,0:T(8,128)(2,1)}) %reduce-scatter.8.cloned.1.call-update) | async-done | bytes 786448 | tf_op jit(solution)/shard_map/reduce_scatter | solution.py:39
  211.0 23.5 %reduce-scatter.10.cloned.1.call-done = bf16[1,1,128,1536]{3,2,1,0:T(8,128)(2,1)} async-done(((bf16[2,1,128,1536]{3,2,1,0:T(8,128)(2,1)}), bf16[1,1,128,1536]{3,2,1,0:T(8,128)(2,1)}) %reduce-scatter.10.cloned.1.call-update) | async-done | bytes 393232 | tf_op jit(solution)/shard_map/reduce_scatter | solution.py:39
  236.9 2.0 add_convert_fusion
  240.1 8.1 fusion.111
  248.2 6.0 reshape_reshape.8
  254.2 15.1 %reshape.753 = bf16[32,1536,48]{2,1,0:T(8,128)(2,1)} reshape(bf16[32,73728]{1,0:T(8,128)(2,1)} %get-tuple-element.184) | data formatting | bytes 9437184 | tf_op jit(solution)/shard_map/reshape | solution.py:28
  269.3 12.0 copy.35
  281.3 7.2 fusion.68
  288.5 3.6 all-gather.11.cloned.1.call-done
  292.1 8.0 fusion.52
  300.1 2.7 fusion.56
  303.1 1.3 copy.37
  304.7 6.1 fusion.55
  312.5 5.1 reduce-scatter.16.cloned.1.call-done
  317.6 15.5 %reduce-scatter.12.cloned.1.call-done = bf16[2,1,128,1536]{3,2,1,0:T(8,128)(2,1)} async-done(((bf16[4,1,128,1536]{3,2,1,0:T(8,128)(2,1)}), bf16[2,1,128,1536]{3,2,1,0:T(8,128)(2,1)}) %reduce-scatter.12.cloned.1.call-update) | async-done | bytes 786448 | tf_op jit(solution)/shard_map/reduce_scatter | solution.py:39
  333.2 6.7 fusion.43
  339.9 16.9 %reduce-scatter.18.cloned.1.call-done = bf16[1,1,128,1536]{3,2,1,0:T(8,128)(2,1)} async-done(((bf16[2,1,128,1536]{3,2,1,0:T(8,128)(2,1)}), bf16[1,1,128,1536]{3,2,1,0:T(8,128)(2,1)}) %reduce-scatter.18.cloned.1.call-update) | async-done | bytes 393232 | tf_op jit(solution)/shard_map/reduce_scatter | solution.py:39
  356.8 1.4 fusion.93
  358.2 21.7 %reduce-scatter.14.cloned.1.call-done = bf16[1,1,128,1536]{3,2,1,0:T(8,128)(2,1)} async-done(((bf16[2,1,128,1536]{3,2,1,0:T(8,128)(2,1)}), bf16[1,1,128,1536]{3,2,1,0:T(8,128)(2,1)}) %reduce-scatter.14.cloned.1.call-update) | async-done | bytes 393232 | tf_op jit(solution)/shard_map/reduce_scatter | solution.py:39
  379.9 2.6 multiply_convert_fusion.1
  383.1 2.0 slice_bitcast_fusion.44
  401.0 1.7 slice_bitcast_fusion.63
  415.0 3.3 fusion.44
  449.1 28.3 %stack.567 = bf16[32,73728]{1,0:T(8,128)(2,1)} concatenate(bf16[1,73728]{1,0:T(2,128)(2,1)} %bitcast.775, bf16[1,73728]{1,0:T(2,128)(2,1)} %bitcast.776, bf16[1,73728]{1,0:T(2,128)(2,1)} %bitcast.777, bf16[1,73728]{1,0:T(2,128)(2,1)} %bitcast.778, bf16[1,73728]{1,0:T(2,128)(2,1)} %bitcast.779, bf16[1,73728]{1,0:T(2,128)(2,1)} %bitcast.780, bf16[1,73728]{1,0:T(2,128)(2,1)} %bitcast.781, ...), dimensions={0} | concatenate | bytes 9437184 | tf_op jit(solution)/shard_map/stack | solution.py:44
  477.4 28.6 %stack.600 = bf16[32,73728]{1,0:T(8,128)(2,1)} concatenate(bf16[1,73728]{1,0:T(2,128)(2,1)} %bitcast.807, bf16[1,73728]{1,0:T(2,128)(2,1)} %bitcast.808, bf16[1,73728]{1,0:T(2,128)(2,1)} %bitcast.809, bf16[1,73728]{1,0:T(2,128)(2,1)} %bitcast.810, bf16[1,73728]{1,0:T(2,128)(2,1)} %bitcast.811, bf16[1,73728]{1,0:T(2,128)(2,1)} %bitcast.812, bf16[1,73728]{1,0:T(2,128)(2,1)} %bitcast.813, ...), dimensions={0} | concatenate | bytes 9437184 | tf_op jit(solution)/shard_map/stack | solution.py:44
  506.0 2.7 fusion.75
  511.9 24.3 %while.25 = (s32[]{:T(128)}, bf16[3,512,128]{1,2,0:T(8,128)(2,1)}, bf16[3,512,128]{1,2,0:T(8,128)(2,1)}, bf16[3,512,128]{1,2,0:T(8,128)(2,1)}, bf16[3,512,128]{2...) while((s32[]{:T(128)}, bf16[3,512,128]{1,2,0:T(8,128)(2,1)}, ...), condition=%wide.region_20.21_spmd, body=%wide.region_16.20_spmd.sunk | while | flops 340982272 | bytes 16547457 | solution.py:187
  512.4 1.3 multiply_reduce_fusion.3
  517.4 1.8 fusion.151
  520.4 1.3 multiply_reduce_fusion.3
  525.4 1.8 fusion.151
  528.4 1.3 multiply_reduce_fusion.3
  533.3 1.8 fusion.151
  536.3 4.0 fusion.45
  545.1 3.5 fusion.58
  551.2 1.8 copy.72
  553.0 1.8 copy.73
  554.8 1.8 copy.74
  556.6 1.8 copy.75
  558.3 1.8 copy.76
  560.1 1.8 copy.77
  561.9 1.8 copy.78
  563.6 1.8 copy.79
  565.4 1.8 copy.80
  567.2 1.8 copy.81
  600.0 23.8 %stack.501 = bf16[32,55296]{1,0:T(8,128)(2,1)} concatenate(bf16[1,55296]{1,0:T(2,128)(2,1)} %bitcast.848, bf16[1,55296]{1,0:T(2,128)(2,1)} %bitcast.849, bf16[1,55296]{1,0:T(2,128)(2,1)} %bitcast.850, bf16[1,55296]{1,0:T(2,128)(2,1)} %bitcast.851, bf16[1,55296]{1,0:T(2,128)(2,1)} %bitcast.839, bf16[1,55296]{1,0:T(2,128)(2,1)} %bitcast.840, bf16[1,55296]{1,0:T(2,128)(2,1)} %bitcast.841, ...), dimensions={0} | concatenate | bytes 7077888 | tf_op jit(solution)/shard_map/stack | solution.py:44
  623.8 9.1 stack.534
  632.9 31.7 %pad_maximum_fusion = bf16[32,221184]{1,0:T(8,128)(2,1)} fusion(bf16[32,73728]{1,0:T(8,128)(2,1)} %stack.600, bf16[32,73728]{1,0:T(8,128)(2,1)} %stack.567, bf16[32,18432]{1,0:T(8,128)(2,1)S(1)} %stack.534, bf16[32,55296]{1,0:T(8,128)(2,1)} %stack.501), kind=kLoop, calls=%fused_computation.54 | loop fusion | flops 56623104 | bytes 28311552 | tf_op jit(solution)/shard_map/concatenate | solution.py:55
  665.8 1.3 fusion.99
  667.1 2.2 fusion.88
  669.4 615.7 %all-reduce.3.cloned.1.call-done = bf16[32,221184]{1,0:T(8,128)(2,1)} async-done(((bf16[32,221184]{1,0:T(8,128)(2,1)}), bf16[32,221184]{1,0:T(8,128)(2,1)}) %all-reduce.3.cloned.1.call-update) | async-done | bytes 14155792
  1285.1 4.4 fusion.101
  1291.0 2.5 fusion.103
  1294.3 1.9 fusion.104
  (386 shorter events, 138.6 us)
Async XLA Ops:
  7.2 147.5 %all-gather.15.cloned.1.call-start = ((), (), s32[]{:S(2)}) async-start(), calls=%async_computation.18 | async-start | bytes 14598144 | tf_op jit(solution)/shard_map/all_gather | solution.py:26
  12.9 166.3 %all-gather.7.cloned.1.call-start = ((), (), s32[]{:S(2)}) async-start(), calls=%async_computation.7 | async-start | bytes 1966080 | tf_op jit(solution)/shard_map/all_gather | solution.py:217
  13.6 141.1 %copy-start.51 = (f32[1536]{0:T(1024)}, f32[1536]{0:T(1024)S(1)}, u32[]{:S(2)}) copy-start(f32[1536]{0:T(1024)S(1)} %get-tuple-element.145) | copy-start | bytes 18436
  13.8 141.0 %copy-start.56 = (f32[128]{0:T(128)}, f32[128]{0:T(128)S(1)}, u32[]{:S(2)}) copy-start(f32[128]{0:T(128)S(1)} %broadcast_multiply_fusion.5) | copy-start | bytes 1540
  14.1 140.7 %copy-start.58 = (f32[128]{0:T(128)}, f32[128]{0:T(128)S(1)}, u32[]{:S(2)}) copy-start(f32[128]{0:T(128)S(1)} %add_rsqrt_fusion.1) | copy-start | bytes 1540
  15.1 195.8 %reduce-scatter.8.cloned.1.call-start = ((), (), s32[]{:S(2)}) async-start(), calls=%async_computation.8 | async-start | bytes 2359296 | tf_op jit(solution)/shard_map/reduce_scatter | solution.py:39
  196.4 38.0 %copy-start.1 = (bf16[1,128,1536]{2,1,0:T(8,128)(2,1)S(1)}, bf16[1,128,1536]{2,1,0:T(8,128)(2,1)}, u32[]{:S(2)}) copy-start(bf16[1,128,1536]{2,1,0:T(8,128)(2,1)} %param.11) | copy-start | bytes 1179652
  196.4 40.5 %copy-start.55 = (f32[1536]{0:T(1024)S(1)}, f32[1536]{0:T(1024)}, u32[]{:S(2)}) copy-start(f32[1536]{0:T(1024)} %get-tuple-element.142) | copy-start | bytes 18436
  197.7 41.3 %copy-start.5 = (bf16[1,128,1536]{2,1,0:T(8,128)(2,1)S(1)}, bf16[1,128,1536]{2,1,0:T(8,128)(2,1)}, u32[]{:S(2)}) copy-start(bf16[1,128,1536]{2,1,0:T(8,128)(2,1)} %param.17) | copy-start | bytes 1179652
  197.7 41.3 %copy-start.53 = (f32[1536]{0:T(1024)S(1)}, f32[1536]{0:T(1024)}, u32[]{:S(2)}) copy-start(f32[1536]{0:T(1024)} %get-tuple-element.141) | copy-start | bytes 18436
  197.8 36.7 %reduce-scatter.10.cloned.1.call-start = ((), (), s32[]{:S(2)}) async-start(), calls=%async_computation.9 | async-start | bytes 1179648 | tf_op jit(solution)/shard_map/reduce_scatter | solution.py:39
  210.9 70.4 %all-gather.9.cloned.1.call-start = ((), (), s32[]{:S(2)}) async-start(), calls=%async_computation.10 | async-start | bytes 1966080 | tf_op jit(solution)/shard_map/all_gather | solution.py:231
  238.9 53.1 %all-gather.11.cloned.1.call-start = ((), (), s32[]{:S(2)}) async-start(), calls=%async_computation.13 | async-start | bytes 1966080 | tf_op jit(solution)/shard_map/all_gather | solution.py:276
  239.8 77.7 %reduce-scatter.16.cloned.1.call-start = ((), (), s32[]{:S(2)}) async-start(), calls=%async_computation.14 | async-start | bytes 2359296 | tf_op jit(solution)/shard_map/reduce_scatter | solution.py:39
  281.3 18.7 %slice-start.2 = ((s8[4718592]{0:T(1024)(128)(4,1)}), s8[524288]{0:T(1024)(128)(4,1)S(1)}, s32[]{:S(2)}) async-start(s8[4718592]{0:T(1024)(128)(4,1)} %bitcast.748), calls=%async_computation.22 | async-start | bytes 1048576
  292.1 8.0 slice-start.3
  304.4 28.7 %reduce-scatter.12.cloned.1.call-start = ((), (), s32[]{:S(2)}) async-start(), calls=%async_computation.11 | async-start | bytes 2359296 | tf_op jit(solution)/shard_map/reduce_scatter | solution.py:39
  312.4 44.4 %reduce-scatter.18.cloned.1.call-start = ((), (), s32[]{:S(2)}) async-start(), calls=%async_computation.15 | async-start | bytes 1179648 | tf_op jit(solution)/shard_map/reduce_scatter | solution.py:39
  317.6 62.4 %reduce-scatter.14.cloned.1.call-start = ((), (), s32[]{:S(2)}) async-start(), calls=%async_computation.12 | async-start | bytes 1179648 | tf_op jit(solution)/shard_map/reduce_scatter | solution.py:39
  333.1 23.7 %copy-start.2 = (bf16[1,1,128,1536]{3,2,1,0:T(8,128)(2,1)S(1)}, bf16[1,1,128,1536]{3,2,1,0:T(8,128)(2,1)}, u32[]{:S(2)}) copy-start(bf16[1,1,128,1536]{3,2,1,0:T(8,128)(2,1)} %reduce-scatter.10.cloned.1.call-done) | copy-start | bytes 1179652
  333.1 172.9 %all-gather.13.cloned.1.call-start = ((), (), s32[]{:S(2)}) async-start(), calls=%async_computation.16 | async-start | bytes 1966080 | tf_op jit(solution)/shard_map/all_gather | solution.py:287
  382.6 283.3 %reduce-scatter.20.cloned.1.call-start = ((), (), s32[]{:S(2)}) async-start(), calls=%async_computation.17 | async-start | bytes 1966080 | tf_op jit(solution)/shard_map/reduce_scatter | solution.py:298
  402.7 12.3 copy-start.61
  402.7 12.3 copy-start.64
  548.6 20.3 %copy-start.18 = (bf16[1,1,48,1152]{3,2,1,0:T(8,128)(2,1)S(1)}, bf16[1,1,48,1152]{3,2,1,0:T(8,128)(2,1)}, u32[]{:S(2)}) copy-start(bf16[1,1,48,1152]{3,2,1,0:T(8,128)(2,1)} %get-tuple-element.276) | copy-start | bytes 331780
  548.8 21.0 %copy-start.17 = (bf16[1,1,48,1152]{3,2,1,0:T(8,128)(2,1)S(1)}, bf16[1,1,48,1152]{3,2,1,0:T(8,128)(2,1)}, u32[]{:S(2)}) copy-start(bf16[1,1,48,1152]{3,2,1,0:T(8,128)(2,1)} %get-tuple-element.275) | copy-start | bytes 331780
  549.0 21.7 %copy-start.16 = (bf16[1,1,48,1152]{3,2,1,0:T(8,128)(2,1)S(1)}, bf16[1,1,48,1152]{3,2,1,0:T(8,128)(2,1)}, u32[]{:S(2)}) copy-start(bf16[1,1,48,1152]{3,2,1,0:T(8,128)(2,1)} %get-tuple-element.274) | copy-start | bytes 331780
  549.2 22.4 %copy-start.15 = (bf16[1,1,48,1152]{3,2,1,0:T(8,128)(2,1)S(1)}, bf16[1,1,48,1152]{3,2,1,0:T(8,128)(2,1)}, u32[]{:S(2)}) copy-start(bf16[1,1,48,1152]{3,2,1,0:T(8,128)(2,1)} %get-tuple-element.273) | copy-start | bytes 331780
  549.4 23.1 %copy-start.14 = (bf16[1,1,48,1152]{3,2,1,0:T(8,128)(2,1)S(1)}, bf16[1,1,48,1152]{3,2,1,0:T(8,128)(2,1)}, u32[]{:S(2)}) copy-start(bf16[1,1,48,1152]{3,2,1,0:T(8,128)(2,1)} %get-tuple-element.272) | copy-start | bytes 331780
  549.5 23.8 %copy-start.13 = (bf16[1,1,48,1152]{3,2,1,0:T(8,128)(2,1)S(1)}, bf16[1,1,48,1152]{3,2,1,0:T(8,128)(2,1)}, u32[]{:S(2)}) copy-start(bf16[1,1,48,1152]{3,2,1,0:T(8,128)(2,1)} %get-tuple-element.271) | copy-start | bytes 331780
  549.7 24.4 %copy-start.12 = (bf16[1,1,48,1152]{3,2,1,0:T(8,128)(2,1)S(1)}, bf16[1,1,48,1152]{3,2,1,0:T(8,128)(2,1)}, u32[]{:S(2)}) copy-start(bf16[1,1,48,1152]{3,2,1,0:T(8,128)(2,1)} %get-tuple-element.270) | copy-start | bytes 331780
  549.9 25.1 %copy-start.11 = (bf16[1,1,48,1152]{3,2,1,0:T(8,128)(2,1)S(1)}, bf16[1,1,48,1152]{3,2,1,0:T(8,128)(2,1)}, u32[]{:S(2)}) copy-start(bf16[1,1,48,1152]{3,2,1,0:T(8,128)(2,1)} %get-tuple-element.269) | copy-start | bytes 331780
  550.1 25.8 %copy-start.10 = (bf16[1,1,48,1152]{3,2,1,0:T(8,128)(2,1)S(1)}, bf16[1,1,48,1152]{3,2,1,0:T(8,128)(2,1)}, u32[]{:S(2)}) copy-start(bf16[1,1,48,1152]{3,2,1,0:T(8,128)(2,1)} %get-tuple-element.268) | copy-start | bytes 331780
  551.2 25.5 %copy-start.9 = (bf16[1,1,48,1152]{3,2,1,0:T(8,128)(2,1)S(1)}, bf16[1,1,48,1152]{3,2,1,0:T(8,128)(2,1)}, u32[]{:S(2)}) copy-start(bf16[1,1,48,1152]{3,2,1,0:T(8,128)(2,1)} %get-tuple-element.280) | copy-start | bytes 331780
  553.0 24.6 %copy-start.8 = (bf16[1,1,48,1152]{3,2,1,0:T(8,128)(2,1)S(1)}, bf16[1,1,48,1152]{3,2,1,0:T(8,128)(2,1)}, u32[]{:S(2)}) copy-start(bf16[1,1,48,1152]{3,2,1,0:T(8,128)(2,1)} %get-tuple-element.279) | copy-start | bytes 331780
  558.3 22.1 %copy-start.37 = (bf16[1,1,48,384]{3,2,1,0:T(8,128)(2,1)S(1)}, bf16[1,1,48,384]{3,2,1,0:T(8,128)(2,1)}, u32[]{:S(2)}) copy-start(bf16[1,1,48,384]{3,2,1,0:T(8,128)(2,1)} %get-tuple-element.310) | copy-start | bytes 110596
  560.1 20.5 %copy-start.36 = (bf16[1,1,48,384]{3,2,1,0:T(8,128)(2,1)S(1)}, bf16[1,1,48,384]{3,2,1,0:T(8,128)(2,1)}, u32[]{:S(2)}) copy-start(bf16[1,1,48,384]{3,2,1,0:T(8,128)(2,1)} %get-tuple-element.308) | copy-start | bytes 110596
  560.1 20.5 %copy-start.35 = (bf16[1,1,48,384]{3,2,1,0:T(8,128)(2,1)S(1)}, bf16[1,1,48,384]{3,2,1,0:T(8,128)(2,1)}, u32[]{:S(2)}) copy-start(bf16[1,1,48,384]{3,2,1,0:T(8,128)(2,1)} %get-tuple-element.307) | copy-start | bytes 110596
  561.9 19.5 %copy-start.34 = (bf16[1,1,48,384]{3,2,1,0:T(8,128)(2,1)S(1)}, bf16[1,1,48,384]{3,2,1,0:T(8,128)(2,1)}, u32[]{:S(2)}) copy-start(bf16[1,1,48,384]{3,2,1,0:T(8,128)(2,1)} %get-tuple-element.306) | copy-start | bytes 110596
  561.9 20.2 %copy-start.33 = (bf16[1,1,48,384]{3,2,1,0:T(8,128)(2,1)S(1)}, bf16[1,1,48,384]{3,2,1,0:T(8,128)(2,1)}, u32[]{:S(2)}) copy-start(bf16[1,1,48,384]{3,2,1,0:T(8,128)(2,1)} %get-tuple-element.305) | copy-start | bytes 110596
  563.6 19.1 %copy-start.32 = (bf16[1,1,48,384]{3,2,1,0:T(8,128)(2,1)S(1)}, bf16[1,1,48,384]{3,2,1,0:T(8,128)(2,1)}, u32[]{:S(2)}) copy-start(bf16[1,1,48,384]{3,2,1,0:T(8,128)(2,1)} %get-tuple-element.304) | copy-start | bytes 110596
  563.6 19.8 %copy-start.31 = (bf16[1,1,48,384]{3,2,1,0:T(8,128)(2,1)S(1)}, bf16[1,1,48,384]{3,2,1,0:T(8,128)(2,1)}, u32[]{:S(2)}) copy-start(bf16[1,1,48,384]{3,2,1,0:T(8,128)(2,1)} %get-tuple-element.303) | copy-start | bytes 110596
  563.6 20.5 %copy-start.30 = (bf16[1,1,48,384]{3,2,1,0:T(8,128)(2,1)S(1)}, bf16[1,1,48,384]{3,2,1,0:T(8,128)(2,1)}, u32[]{:S(2)}) copy-start(bf16[1,1,48,384]{3,2,1,0:T(8,128)(2,1)} %get-tuple-element.302) | copy-start | bytes 110596
  565.4 19.4 %copy-start.29 = (bf16[1,1,48,384]{3,2,1,0:T(8,128)(2,1)S(1)}, bf16[1,1,48,384]{3,2,1,0:T(8,128)(2,1)}, u32[]{:S(2)}) copy-start(bf16[1,1,48,384]{3,2,1,0:T(8,128)(2,1)} %get-tuple-element.301) | copy-start | bytes 110596
  565.4 20.0 %copy-start.28 = (bf16[1,1,48,384]{3,2,1,0:T(8,128)(2,1)S(1)}, bf16[1,1,48,384]{3,2,1,0:T(8,128)(2,1)}, u32[]{:S(2)}) copy-start(bf16[1,1,48,384]{3,2,1,0:T(8,128)(2,1)} %get-tuple-element.300) | copy-start | bytes 110596
  565.4 20.7 %copy-start.27 = (bf16[1,1,48,384]{3,2,1,0:T(8,128)(2,1)S(1)}, bf16[1,1,48,384]{3,2,1,0:T(8,128)(2,1)}, u32[]{:S(2)}) copy-start(bf16[1,1,48,384]{3,2,1,0:T(8,128)(2,1)} %get-tuple-element.299) | copy-start | bytes 110596
  567.2 19.7 %copy-start.26 = (bf16[1,1,48,384]{3,2,1,0:T(8,128)(2,1)S(1)}, bf16[1,1,48,384]{3,2,1,0:T(8,128)(2,1)}, u32[]{:S(2)}) copy-start(bf16[1,1,48,384]{3,2,1,0:T(8,128)(2,1)} %get-tuple-element.298) | copy-start | bytes 110596
  567.2 20.4 %copy-start.25 = (bf16[1,1,48,384]{3,2,1,0:T(8,128)(2,1)S(1)}, bf16[1,1,48,384]{3,2,1,0:T(8,128)(2,1)}, u32[]{:S(2)}) copy-start(bf16[1,1,48,384]{3,2,1,0:T(8,128)(2,1)} %get-tuple-element.297) | copy-start | bytes 110596
  567.2 21.1 %copy-start.24 = (bf16[1,1,48,384]{3,2,1,0:T(8,128)(2,1)S(1)}, bf16[1,1,48,384]{3,2,1,0:T(8,128)(2,1)}, u32[]{:S(2)}) copy-start(bf16[1,1,48,384]{3,2,1,0:T(8,128)(2,1)} %get-tuple-element.296) | copy-start | bytes 110596
  568.9 20.0 %copy-start.23 = (bf16[1,1,48,384]{3,2,1,0:T(8,128)(2,1)S(1)}, bf16[1,1,48,384]{3,2,1,0:T(8,128)(2,1)}, u32[]{:S(2)}) copy-start(bf16[1,1,48,384]{3,2,1,0:T(8,128)(2,1)} %get-tuple-element.295) | copy-start | bytes 110596
  569.8 21.2 %copy-start.50 = (bf16[1,1,48,384]{3,2,1,0:T(8,128)(2,1)S(1)}, bf16[1,1,48,384]{3,2,1,0:T(8,128)(2,1)}, u32[]{:S(2)}) copy-start(bf16[1,1,48,384]{3,2,1,0:T(8,128)(2,1)} %get-tuple-element.324) | copy-start | bytes 110596
  569.8 21.9 %copy-start.49 = (bf16[1,1,48,384]{3,2,1,0:T(8,128)(2,1)S(1)}, bf16[1,1,48,384]{3,2,1,0:T(8,128)(2,1)}, u32[]{:S(2)}) copy-start(bf16[1,1,48,384]{3,2,1,0:T(8,128)(2,1)} %get-tuple-element.323) | copy-start | bytes 110596
  569.8 22.5 %copy-start.48 = (bf16[1,1,48,384]{3,2,1,0:T(8,128)(2,1)S(1)}, bf16[1,1,48,384]{3,2,1,0:T(8,128)(2,1)}, u32[]{:S(2)}) copy-start(bf16[1,1,48,384]{3,2,1,0:T(8,128)(2,1)} %get-tuple-element.322) | copy-start | bytes 110596
  570.7 22.3 %copy-start.47 = (bf16[1,1,48,384]{3,2,1,0:T(8,128)(2,1)S(1)}, bf16[1,1,48,384]{3,2,1,0:T(8,128)(2,1)}, u32[]{:S(2)}) copy-start(bf16[1,1,48,384]{3,2,1,0:T(8,128)(2,1)} %get-tuple-element.321) | copy-start | bytes 110596
  570.7 23.0 %copy-start.46 = (bf16[1,1,48,384]{3,2,1,0:T(8,128)(2,1)S(1)}, bf16[1,1,48,384]{3,2,1,0:T(8,128)(2,1)}, u32[]{:S(2)}) copy-start(bf16[1,1,48,384]{3,2,1,0:T(8,128)(2,1)} %get-tuple-element.320) | copy-start | bytes 110596
  570.7 23.7 %copy-start.45 = (bf16[1,1,48,384]{3,2,1,0:T(8,128)(2,1)S(1)}, bf16[1,1,48,384]{3,2,1,0:T(8,128)(2,1)}, u32[]{:S(2)}) copy-start(bf16[1,1,48,384]{3,2,1,0:T(8,128)(2,1)} %get-tuple-element.319) | copy-start | bytes 110596
  571.6 23.5 %copy-start.44 = (bf16[1,1,48,384]{3,2,1,0:T(8,128)(2,1)S(1)}, bf16[1,1,48,384]{3,2,1,0:T(8,128)(2,1)}, u32[]{:S(2)}) copy-start(bf16[1,1,48,384]{3,2,1,0:T(8,128)(2,1)} %get-tuple-element.318) | copy-start | bytes 110596
  571.6 24.2 %copy-start.43 = (bf16[1,1,48,384]{3,2,1,0:T(8,128)(2,1)S(1)}, bf16[1,1,48,384]{3,2,1,0:T(8,128)(2,1)}, u32[]{:S(2)}) copy-start(bf16[1,1,48,384]{3,2,1,0:T(8,128)(2,1)} %get-tuple-element.317) | copy-start | bytes 110596
  571.6 24.9 %copy-start.42 = (bf16[1,1,48,384]{3,2,1,0:T(8,128)(2,1)S(1)}, bf16[1,1,48,384]{3,2,1,0:T(8,128)(2,1)}, u32[]{:S(2)}) copy-start(bf16[1,1,48,384]{3,2,1,0:T(8,128)(2,1)} %get-tuple-element.316) | copy-start | bytes 110596
  572.4 24.7 %copy-start.41 = (bf16[1,1,48,384]{3,2,1,0:T(8,128)(2,1)S(1)}, bf16[1,1,48,384]{3,2,1,0:T(8,128)(2,1)}, u32[]{:S(2)}) copy-start(bf16[1,1,48,384]{3,2,1,0:T(8,128)(2,1)} %get-tuple-element.315) | copy-start | bytes 110596
  572.4 25.4 %copy-start.40 = (bf16[1,1,48,384]{3,2,1,0:T(8,128)(2,1)S(1)}, bf16[1,1,48,384]{3,2,1,0:T(8,128)(2,1)}, u32[]{:S(2)}) copy-start(bf16[1,1,48,384]{3,2,1,0:T(8,128)(2,1)} %get-tuple-element.314) | copy-start | bytes 110596
  572.4 26.1 %copy-start.39 = (bf16[1,1,48,384]{3,2,1,0:T(8,128)(2,1)S(1)}, bf16[1,1,48,384]{3,2,1,0:T(8,128)(2,1)}, u32[]{:S(2)}) copy-start(bf16[1,1,48,384]{3,2,1,0:T(8,128)(2,1)} %get-tuple-element.313) | copy-start | bytes 110596
  573.3 25.9 %copy-start.38 = (bf16[1,1,48,384]{3,2,1,0:T(8,128)(2,1)S(1)}, bf16[1,1,48,384]{3,2,1,0:T(8,128)(2,1)}, u32[]{:S(2)}) copy-start(bf16[1,1,48,384]{3,2,1,0:T(8,128)(2,1)} %get-tuple-element.312) | copy-start | bytes 110596
  600.0 685.1 %all-reduce.3.cloned.1.call-start = ((), (), s32[]{:S(2)}) async-start(), calls=%async_computation.19 | async-start | bytes 28311552
  (21 other events, 58.8 us)
Sparse Core Ops, SparseCore 0:
  13.1 141.6 all-gather.14
  157.0 22.2 all-gather.6
  197.9 12.9 reduce-scatter.7
  213.1 21.2 reduce-scatter.9
  239.1 25.3 all-gather.8
  266.5 25.5 all-gather.10
  304.5 12.9 reduce-scatter.15
  319.9 13.1 reduce-scatter.11
  335.5 21.2 reduce-scatter.17
  359.0 20.8 reduce-scatter.13
  382.7 25.3 all-gather.12
  600.1 24.5 reduce-scatter.19
  664.8 620.2 all-reduce.2
where the time goes:
time: 1320 us; the launch traced here: 1300 us
  waiting for transfers between devices  861 us (65%)
  local copies, waits for them, and re-layouts  298 us (23%)
  matrix products  67.9 us (5%)
  other arithmetic  58.8 us (4%)
  between operations  15 us (1%)
    unnamed x14, waiting for transfers between devices  616 us
    all_gather x1, waiting for transfers between devices, one_gather(): lines, at, gathered = (lax.all_gather(ravelled, axis), 0, [])  140 us
    unnamed x275, local copies, waits for them, and re-layouts  122 us
    reduce_scatter x6, waiting for transfers between devices, own_block(): blocks = lax.psum_scatter(blocks, axes[k], scatter_dimension=0, tiled=True)  95.7 us
    another operation x7, local copies, waits for them, and re-layouts, cut_along(): return jnp.stack(jnp.split(value, count, axis=dim))  90.1 us
    concatenate x1, other arithmetic, sum_packed(): lines = jnp.concatenate([b.reshape(count, -1) for b in blocks], axis=1)  31.7 us
  transfers between devices with their start and end apart: 13, of which 10 were waited for; matrix products, arithmetic and copies ran while one was open for 21% of the time, Pallas kernels for 0%

commit v1 on v0

v1 whole, which is shorter than its diff:
```python
import functools
import math

import jax
import jax.numpy as jnp
from jax import lax
from jax.experimental import pallas as pl
from jax.experimental.pallas import tpu as pltpu
from jax.sharding import Mesh
from jax.sharding import PartitionSpec as P

HEAD_DIM = 128
MESH = pl.DeviceIdType.MESH
FSDP = ("z", "y", "xh")
SP = ("xl", "c")
BF = jnp.bfloat16
F32 = jnp.float32

ln_eps = 1e-06
temper = 2.5
VMEM_LIMIT = 66_000_000

CHUNKS = (
    ((0, 640), (640, 512)),
    ((1152, 128), (1280, 256)),
    ((1536, 768), (2304, 768)),
    ((3072, 768), (3840, 768)),
)
WIDTH = 4608


def turn(axis, step, size):
    return {axis: lax.rem(lax.axis_index(axis) + step + size, size)}


def near(axis, step):
    return lax.rem(lax.axis_index(axis) + step + 4, 4)


class Wires:
    def __init__(self, send, recv):
        self.send, self.recv, self.used, self.open = send, recv, 0, []

    def go(self, src, dst, device):
        at = self.used
        self.used += 1
        copy = pltpu.make_async_remote_copy(
            src_ref=src,
            dst_ref=dst,
            send_sem=self.send.at[at],
            recv_sem=self.recv.at[at],
            device_id=device,
            device_id_type=MESH,
        )
        copy.start()
        self.open.append(copy)
        return copy

    def drain(self):
        for copy in self.open:
            copy.wait_send()
        self.open = []


def greet(sp=False):
    barrier = pltpu.get_barrier_semaphore()
    targets = [turn("z", 1, 4), turn("z", -1, 4), turn("y", 1, 4), turn("y", -1, 4), turn("xh", 1, 2)]
    if sp:
        targets += [turn("xl", 1, 2), turn("c", 1, 2)]
    for device in targets:
        pl.semaphore_signal(barrier, inc=1, device_id=device, device_id_type=MESH)
    pl.semaphore_wait(barrier, len(targets))


def rows_of(start, count):
    return pl.ds(pl.multiple_of(start, 16), count)


def cols_of(cols):
    return pl.ds(cols[0], cols[1])


class Gather:
    def __init__(self, wires, w):
        self.wires, self.w = wires, w
        self.z, self.y, self.xh = (lax.axis_index(a) for a in FSDP)
        self.one, self.two, self.relay2, self.three, self.relay3 = {}, {}, {}, {}, {}

    def same(self, part, device):
        return self.wires.go(part, part, device)

    def s1(self, k):
        (a0, an), (b0, bn) = CHUNKS[k]
        part = self.w.at[self.z, rows_of(96 * self.y + 48 * self.xh, 48), pl.ds(a0, an + bn)]
        self.one[k] = self.same(part, turn("xh", 1, 2))

    def s2(self, k):
        self.one[k].wait_recv()
        ca, cb = map(cols_of, CHUNKS[k])
        pa = self.w.at[self.z, rows_of(96 * self.y, 96), ca]
        pb = self.w.at[self.z, rows_of(96 * self.y, 96), cb]
        self.two[k] = [
            self.same(pa, turn("y", 1, 4)),
            self.same(pa, turn("y", -1, 4)),
            self.same(pb, turn("z", 1, 4)),
            self.same(pb, turn("z", -1, 4)),
        ]

    def s2b(self, k):
        ca, cb = map(cols_of, CHUNKS[k])
        for copy in self.two[k]:
            copy.wait_recv()
        w, z, y = self.w, self.z, self.y
        self.relay2[k] = [
            self.same(w.at[z, rows_of(96 * near("y", -1), 48), ca], turn("y", 1, 4)),
            self.same(w.at[z, rows_of(96 * near("y", 1) + 48, 48), ca], turn("y", -1, 4)),
            self.same(w.at[near("z", -1), rows_of(96 * y, 48), cb], turn("z", 1, 4)),
            self.same(w.at[near("z", 1), rows_of(96 * y + 48, 48), cb], turn("z", -1, 4)),
        ]

    def s3(self, k):
        ca, cb = map(cols_of, CHUNKS[k])
        for copy in self.relay2[k]:
            copy.wait_recv()
        pa = self.w.at[self.z, :, ca]
        pb = self.w.at[:, rows_of(96 * self.y, 96), cb]
        self.three[k] = [
            self.same(pa, turn("z", 1, 4)),
            self.same(pa, turn("z", -1, 4)),
            self.same(pb, turn("y", 1, 4)),
            self.same(pb, turn("y", -1, 4)),
        ]

    def s3b(self, k):
        ca, cb = map(cols_of, CHUNKS[k])
        for copy in self.three[k]:
            copy.wait_recv()
        w = self.w
        self.relay3[k] = [
            self.same(w.at[near("z", -1), pl.ds(0, 192), ca], turn("z", 1, 4)),
            self.same(w.at[near("z", 1), pl.ds(192, 192), ca], turn("z", -1, 4)),
            self.same(w.at[:, rows_of(96 * near("y", -1), 48), cb], turn("y", 1, 4)),
            self.same(w.at[:, rows_of(96 * near("y", 1) + 48, 48), cb], turn("y", -1, 4)),
        ]

    def done(self, k):
        for copy in self.relay3[k]:
            copy.wait_recv()


def add_into(dst, *srcs):
    planes, rows, columns = dst.shape

    @pl.loop(0, planes * (rows // 48))
    def _(i):
        at = (i // (rows // 48), pl.ds(pl.multiple_of((i % (rows // 48)) * 48, 48), 48), slice(None))
        total = dst[at].astype(F32)
        for src in srcs:
            total = total + src[at].astype(F32)
        dst[at] = total.astype(dst.dtype)


class Scatter:
    def __init__(self, wires, g, half_a, full_a, half_b, full_b, half2, full2, last, out):
        self.wires, self.g, self.out = wires, g, out
        self.half_a, self.full_a, self.half_b, self.full_b = half_a, full_a, half_b, full_b
        self.half2, self.full2, self.last = half2, full2, last
        self.z, self.y, self.xh = (lax.axis_index(a) for a in FSDP)
        self.copies = {}

    def block_a(self, step, start, count, cols):
        return self.g.at[pl.ds(near("z", step), 1), pl.ds(start, count), cols]

    def block_b(self, step, start, count, cols):
        return self.g.at[:, rows_of(96 * near("y", step) + start, count), cols]

    def sub_a(self, step, start, count, cols):
        return self.g.at[pl.ds(self.z, 1), rows_of(96 * near("y", step) + start, count), cols]

    def sub_b(self, step, start, count, cols):
        return self.g.at[pl.ds(near("z", step), 1), rows_of(96 * self.y + start, count), cols]

    def r1(self, k):
        ca, cb = map(cols_of, CHUNKS[k])
        go = self.wires.go
        self.copies[k, 1] = [
            go(self.block_a(2, 0, 192, ca), self.half_a[k].at[pl.ds(0, 1)], turn("z", 1, 4)),
            go(self.block_a(2, 192, 192, ca), self.half_a[k].at[pl.ds(1, 1)], turn("z", -1, 4)),
            go(self.block_b(2, 0, 48, cb), self.half_b[k].at[0], turn("y", 1, 4)),
            go(self.block_b(2, 48, 48, cb), self.half_b[k].at[1], turn("y", -1, 4)),
        ]

    def r1b(self, k):
        ca, cb = map(cols_of, CHUNKS[k])
        go, copies = self.wires.go, self.copies[k, 1]
        sent = []
        copies[0].wait_recv()
        add_into(self.block_a(1, 0, 192, ca), self.half_a[k].at[pl.ds(0, 1)])
        sent.append(go(self.block_a(1, 0, 384, ca), self.full_a[k].at[pl.ds(0, 1)], turn("z", 1, 4)))
        copies[1].wait_recv()
        add_into(self.block_a(-1, 192, 192, ca), self.half_a[k].at[pl.ds(1, 1)])
        sent.append(go(self.block_a(-1, 0, 384, ca), self.full_a[k].at[pl.ds(1, 1)], turn("z", -1, 4)))
        copies[2].wait_recv()
        add_into(self.block_b(1, 0, 48, cb), self.half_b[k].at[0])
        sent.append(go(self.block_b(1, 0, 96, cb), self.full_b[k].at[0], turn("y", 1, 4)))
        copies[3].wait_recv()
        add_into(self.block_b(-1, 48, 48, cb), self.half_b[k].at[1])
        sent.append(go(self.block_b(-1, 0, 96, cb), self.full_b[k].at[1], turn("y", -1, 4)))
        self.copies[k, 2] = sent

    def r2(self, k):
        ca, cb = map(cols_of, CHUNKS[k])
        go, copies = self.wires.go, self.copies[k, 2]
        copies[0].wait_recv()
        copies[1].wait_recv()
        add_into(
            self.block_a(0, 0, 384, ca), self.full_a[k].at[pl.ds(0, 1)], self.full_a[k].at[pl.ds(1, 1)]
        )
        sent = [
            go(self.sub_a(2, 0, 48, ca), self.half2[k][0].at[pl.ds(0, 1)], turn("y", 1, 4)),
            go(self.sub_a(2, 48, 48, ca), self.half2[k][0].at[pl.ds(1, 1)], turn("y", -1, 4)),
        ]
        copies[2].wait_recv()
        copies[3].wait_recv()
        add_into(self.block_b(0, 0, 96, cb), self.full_b[k].at[0], self.full_b[k].at[1])
        sent += [
            go(self.sub_b(2, 0, 48, cb), self.half2[k][1].at[pl.ds(0, 1)], turn("z", 1, 4)),
            go(self.sub_b(2, 48, 48, cb), self.half2[k][1].at[pl.ds(1, 1)], turn("z", -1, 4)),
        ]
        self.copies[k, 3] = sent

    def r2b(self, k):
        go, copies = self.wires.go, self.copies[k, 3]
        sent = []
        for colour, (sub, axis) in enumerate(((self.sub_a, "y"), (self.sub_b, "z"))):
            cols = cols_of(CHUNKS[k][colour])
            half, full = self.half2[k][colour], self.full2[k][colour]
            copies[2 * colour].wait_recv()
            add_into(sub(1, 0, 48, cols), half.at[pl.ds(0, 1)])
            sent.append(go(sub(1, 0, 96, cols), full.at[pl.ds(0, 1)], turn(axis, 1, 4)))
            copies[2 * colour + 1].wait_recv()
            add_into(sub(-1, 48, 48, cols), half.at[pl.ds(1, 1)])
            sent.append(go(sub(-1, 0, 96, cols), full.at[pl.ds(1, 1)], turn(axis, -1, 4)))
        self.copies[k, 4] = sent

    def r3(self, k):
        go, copies = self.wires.go, self.copies[k, 4]
        (a0, an), (b0, bn) = CHUNKS[k]
        for colour, sub in enumerate((self.sub_a, self.sub_b)):
            cols, full = cols_of(CHUNKS[k][colour]), self.full2[k][colour]
            copies[2 * colour].wait_recv()
            copies[2 * colour + 1].wait_recv()
            add_into(sub(0, 0, 96, cols), full.at[pl.ds(0, 1)], full.at[pl.ds(1, 1)])
        part = self.g.at[self.z, rows_of(96 * self.y + 48 * (1 - self.xh), 48), pl.ds(a0, an + bn)]
        self.copies[k, 5] = [go(part, self.last.at[:, pl.ds(a0, an + bn)], turn("xh", 1, 2))]

    def done(self, k):
        (a0, an), (b0, bn) = CHUNKS[k]
        self.copies[k, 5][0].wait_recv()
        cols = pl.ds(a0, an + bn)
        own = self.g[self.z, rows_of(96 * self.y + 48 * self.xh, 48), cols]
        self.out[:, cols] = own.astype(F32) + self.last[:, cols].astype(F32)


def scatter_buffers():
    shapes = []
    for (a0, an), (b0, bn) in CHUNKS:
        shapes += [
            pltpu.VMEM((2, 192, an), BF),
            pltpu.VMEM((2, 384, an), BF),
            pltpu.VMEM((2, 4, 48, bn), BF),
            pltpu.VMEM((2, 4, 96, bn), BF),
            pltpu.VMEM((2, 48, an), BF),
            pltpu.VMEM((2, 96, an), BF),
            pltpu.VMEM((2, 48, bn), BF),
            pltpu.VMEM((2, 96, bn), BF),
        ]
    return shapes


def make_scatter(wires, g, bufs, last, out):
    n = len(CHUNKS)
    groups = [bufs[8 * k : 8 * k + 8] for k in range(n)]
    return Scatter(
        wires,
        g,
        [b[0] for b in groups],
        [b[1] for b in groups],
        [b[2] for b in groups],
        [b[3] for b in groups],
        [(b[4], b[6]) for b in groups],
        [(b[5], b[7]) for b in groups],
        last,
        out,
    )


def gather_kernel(shard_ref, out_ref, w, send, recv, local_sem):
    z, y, xh = (lax.axis_index(a) for a in FSDP)
    own = pltpu.make_async_copy(shard_ref, w.at[z, rows_of(96 * y + 48 * xh, 48), :], local_sem)
    own.start()
    greet()
    own.wait()
    wires = Wires(send, recv)
    ag = Gather(wires, w)
    n = len(CHUNKS)
    for k in range(n):
        ag.s1(k)
    ag.s2(0)
    ag.s2(1)
    ag.s2b(0)
    ag.s3(0)
    ag.s2b(1)
    ag.s2(2)
    ag.s3b(0)
    ag.s3(1)
    ag.s2b(2)
    ag.s2(3)
    ag.s3(2)
    ag.s3b(1)
    ag.s2b(3)
    ag.s3b(2)
    ag.s3(3)
    ag.s3b(3)
    for k in range(n):
        ag.done(k)
    wires.drain()
    back = pltpu.make_async_copy(w, out_ref, local_sem)
    back.start()
    back.wait()


def gather_rows(shard):
    return pl.pallas_call(
        gather_kernel,
        out_shape=jax.ShapeDtypeStruct((4, 384, WIDTH), BF),
        in_specs=[pl.BlockSpec(memory_space=pl.ANY)],
        out_specs=pl.BlockSpec(memory_space=pl.ANY),
        scratch_shapes=[
            pltpu.VMEM((4, 384, WIDTH), BF),
            pltpu.SemaphoreType.DMA((17 * len(CHUNKS),)),
            pltpu.SemaphoreType.DMA((17 * len(CHUNKS),)),
            pltpu.SemaphoreType.DMA,
        ],
        compiler_params=pltpu.CompilerParams(
            collective_id=0, has_side_effects=True, vmem_limit_bytes=VMEM_LIMIT
        ),
        name="gather_rows",
    )(shard)


def scatter_kernel(g_ref, out_ref, g, last, send, recv, local_sem, *bufs):
    own = pltpu.make_async_copy(g_ref, g, local_sem)
    own.start()
    greet()
    own.wait()
    wires = Wires(send, recv)
    rs = make_scatter(wires, g, bufs, last, out_ref)
    order = (3, 2, 1, 0)
    for k in order:
        rs.r1(k)
    for k in order:
        rs.r1b(k)
    for k in order:
        rs.r2(k)
    for k in order:
        rs.r2b(k)
    for k in order:
        rs.r3(k)
    for k in order:
        rs.done(k)
    wires.drain()


def scatter_rows(g):
    return pl.pallas_call(
        scatter_kernel,
        out_shape=jax.ShapeDtypeStruct((48, WIDTH), F32),
        in_specs=[pl.BlockSpec(memory_space=pl.ANY)],
        out_specs=pl.BlockSpec(memory_space=pltpu.VMEM),
        scratch_shapes=[
            pltpu.VMEM((4, 384, WIDTH), BF),
            pltpu.VMEM((48, WIDTH), BF),
            pltpu.SemaphoreType.DMA((17 * len(CHUNKS),)),
            pltpu.SemaphoreType.DMA((17 * len(CHUNKS),)),
            pltpu.SemaphoreType.DMA,
            *scatter_buffers(),
        ],
        compiler_params=pltpu.CompilerParams(
            collective_id=1, has_side_effects=True, vmem_limit_bytes=VMEM_LIMIT
        ),
        name="scatter_rows",
    )(g)


def normalize(stream):
    mean_part = jnp.mean(stream, axis=-1, keepdims=True)
    centred = stream - mean_part
    rstd = lax.rsqrt(jnp.mean(centred * centred, axis=-1, keepdims=True) + ln_eps)
    return (centred * rstd, rstd)


def norm_back(normed, rstd, incoming):
    first = jnp.mean(incoming, axis=-1, keepdims=True)
    second = jnp.mean(incoming * normed, axis=-1, keepdims=True)
    return rstd * (incoming - first - normed * second)


def gelu_tanh(hidden):
    return jax.nn.gelu(hidden, approximate=True)


def nn(a, b):
    return jnp.dot(a, b, preferred_element_type=F32)


def nt(a, b):
    return lax.dot_general(a, b, (((1,), (1,)), ((), ())), preferred_element_type=F32)


def tn(a, b):
    return lax.dot_general(a, b, (((0,), (0,)), ((), ())), preferred_element_type=F32)


def spread(rows):
    return lax.all_gather(rows, SP, axis=0, tiled=True)


def collect(part):
    return lax.psum_scatter(part.astype(BF), SP, scatter_dimension=0, tiled=True).astype(F32)


def body(tokens, modulation, w_qkv, w_out, w_in, w_back, out_grad):
    heads = w_qkv.shape[3] // HEAD_DIM
    own = w_qkv.shape[3]
    scale = 1.0 / math.sqrt(32 * 512)
    c = temper / math.sqrt(HEAD_DIM)
    shard = jnp.concatenate(
        [w_qkv[0].reshape(48, 3 * own), w_out[0].T, w_in[0], w_back[0].T], axis=1
    )
    w = gather_rows(shard).reshape(1536, WIDTH)
    wq, wot, wi, wbt = w[:, :1152], w[:, 1152:1536], w[:, 1536:3072], w[:, 3072:]
    m = modulation[0, 0][:, None, :]
    x = tokens[0].astype(F32)
    dx = out_grad[0].astype(F32)
    n1, r1 = normalize(x)
    a1 = spread((n1 * (1.0 + m[1]) + m[0]).astype(BF))
    dm = spread((m[5] * dx).astype(BF))
    qkv = nn(a1, wq).astype(BF).reshape(512, 3, heads, HEAD_DIM).transpose(1, 2, 0, 3)
    q, k, v = qkv[0], qkv[1], qkv[2]
    s = jnp.einsum("hqd,hkd->hqk", q, k, preferred_element_type=F32) * c
    p = jax.nn.softmax(s, axis=-1)
    o = jnp.einsum("hqk,hkd->hqd", p.astype(BF), v, preferred_element_type=F32)
    o = o.astype(BF).transpose(1, 0, 2).reshape(512, own)
    mid = x + m[2] * collect(nt(o, wot))
    n2, r2 = normalize(mid)
    a2 = spread((n2 * (1.0 + m[4]) + m[3]).astype(BF))
    u = nn(a2, wi)
    g, pull = jax.vjp(gelu_tanh, u)
    g = g.astype(BF)
    final = (mid + m[5] * collect(nt(g, wbt))).astype(BF)
    du = pull(nn(dm, wbt))[0].astype(BF)
    dmid = dx + norm_back(n2, r2, collect(nt(du, wi)) * (1.0 + m[4]))
    da = spread((m[2] * dmid).astype(BF))
    do = nn(da, wot).astype(BF).reshape(512, heads, HEAD_DIM).transpose(1, 0, 2)
    dp = jnp.einsum("hqd,hkd->hqk", do, v, preferred_element_type=F32)
    ds = c * p * (dp - jnp.sum(p * dp, axis=-1, keepdims=True))
    ds = ds.astype(BF)
    dq = jnp.einsum("hqk,hkd->hqd", ds, k, preferred_element_type=F32)
    dk = jnp.einsum("hqk,hqd->hkd", ds, q, preferred_element_type=F32)
    dv = jnp.einsum("hqk,hqd->hkd", p.astype(BF), do, preferred_element_type=F32)
    dqkv = jnp.stack([dq, dk, dv]).astype(BF).transpose(2, 0, 1, 3).reshape(512, 3 * own)
    dlast = dmid + norm_back(n1, r1, collect(nt(dqkv, wq)) * (1.0 + m[1]))
    grads = jnp.concatenate([tn(a1, dqkv), tn(da, o), tn(a2, du), tn(dm, g)], axis=1)
    sums = scatter_rows((grads * scale).astype(BF).reshape(4, 384, WIDTH))
    return (
        final[None],
        dlast[None],
        sums[:, :1152].reshape(1, 48, 3, own),
        sums[:, 1152:1536].T[None],
        sums[:, 1536:3072][None],
        sums[:, 3072:].T[None],
    )


def solution(mesh):
    torus = Mesh(mesh.devices.reshape(4, 4, 2, 2, 2), FSDP + SP)
    return jax.shard_map(
        body,
        mesh=torus,
        in_specs=(
            P(FSDP, SP, None),
            P(FSDP, None, None, None),
            P(None, FSDP, None, SP),
            P(None, SP, FSDP),
            P(None, FSDP, SP),
            P(None, SP, FSDP),
            P(FSDP, SP, None),
        ),
        out_specs=(
            P(FSDP, SP, None),
            P(FSDP, SP, None),
            P(None, FSDP, None, SP),
            P(None, SP, FSDP),
            P(None, FSDP, SP),
            P(None, SP, FSDP),
        ),
        check_vma=False,
    )
```

time: 1320 us -> 465 us (0.35); the launches traced: 1300 us -> 464 us
  waiting for transfers between devices: 861 us -> 122 us
  local copies, waits for them, and re-layouts: 298 us -> 18.2 us
  Pallas kernels: 0 us -> 187 us
  other arithmetic: 58.8 us -> 39.8 us
  matrix products: 67.9 us -> 81.3 us
    unnamed x14 -> x8, waiting for transfers between devices: 616 us -> 0.13 us
    pallas_call x0 -> x2, Pallas kernels: none -> 187 us  [the longest x1 96.3 us: gather_rows(): pl.pallas_call(gather_kernel, out_shape=jax.ShapeDtypeStruct((4, 384, WID...]
    unnamed x275 -> x45, local copies, waits for them, and re-layouts: 122 us -> 8.15 us
    another operation x21 -> x0, local copies, waits for them, and re-layouts: 105 us -> none  [the longest x7 90.1 us: cut_along(): return jnp.stack(jnp.split(value, count, axis=dim))]
    all_gather x5 -> x4, waiting for transfers between devices: 150 us -> 58.1 us  [spread(): return lax.all_gather(rows, SP, axis=0, tiled=True)]
    reduce_scatter x7 -> x4, waiting for transfers between devices: 95.7 us -> 64.2 us  [collect(): lax.psum_scatter(part.astype(BF), SP, scatter_dimension=0, tiled=True)]
    concatenate x3 -> x1, other arithmetic: 32.5 us -> 1.78 us  [body(): jnp.concatenate([w_qkv[0].reshape(48, 3 * own), w_out[0].T, w_in[0], w_ba...]
    transpose x5 -> x0, local copies, waits for them, and re-layouts: 19 us -> none  [the longest x2 15.2 us: laid_out(): blocks = jnp.moveaxis(blocks, 0, dim)]
  transfers between devices with their start and end apart: 13 -> 8, of which waited for: 10 -> 6; matrix products, arithmetic and copies ran while one was open for 21% -> 15% of each run, Pallas kernels for 0% -> 40%
where the time goes in v1:
time: 465 us; the launch traced here: 464 us
  Pallas kernels  187 us (40%)
  waiting for transfers between devices  122 us (26%)
  matrix products  81.3 us (17%)
  other arithmetic  39.8 us (9%)
  local copies, waits for them, and re-layouts  18.2 us (4%)
  between operations  14.5 us (3%)
    pallas_call x1, Pallas kernels, gather_rows(): pl.pallas_call(gather_kernel, out_shape=jax.ShapeDtypeStruct((4, 384, WID...  96.3 us
    pallas_call x1, Pallas kernels, scatter_rows(): pl.pallas_call(scatter_kernel, out_shape=jax.ShapeDtypeStruct((48, WIDTH)...  90.5 us
    reduce_scatter x4, waiting for transfers between devices, collect(): lax.psum_scatter(part.astype(BF), SP, scatter_dimension=0, tiled=True)  64.2 us
    all_gather x4, waiting for transfers between devices, spread(): return lax.all_gather(rows, SP, axis=0, tiled=True)  58.1 us
    dot_general x4, matrix products, nn(): return jnp.dot(a, b, preferred_element_type=F32)  22.9 us
    dot_general x4, matrix products, tn(): lax.dot_general(a, b, (((0,), (0,)), ((), ())), preferred_element_type=F32)  22.9 us
    dot_general x4, matrix products, nt(): lax.dot_general(a, b, (((1,), (1,)), ((), ())), preferred_element_type=F32)  22.5 us
    convert_element_type x1, other arithmetic, body(): sums = scatter_rows((grads * scale).astype(BF).reshape(4, 384, WIDTH))  14.2 us
  transfers between devices with their start and end apart: 8, of which 6 were waited for; matrix products, arithmetic and copies ran while one was open for 15% of the time, Pallas kernels for 40%

profile of v1, /device:TPU:0, one launch (start us, length us, event | category | flops | bytes accessed | tf_op | source)
XLA Modules:
  0.0 463.7 jit_solution(3127852463059744207)
XLA Ops:
  7.2 1.1 convert_reduce_fusion
  8.4 1.2 fusion.58
  9.6 1.5 slice_reduce_fusion.1
  11.1 2.0 fusion.52
  13.2 1.0 copy.28
  14.2 1.8 pad_maximum_fusion.1.shard_ref
  16.0 96.3 %gather_rows.1 = bf16[4,384,4608]{2,1,0:T(8,128)(2,1)} custom-call(bf16[48,4608]{1,0:T(8,128)(2,1)} %pad_maximum_fusion.1.shard_ref), custom_call_target="tpu_custom_call" | custom-call | tf_op jit(solution)/shard_map/gather_rows/pallas_call | solution.py:334
  112.4 4.7 %fusion.23 = bf16[512,1152]{1,0:T(8,128)(2,1)S(1)} fusion(bf16[512,1536]{1,0:T(8,128)(2,1)} %all-gather.5.cloned.1.call-done, bf16[1536,4608]{1,0:T(8,128)(2,1)} %bitcast.134), kind=kOutput, calls=%fused_computation.28 | convolution fusion | flops 1812529152 | bytes 6291456 | tf_op jit(solution)/shard_map/dot_general | solution.py:414
  117.1 0.6 copy.29
  117.7 0.7 copy.30
  118.4 1.0 copy-done.2
  119.4 0.6 fusion.65
  120.0 1.7 copy-done.1
  121.7 1.9 fusion.78
  123.6 0.6 copy-done.11
  124.2 4.9 %convolution_convert_fusion.4 = bf16[3,512,128]{1,2,0:T(8,128)(2,1)} fusion(bf16[3,3,512,128]{3,2,1,0:T(8,128)(2,1)} %bitcast.145, f32[3,512]{1,0:T(4,128)S(1)} %get-tuple-element.33, f32[3,512,512]{1,2,0:T(8,128)} %copy-done.1), kind=kOutput, calls=%fused_computation.40 | convolution fusion | flops 205457408 | bytes 7084032 | tf_op jit(solution)/shard_map/hqk,hkd->hqd/dot_general | solution.py:453
  129.1 3.6 convolution_convert_fusion
  132.8 21.6 %reduce-scatter.5.cloned.1.call-done = bf16[128,1536]{1,0:T(8,128)(2,1)} async-done(((bf16[512,1536]{1,0:T(8,128)(2,1)}), bf16[128,1536]{1,0:T(8,128)(2,1)}) %reduce-scatter.5.cloned.1.call-update) | async-done | bytes 393232 | tf_op jit(solution)/shard_map/reduce_scatter | solution.py:430
  154.4 1.2 fusion.67
  155.6 1.3 multiply_reduce_fusion.3
  156.9 0.6 copy-done.16
  157.5 2.0 add_convert_fusion.1
  159.5 0.0 all-gather.9.cloned.1.call-start
  159.6 1.8 fusion.59
  161.4 0.2 reduce-scatter.9.cloned.1.call-start
  161.6 23.5 %all-gather.7.cloned.1.call-done = bf16[512,1536]{1,0:T(8,128)(2,1)} async-done(((bf16[128,1536]{1,0:T(8,128)(2,1)}), bf16[512,1536]{1,0:T(8,128)(2,1)}) %all-gather.7.cloned.1.call-update) | async-done | bytes 1572880 | tf_op jit(solution)/shard_map/all_gather | solution.py:426
  185.1 7.1 %fusion.8 = f32[512,1536]{1,0:T(8,128)} fusion(bf16[512,1536]{1,0:T(8,128)(2,1)} %all-gather.7.cloned.1.call-done, bf16[1536,4608]{1,0:T(8,128)(2,1)} %bitcast.136), kind=kOutput, calls=%fused_computation.11 | convolution fusion | flops 2415919104 | bytes 9437184 | tf_op jit(solution)/shard_map/dot_general | solution.py:414
  192.2 20.6 %all-gather.9.cloned.1.call-done = bf16[512,1536]{1,0:T(8,128)(2,1)} async-done(((bf16[128,1536]{1,0:T(8,128)(2,1)}), bf16[512,1536]{1,0:T(8,128)(2,1)}) %all-gather.9.cloned.1.call-update) | async-done | bytes 1572880 | tf_op jit(solution)/shard_map/all_gather | solution.py:426
  212.7 7.8 %fusion.16 = bf16[512,1536]{1,0:T(8,128)(2,1)S(1)} fusion(f32[512,1536]{1,0:T(8,128)} %fusion.8, bf16[512,1536]{1,0:T(8,128)(2,1)} %all-gather.9.cloned.1.call-done, bf16[1536,4608]{1,0:T(8,128)(2,1)} %bitcast.137), kind=kOutput, calls=%fused_computation.19 | convolution fusion | flops 2431647744 | bytes 11010048 | tf_op jit(solution)/shard_map/dot_general | solution.py:414
  220.6 1.1 copy-done.20
  221.7 6.1 %fusion.29 = bf16[512,1536]{1,0:T(8,128)(2,1)} fusion(bf16[512,1536]{1,0:T(8,128)(2,1)S(1)} %fusion.16, bf16[1536,4608]{1,0:T(8,128)(2,1)} %bitcast.138), kind=kOutput, calls=%fused_computation.30 | convolution fusion | flops 2416705536 | bytes 7864320 | tf_op jit(solution)/shard_map/dot_general | solution.py:418
  227.9 7.2 %fusion.32 = bf16[512,1536]{1,0:T(8,128)(2,1)} fusion(bf16[1536,4608]{1,0:T(8,128)(2,1)} %bitcast.139, f32[512,1536]{1,0:T(8,128)} %fusion.8), kind=kOutput, calls=%fused_computation.31 | convolution fusion | flops 2423783424 | bytes 9437184 | tf_op jit(solution)/shard_map/dot_general | solution.py:418
  235.3 17.6 %reduce-scatter.9.cloned.1.call-done = bf16[128,1536]{1,0:T(8,128)(2,1)} async-done(((bf16[512,1536]{1,0:T(8,128)(2,1)}), bf16[128,1536]{1,0:T(8,128)(2,1)}) %reduce-scatter.9.cloned.1.call-update) | async-done | bytes 393232 | tf_op jit(solution)/shard_map/reduce_scatter | solution.py:430
  252.8 1.5 fusion.61
  254.3 0.5 broadcast_multiply_fusion.2
  254.9 25.0 %reduce-scatter.7.cloned.1.call-done = bf16[128,1536]{1,0:T(8,128)(2,1)} async-done(((bf16[512,1536]{1,0:T(8,128)(2,1)}), bf16[128,1536]{1,0:T(8,128)(2,1)}) %reduce-scatter.7.cloned.1.call-update) | async-done | bytes 393232 | tf_op jit(solution)/shard_map/reduce_scatter | solution.py:430
  279.8 3.2 multiply_convert_fusion.2
  283.0 0.3 reduce-scatter.11.cloned.1.call-start
  283.3 2.6 copy.54
  285.9 8.7 %fusion.69 = f32[1536,1536]{1,0:T(8,128)} fusion(bf16[512,1536]{1,0:T(8,128)(2,1)} %all-gather.9.cloned.1.call-done, f32[512,1536]{1,0:T(8,128)} %fusion.8), kind=kOutput, calls=%fused_computation.106 | convolution fusion | flops 2422996992 | bytes 14155776 | tf_op jit(solution)/shard_map/dot_general | solution.py:422
  294.6 14.0 %all-gather.11.cloned.1.call-done = bf16[512,1536]{1,0:T(8,128)(2,1)} async-done(((bf16[128,1536]{1,0:T(8,128)(2,1)}), bf16[512,1536]{1,0:T(8,128)(2,1)}) %all-gather.11.cloned.1.call-update) | async-done | bytes 1572880 | tf_op jit(solution)/shard_map/all_gather | solution.py:426
  308.6 3.3 convolution_convert_fusion.5
  312.0 4.9 %fusion.41 = bf16[1,3,512,128]{2,3,1,0:T(8,128)(2,1)} fusion(bf16[3,512,128]{1,2,0:T(8,128)(2,1)} %bitcast.163, f32[3,512]{1,0:T(4,128)S(1)} %copy-done.12, f32[3,512,512]{1,2,0:T(8,128)} %copy-done.1), kind=kOutput, calls=%fused_computation.44 | convolution fusion | flops 205457408 | bytes 3938304 | tf_op jit(solution)/shard_map/hqk,hqd->hkd/dot_general | solution.py:471
  316.8 1.7 multiply_reduce_fusion
  318.5 0.8 multiply_convert_fusion
  319.4 0.4 copy-done.3
  319.8 0.6 fusion.40
  320.4 0.4 fusion.39
  320.9 0.1 pad_maximum_fusion
  321.0 1.0 copy-done.7
  322.0 5.5 %fusion.26 = bf16[512,1536]{1,0:T(8,128)(2,1)} fusion(bf16[512,1152]{0,1:T(8,128)(2,1)S(1)} %bitcast.154, bf16[1536,4608]{1,0:T(8,128)(2,1)} %bitcast.141), kind=kOutput, calls=%fused_computation.29 | convolution fusion | flops 1812725760 | bytes 6291456 | tf_op jit(solution)/shard_map/dot_general | solution.py:418
  327.6 6.6 %fusion.81 = f32[1536,1536]{1,0:T(8,128)} fusion(bf16[512,1536]{1,0:T(8,128)(2,1)S(1)} %copy-done.19, bf16[512,1536]{1,0:T(8,128)(2,1)} %copy-done.20), kind=kOutput, calls=%fused_computation.110 | convolution fusion | flops 2415919104 | bytes 12582912 | tf_op jit(solution)/shard_map/dot_general | solution.py:422
  334.1 1.6 copy.56
  335.7 2.6 fusion.80
  338.3 5.1 %fusion.79 = f32[4,384,1152]{2,1,0:T(8,128)} fusion(bf16[4,384,512]{2,1,0:T(8,128)(2,1)S(1)} %bitcast.153, bf16[512,1152,1]{0,1,2:T(8,128)(2,1)S(1)} %bitcast.155), kind=kOutput, calls=%fused_computation.108 | convolution fusion | flops 1811939328 | bytes 9830400 | tf_op jit(solution)/shard_map/dot_general | solution.py:422
  343.4 14.2 %fusion.1.g_ref = bf16[4,384,4608]{2,1,0:T(8,128)(2,1)} fusion(f32[4,384,1536]{2,1,0:T(8,128)} %bitcast.142, f32[4,384,1536]{2,1,0:T(8,128)} %bitcast.143, f32[4,384,384]{2,1,0:T(8,128)S(1)} %fusion.80, f32[4,384,1152]{2,1,0:T(8,128)} %fusion.79), kind=kLoop, calls=%fused_computation.2 | loop fusion | flops 35389440 | bytes 42467328 | tf_op jit(solution)/shard_map/convert_element_type | solution.py:475
  357.6 90.5 %scatter_rows.1 = f32[48,4608]{1,0:T(8,128)} custom-call(bf16[4,384,4608]{2,1,0:T(8,128)(2,1)} %fusion.1.g_ref), custom_call_target="tpu_custom_call" | custom-call | tf_op jit(solution)/shard_map/scatter_rows/pallas_call | solution.py:376
  448.1 1.0 slice.74
  449.1 0.1 reshape.122
  449.2 0.7 copy.43
  449.9 1.5 slice_bitcast_fusion.11
  451.4 1.9 slice_bitcast_fusion.9
  453.3 1.3 fusion.60
  454.7 2.2 fusion.57
  (57 shorter events, 0.5 us)
Async XLA Ops:
  7.2 105.2 %all-gather.5.cloned.1.call-start = ((), (), s32[]{:S(2)}) async-start(), calls=%async_computation.4 | async-start | bytes 1966080 | tf_op jit(solution)/shard_map/all_gather | solution.py:426
  8.3 4.8 %copy-start.14 = (f32[128]{0:T(128)}, f32[128]{0:T(128)S(1)}, u32[]{:S(2)}) copy-start(f32[128]{0:T(128)S(1)} %broadcast_multiply_fusion.5) | copy-start | bytes 1540
  9.6 3.6 copy-start.17
  13.2 141.2 %reduce-scatter.5.cloned.1.call-start = ((), (), s32[]{:S(2)}) async-start(), calls=%async_computation.5 | async-start | bytes 1966080 | tf_op jit(solution)/shard_map/reduce_scatter | solution.py:430
  118.4 1.0 copy-start.2
  120.0 1.7 copy-start.1
  123.6 0.6 copy-start.11
  129.1 25.3 %copy-start = (bf16[1,128,1536]{2,1,0:T(8,128)(2,1)S(1)}, bf16[1,128,1536]{2,1,0:T(8,128)(2,1)}, u32[]{:S(2)}) copy-start(bf16[1,128,1536]{2,1,0:T(8,128)(2,1)} %param.7) | copy-start | bytes 1179652
  132.7 52.4 %all-gather.7.cloned.1.call-start = ((), (), s32[]{:S(2)}) async-start(), calls=%async_computation.6 | async-start | bytes 1966080 | tf_op jit(solution)/shard_map/all_gather | solution.py:426
  155.6 1.3 copy-start.13
  156.9 0.6 copy-start.16
  159.5 53.2 %all-gather.9.cloned.1.call-start = ((), (), s32[]{:S(2)}) async-start(), calls=%async_computation.8 | async-start | bytes 1966080 | tf_op jit(solution)/shard_map/all_gather | solution.py:426
  161.4 91.5 %reduce-scatter.9.cloned.1.call-start = ((), (), s32[]{:S(2)}) async-start(), calls=%async_computation.9 | async-start | bytes 1966080 | tf_op jit(solution)/shard_map/reduce_scatter | solution.py:430
  220.6 1.2 copy-start.20
  227.9 52.0 %reduce-scatter.7.cloned.1.call-start = ((), (), s32[]{:S(2)}) async-start(), calls=%async_computation.7 | async-start | bytes 1966080 | tf_op jit(solution)/shard_map/reduce_scatter | solution.py:430
  235.2 73.4 %all-gather.11.cloned.1.call-start = ((), (), s32[]{:S(2)}) async-start(), calls=%async_computation.10 | async-start | bytes 1966080 | tf_op jit(solution)/shard_map/all_gather | solution.py:426
  283.0 170.3 %reduce-scatter.11.cloned.1.call-start = ((), (), s32[]{:S(2)}) async-start(), calls=%async_computation.11 | async-start | bytes 1966080 | tf_op jit(solution)/shard_map/reduce_scatter | solution.py:430
  294.6 17.3 %copy-start.12 = (f32[3,512]{1,0:T(4,128)S(1)}, f32[3,512]{1,0:T(4,128)}, u32[]{:S(2)}) copy-start(f32[3,512]{1,0:T(4,128)} %copy-done.11) | copy-start | bytes 18436
  318.5 1.3 copy-start.3
  319.8 1.1 copy-start.10
  321.0 1.0 copy-start.7
  322.0 5.5 %copy-start.19 = (bf16[512,1536]{1,0:T(8,128)(2,1)S(1)}, bf16[512,1536]{1,0:T(8,128)(2,1)}, u32[]{:S(2)}) copy-start(bf16[512,1536]{1,0:T(8,128)(2,1)} %all-gather.7.cloned.1.call-done) | copy-start | bytes 4718596
  327.6 6.6 %copy-start.5 = (bf16[512,1536]{1,0:T(8,128)(2,1)S(1)}, bf16[512,1536]{1,0:T(8,128)(2,1)}, u32[]{:S(2)}) copy-start(bf16[512,1536]{1,0:T(8,128)(2,1)} %all-gather.11.cloned.1.call-done) | copy-start | bytes 4718596
  334.1 1.6 copy-start.9
  335.7 2.6 copy-start.6
  335.7 2.6 copy-start.8
  357.5 95.8 %copy-start.15 = (f32[128]{0:T(128)S(1)}, f32[128]{0:T(128)}, u32[]{:S(2)}) copy-start(f32[128]{0:T(128)} %copy-done.14) | copy-start | bytes 1540
  357.5 95.8 %copy-start.18 = (f32[128]{0:T(128)S(1)}, f32[128]{0:T(128)}, u32[]{:S(2)}) copy-start(f32[128]{0:T(128)} %copy-done.17) | copy-start | bytes 1540
  448.1 6.6 %copy-start.4 = (f32[128,1536]{1,0:T(8,128)S(1)}, f32[128,1536]{1,0:T(8,128)}, u32[]{:S(2)}) copy-start(f32[128,1536]{1,0:T(8,128)} %get-tuple-element.29) | copy-start | bytes 2359300
Sparse Core Ops, SparseCore 0:
  13.3 30.8 all-gather.4
  132.9 21.4 reduce-scatter.4
  159.6 25.4 all-gather.6
  187.2 25.5 all-gather.8
  228.0 24.7 reduce-scatter.8
  255.1 24.6 reduce-scatter.6
  283.2 25.4 all-gather.10
  327.7 24.7 reduce-scatter.10

commit v2 on v1

--- a/solution.py
+++ b/solution.py
@@ -18,7 +18,7 @@
 
 ln_eps = 1e-06
 temper = 2.5
-VMEM_LIMIT = 66_000_000
+VMEM_LIMIT = 67_000_000
 
 CHUNKS = (
     ((0, 640), (640, 512)),
@@ -55,6 +55,10 @@
         copy.start()
         self.open.append(copy)
         return copy
+
+    def sent(self, copy):
+        copy.wait_send()
+        self.open = [other for other in self.open if other is not copy]
 
     def drain(self):
         for copy in self.open:
@@ -295,187 +299,452 @@
     )
 
 
-def gather_kernel(shard_ref, out_ref, w, send, recv, local_sem):
-    z, y, xh = (lax.axis_index(a) for a in FSDP)
-    own = pltpu.make_async_copy(shard_ref, w.at[z, rows_of(96 * y + 48 * xh, 48), :], local_sem)
-    own.start()
-    greet()
-    own.wait()
+def nn(a, b):
+    return jnp.dot(a, b, preferred_element_type=F32)
+
+
+def nt(a, b):
+    return lax.dot_general(a, b, (((1,), (1,)), ((), ())), preferred_element_type=F32)
+
+
+def tn(a, b):
+    return lax.dot_general(a, b, (((0,), (0,)), ((), ())), preferred_element_type=F32)
+
+
+class Spread:
+    def __init__(self, wires, buf):
+        self.wires, self.buf = wires, buf
+        self.xl, self.c = (lax.axis_index(a) for a in SP)
+
+    def block(self, xl, c, start=0, count=128):
+        return self.buf.at[rows_of(256 * xl + 128 * c + start, count), :]
+
+    def start(self):
+        own = self.block(self.xl, self.c)
+        go = self.wires.go
+        self.far = []
+        for i in range(2):
+            part = self.block(self.xl, self.c, 64 * i, 64)
+            self.far.append(go(part, part, turn("xl", 1, 2)))
+        self.near = go(own, own, turn("c", 1, 2))
+
+    def relay(self):
+        self.relays = []
+        for i in range(2):
+            self.far[i].wait_recv()
+            part = self.block(1 - self.xl, self.c, 64 * i, 64)
+            self.relays.append(self.wires.go(part, part, turn("c", 1, 2)))
+
+    def own_half(self):
+        self.near.wait_recv()
+
+    def done(self):
+        for copy in self.relays:
+            copy.wait_recv()
+
+
+class Collect:
+    def __init__(self, wires, part, pair, cross):
+        self.wires, self.part, self.pair, self.cross = wires, part, pair, cross
+        self.xl, self.c = (lax.axis_index(a) for a in SP)
+
+    def block(self, xl, c):
+        return self.part.at[rows_of(256 * xl + 128 * c, 128), :]
+
+    def other(self):
+        self.first = self.wires.go(self.block(1 - self.xl, 1 - self.c), self.pair.at[0], turn("c", 1, 2))
+
+    def send(self):
+        self.first.wait_recv()
+        mine = self.block(1 - self.xl, self.c)
+        for i in range(2):
+            rows = pl.ds(64 * i, 64)
+            add2(mine.at[rows, :], self.pair.at[0, rows, :])
+        self.third = self.wires.go(mine, self.cross, turn("xl", 1, 2))
+
+    def own(self):
+        self.second = self.wires.go(self.block(self.xl, 1 - self.c), self.pair.at[1], turn("c", 1, 2))
+
+    def wait(self):
+        self.second.wait_recv()
+        self.third.wait_recv()
+
+    def release(self):
+        for copy in (self.first, self.second, self.third):
+            self.wires.sent(copy)
+
+    def rows(self, start, count):
+        at = rows_of(256 * self.xl + 128 * self.c + start, count)
+        total = self.part[at, :].astype(F32) + self.pair[1, pl.ds(start, count), :].astype(F32)
+        return total + self.cross[pl.ds(start, count), :].astype(F32)
+
+
+def add2(dst, src):
+    rows = dst.shape[0]
+
+    @pl.loop(0, rows // 16)
+    def _(i):
+        at = (pl.ds(pl.multiple_of(i * 16, 16), 16), slice(None))
+        dst[at] = (dst[at].astype(F32) + src[at].astype(F32)).astype(dst.dtype)
+
+
+def normalize(stream):
+    mean_part = jnp.mean(stream, axis=-1, keepdims=True)
+    centred = stream - mean_part
+    rstd = lax.rsqrt(jnp.mean(centred * centred, axis=-1, keepdims=True) + ln_eps)
+    return (centred * rstd, rstd)
+
+
+def norm_back(normed, rstd, incoming):
+    first = jnp.mean(incoming, axis=-1, keepdims=True)
+    second = jnp.mean(incoming * normed, axis=-1, keepdims=True)
+    return rstd * (incoming - first - normed * second)
+
+
+BLOCK = 16
+ROOT = math.sqrt(2.0 / math.pi)
+
+
+def by_rows(fn):
+    @pl.loop(0, 128 // BLOCK)
+    def _(i):
+        fn(pl.multiple_of(i * BLOCK, BLOCK))
+
+
+def block_kernel(
+    x_ref, m_ref, og_ref, wq_ref, wo_ref, wi_ref, wb_ref,
+    final_ref, ig_ref, sums_ref,
+    w, g, last, a1, dm, a2, da, qkv, o, do, gp, act, part0, part1, pair0, cross0, pair1, cross1,
+    mid, dmid, acck, accv, send, recv, local_sem, *bufs,
+):
+    z, y, xh, xl, c = (lax.axis_index(a) for a in FSDP + SP)
+    shard_rows = rows_of(96 * y + 48 * xh, 48)
+    loads = []
+    for i, (ref, at, count) in enumerate(
+        ((wq_ref, 0, 1152), (wo_ref, 1152, 384), (wi_ref, 1536, 1536), (wb_ref, 3072, 1536))
+    ):
+        load = pltpu.make_async_copy(ref, w.at[z, shard_rows, pl.ds(at, count)], local_sem.at[i])
+        load.start()
+        loads.append(load)
+    greet(sp=True)
     wires = Wires(send, recv)
     ag = Gather(wires, w)
-    n = len(CHUNKS)
-    for k in range(n):
-        ag.s1(k)
+    rs = make_scatter(wires, g, bufs, last, sums_ref)
+    own_row = 256 * xl + 128 * c
+    own_start, other_start = 256 * xl, 256 * (1 - xl)
+    scale = 1.0 / math.sqrt(32 * 512)
+    factor = temper / math.sqrt(HEAD_DIM)
+
+    def mod(i):
+        return m_ref[pl.ds(i, 1), :]
+
+    def own(start):
+        return (rows_of(own_row + start, BLOCK), slice(None))
+
+    def weights(start, count):
+        return w[:, :, pl.ds(start, count)].reshape(1536, count)
+
+    loads[0].wait()
+    ag.s1(0)
+
+    def first_norm(r):
+        n1, _ = normalize(x_ref[pl.ds(r, BLOCK), :].astype(F32))
+        a1[own(r)] = (n1 * (1.0 + mod(1)) + mod(0)).astype(BF)
+
+    by_rows(first_norm)
+    sp1 = Spread(wires, a1)
+    sp1.start()
+    for load in loads[1:]:
+        load.wait()
+    ag.s1(1)
+    ag.s1(2)
     ag.s2(0)
-    ag.s2(1)
+
+    def gate_grad(r):
+        dm[own(r)] = (mod(5) * og_ref[pl.ds(r, BLOCK), :].astype(F32)).astype(BF)
+
+    by_rows(gate_grad)
     ag.s2b(0)
     ag.s3(0)
+    ag.s2(1)
+    ag.s1(3)
+    sp1.relay()
+    spm = Spread(wires, dm)
+    spm.start()
     ag.s2b(1)
     ag.s2(2)
     ag.s3b(0)
     ag.s3(1)
     ag.s2b(2)
     ag.s2(3)
+    sp1.own_half()
+    sp1.done()
+    ag.done(0)
+
+    def project_qkv(start, count):
+        qkv[:, pl.ds(start, count)] = nn(a1[...], weights(start, count)).astype(BF)
+
+    @pl.loop(0, 4)
+    def _(j):
+        project_qkv(pl.multiple_of(j * 256, 256), 256)
+
+    project_qkv(1024, 128)
+    ag.s3b(1)
     ag.s3(2)
-    ag.s3b(1)
     ag.s2b(3)
+
+    def probs(q, k):
+        s = nt(q, k) * factor
+        e = jnp.exp(s - jnp.max(s, axis=-1, keepdims=True))
+        return e, 1.0 / jnp.sum(e, axis=-1, keepdims=True)
+
+    def lanes(h, which):
+        return pl.ds(pl.multiple_of(384 * which + 128 * h, 128), 128)
+
+    @pl.loop(0, 3)
+    def _(h):
+        k, v = qkv[:, lanes(h, 1)], qkv[:, lanes(h, 2)]
+
+        @pl.loop(0, 4)
+        def _(i):
+            rows = pl.ds(pl.multiple_of(i * 128, 128), 128)
+            e, inv = probs(qkv[rows, lanes(h, 0)], k)
+            o[rows, lanes(h, 0)] = (nn(e.astype(BF), v) * inv).astype(BF)
+
+    ag.done(1)
+
+    def back_half(dst, lhs, start, at, count):
+        rows = rows_of(start, 256)
+
+        @pl.loop(0, 2)
+        def _(j):
+            rhs = w[pl.ds(2 * j, 2), :, pl.ds(at, count)].reshape(768, count)
+            dst[rows, pl.ds(pl.multiple_of(768 * j, 128), 768)] = nt(lhs[rows, :], rhs).astype(BF)
+
+    def collect(red, dst, lhs, at, count):
+        back_half(dst, lhs, other_start, at, count)
+        red.other()
+        back_half(dst, lhs, own_start, at, count)
+        red.own()
+        red.send()
+
+    red1 = Collect(wires, part0, pair0, cross0)
+    collect(red1, part0, o, 1152, 384)
+    spm.relay()
+    red1.wait()
+
+    def second_norm(r):
+        rows = pl.ds(r, BLOCK)
+        value = x_ref[rows, :].astype(F32) + mod(2) * red1.rows(r, BLOCK)
+        mid[rows, :] = value
+        n2, _ = normalize(value)
+        a2[own(r)] = (n2 * (1.0 + mod(4)) + mod(3)).astype(BF)
+
+    by_rows(second_norm)
+    sp2 = Spread(wires, a2)
+    sp2.start()
     ag.s3b(2)
     ag.s3(3)
+    sp2.relay()
+    sp2.own_half()
+    ag.done(2)
+
+    def hidden(start):
+        rows = rows_of(start, 256)
+
+        @pl.loop(0, 6)
+        def _(j):
+            at = pl.multiple_of(j * 256, 256)
+            u = nn(a2[rows, :], weights(pl.multiple_of(1536 + at, 256), 256))
+            sq = u * u
+            t = jnp.tanh(ROOT * u * (1.0 + 0.044715 * sq))
+            half = 0.5 * (1.0 + t)
+            act[rows, pl.ds(at, 256)] = (u * half).astype(BF)
+            slope = half + (0.5 * ROOT) * u * (1.0 - t * t) * (1.0 + (3 * 0.044715) * sq)
+            gp[rows, pl.ds(at, 256)] = slope.astype(BF)
+
+    hidden(own_start)
+    sp2.done()
+    hidden(other_start)
+    spm.own_half()
+    spm.done()
+
+    def grad(left, right, right_at, at, count):
+        @pl.loop(0, 4)
+        def _(j):
+            lhs = left[:, pl.ds(pl.multiple_of(384 * j, 128), 384)]
+            value = tn(lhs, right[:, pl.ds(right_at, count)]) * scale
+            g[j, :, pl.ds(at, count)] = value.astype(BF)
+
+    grad(dm, act, 0, 3072, 768)
+    grad(dm, act, 768, 3840, 768)
+    rs.r1(3)
     ag.s3b(3)
-    for k in range(n):
-        ag.done(k)
+    ag.done(3)
+
+    @pl.loop(0, 6)
+    def _(j):
+        at = pl.multiple_of(j * 256, 256)
+        cols = pl.ds(at, 256)
+        dg = nn(dm[...], weights(pl.multiple_of(3072 + at, 256), 256))
+        gp[:, cols] = (gp[:, cols].astype(F32) * dg).astype(BF)
+
+    du = gp
+    red1.release()
+    red2 = Collect(wires, part0, pair0, cross0)
+    collect(red2, part0, du, 1536, 1536)
+    rs.r1b(3)
+    grad(a2, du, 0, 1536, 768)
+    grad(a2, du, 768, 2304, 768)
+    rs.r1(2)
+    red2.wait()
+
+    def mid_grad(r):
+        rows = pl.ds(r, BLOCK)
+        n2, r2 = normalize(mid[rows, :])
+        value = og_ref[rows, :].astype(F32) + norm_back(n2, r2, red2.rows(r, BLOCK) * (1.0 + mod(4)))
+        dmid[rows, :] = value
+        da[own(r)] = (mod(2) * value).astype(BF)
+
+    by_rows(mid_grad)
+    spa = Spread(wires, da)
+    spa.start()
+    rs.r2(3)
+    back_half(part1, act, other_start, 3072, 1536)
+    back_half(part1, act, own_start, 3072, 1536)
+    spa.relay()
+    rs.r1b(2)
+    redf = Collect(wires, part1, pair1, cross1)
+    redf.other()
+    redf.own()
+    redf.send()
+    spa.own_half()
+
+    def head_grads(start):
+        rows = rows_of(start, 256)
+        do[rows, :] = nn(da[rows, :], weights(1152, 384)).astype(BF)
+
+    head_grads(own_start)
+    spa.done()
+    head_grads(other_start)
+    grad(da, o, 0, 1152, 128)
+    grad(da, o, 128, 1280, 256)
+    rs.r1(1)
+    rs.r2b(3)
+
+    @pl.loop(0, 3)
+    def _(h):
+        k, v = qkv[:, lanes(h, 1)], qkv[:, lanes(h, 2)]
+        acck[...] = jnp.zeros_like(acck)
+        accv[...] = jnp.zeros_like(accv)
+
+        @pl.loop(0, 4)
+        def _(i):
+            rows = pl.ds(pl.multiple_of(i * 128, 128), 128)
+            q = qkv[rows, lanes(h, 0)]
+            up = do[rows, lanes(h, 0)]
+            e, inv = probs(q, k)
+            p = e * inv
+            dp = nt(up, v)
+            ds = factor * p * (dp - jnp.sum(p * dp, axis=-1, keepdims=True))
+            ds = ds.astype(BF)
+            qkv[rows, lanes(h, 0)] = nn(ds, k).astype(BF)
+            acck[...] += tn(ds, q)
+            accv[...] += tn(p.astype(BF), up)
+
+        qkv[:, lanes(h, 1)] = acck[...].astype(BF)
+        qkv[:, lanes(h, 2)] = accv[...].astype(BF)
+
+    grad(a1, qkv, 0, 0, 640)
+    grad(a1, qkv, 640, 640, 512)
+    rs.r1(0)
+    red2.release()
+    red3 = Collect(wires, part0, pair0, cross0)
+    collect(red3, part0, qkv, 0, 1152)
+    rs.r2(2)
+    rs.r1b(1)
+    rs.r3(3)
+    rs.r1b(0)
+    rs.r2b(2)
+    rs.r2(1)
+    redf.wait()
+
+    def last_out(r):
+        rows = pl.ds(r, BLOCK)
+        final_ref[rows, :] = (mid[rows, :] + mod(5) * redf.rows(r, BLOCK)).astype(BF)
+
+    by_rows(last_out)
+    rs.done(3)
+    red3.wait()
+
+    def first_grad(r):
+        rows = pl.ds(r, BLOCK)
+        n1, r1 = normalize(x_ref[rows, :].astype(F32))
+        ig_ref[rows, :] = dmid[rows, :] + norm_back(n1, r1, red3.rows(r, BLOCK) * (1.0 + mod(1)))
+
+    by_rows(first_grad)
+    rs.r3(2)
+    rs.r2b(1)
+    rs.r2(0)
+    rs.done(2)
+    rs.r3(1)
+    rs.r2b(0)
+    rs.done(1)
+    rs.r3(0)
+    rs.done(0)
     wires.drain()
-    back = pltpu.make_async_copy(w, out_ref, local_sem)
-    back.start()
-    back.wait()
-
-
-def gather_rows(shard):
-    return pl.pallas_call(
-        gather_kernel,
-        out_shape=jax.ShapeDtypeStruct((4, 384, WIDTH), BF),
-        in_specs=[pl.BlockSpec(memory_space=pl.ANY)],
-        out_specs=pl.BlockSpec(memory_space=pl.ANY),
+
+
+def body(tokens, modulation, w_qkv, w_out, w_in, w_back, out_grad):
+    own = w_qkv.shape[3]
+    vmem = pl.BlockSpec(memory_space=pltpu.VMEM)
+    far = pl.BlockSpec(memory_space=pl.ANY)
+    copies = 34 * len(CHUNKS) + 32
+    rows = lambda n, dtype=BF: pltpu.VMEM((512, n), dtype)
+    final, grad_in_rows, sums = pl.pallas_call(
+        block_kernel,
+        out_shape=(
+            jax.ShapeDtypeStruct((128, 1536), BF),
+            jax.ShapeDtypeStruct((128, 1536), F32),
+            jax.ShapeDtypeStruct((48, WIDTH), F32),
+        ),
+        in_specs=[vmem, vmem, vmem, far, far, far, far],
+        out_specs=(vmem, vmem, vmem),
         scratch_shapes=[
             pltpu.VMEM((4, 384, WIDTH), BF),
-            pltpu.SemaphoreType.DMA((17 * len(CHUNKS),)),
-            pltpu.SemaphoreType.DMA((17 * len(CHUNKS),)),
-            pltpu.SemaphoreType.DMA,
+            pltpu.VMEM((4, 384, WIDTH), BF),
+            pltpu.VMEM((48, WIDTH), BF),
+            rows(1536), rows(1536), rows(1536), rows(1536),
+            rows(1152), rows(384), rows(384),
+            rows(1536), rows(1536), rows(1536), rows(1536),
+            pltpu.VMEM((2, 128, 1536), BF),
+            pltpu.VMEM((128, 1536), BF),
+            pltpu.VMEM((2, 128, 1536), BF),
+            pltpu.VMEM((128, 1536), BF),
+            pltpu.VMEM((128, 1536), F32),
+            pltpu.VMEM((128, 1536), F32),
+            rows(128, F32), rows(128, F32),
+            pltpu.SemaphoreType.DMA((copies,)),
+            pltpu.SemaphoreType.DMA((copies,)),
+            pltpu.SemaphoreType.DMA((4,)),
+            *scatter_buffers(),
         ],
         compiler_params=pltpu.CompilerParams(
             collective_id=0, has_side_effects=True, vmem_limit_bytes=VMEM_LIMIT
         ),
-        name="gather_rows",
-    )(shard)
-
-
-def scatter_kernel(g_ref, out_ref, g, last, send, recv, local_sem, *bufs):
-    own = pltpu.make_async_copy(g_ref, g, local_sem)
-    own.start()
-    greet()
-    own.wait()
-    wires = Wires(send, recv)
-    rs = make_scatter(wires, g, bufs, last, out_ref)
-    order = (3, 2, 1, 0)
-    for k in order:
-        rs.r1(k)
-    for k in order:
-        rs.r1b(k)
-    for k in order:
-        rs.r2(k)
-    for k in order:
-        rs.r2b(k)
-    for k in order:
-        rs.r3(k)
-    for k in order:
-        rs.done(k)
-    wires.drain()
-
-
-def scatter_rows(g):
-    return pl.pallas_call(
-        scatter_kernel,
-        out_shape=jax.ShapeDtypeStruct((48, WIDTH), F32),
-        in_specs=[pl.BlockSpec(memory_space=pl.ANY)],
-        out_specs=pl.BlockSpec(memory_space=pltpu.VMEM),
-        scratch_shapes=[
-            pltpu.VMEM((4, 384, WIDTH), BF),
-            pltpu.VMEM((48, WIDTH), BF),
-            pltpu.SemaphoreType.DMA((17 * len(CHUNKS),)),
-            pltpu.SemaphoreType.DMA((17 * len(CHUNKS),)),
-            pltpu.SemaphoreType.DMA,
-            *scatter_buffers(),
-        ],
-        compiler_params=pltpu.CompilerParams(
-            collective_id=1, has_side_effects=True, vmem_limit_bytes=VMEM_LIMIT
-        ),
-        name="scatter_rows",
-    )(g)
-
-
-def normalize(stream):
-    mean_part = jnp.mean(stream, axis=-1, keepdims=True)
-    centred = stream - mean_part
-    rstd = lax.rsqrt(jnp.mean(centred * centred, axis=-1, keepdims=True) + ln_eps)
-    return (centred * rstd, rstd)
-
-
-def norm_back(normed, rstd, incoming):
-    first = jnp.mean(incoming, axis=-1, keepdims=True)
-    second = jnp.mean(incoming * normed, axis=-1, keepdims=True)
-    return rstd * (incoming - first - normed * second)
-
-
-def gelu_tanh(hidden):
-    return jax.nn.gelu(hidden, approximate=True)
-
-
-def nn(a, b):
-    return jnp.dot(a, b, preferred_element_type=F32)
-
-
-def nt(a, b):
-    return lax.dot_general(a, b, (((1,), (1,)), ((), ())), preferred_element_type=F32)
-
-
-def tn(a, b):
-    return lax.dot_general(a, b, (((0,), (0,)), ((), ())), preferred_element_type=F32)
-
-
-def spread(rows):
-    return lax.all_gather(rows, SP, axis=0, tiled=True)
-
-
-def collect(part):
-    return lax.psum_scatter(part.astype(BF), SP, scatter_dimension=0, tiled=True).astype(F32)
-
-
-def body(tokens, modulation, w_qkv, w_out, w_in, w_back, out_grad):
-    heads = w_qkv.shape[3] // HEAD_DIM
-    own = w_qkv.shape[3]
-    scale = 1.0 / math.sqrt(32 * 512)
-    c = temper / math.sqrt(HEAD_DIM)
-    shard = jnp.concatenate(
-        [w_qkv[0].reshape(48, 3 * own), w_out[0].T, w_in[0], w_back[0].T], axis=1
+        name="block",
+    )(
+        tokens[0],
+        modulation[0, 0],
+        out_grad[0],
+        w_qkv[0].reshape(48, 3 * own),
+        w_out[0].T,
+        w_in[0],
+        w_back[0].T,
     )
-    w = gather_rows(shard).reshape(1536, WIDTH)
-    wq, wot, wi, wbt = w[:, :1152], w[:, 1152:1536], w[:, 1536:3072], w[:, 3072:]
-    m = modulation[0, 0][:, None, :]
-    x = tokens[0].astype(F32)
-    dx = out_grad[0].astype(F32)
-    n1, r1 = normalize(x)
-    a1 = spread((n1 * (1.0 + m[1]) + m[0]).astype(BF))
-    dm = spread((m[5] * dx).astype(BF))
-    qkv = nn(a1, wq).astype(BF).reshape(512, 3, heads, HEAD_DIM).transpose(1, 2, 0, 3)
-    q, k, v = qkv[0], qkv[1], qkv[2]
-    s = jnp.einsum("hqd,hkd->hqk", q, k, preferred_element_type=F32) * c
-    p = jax.nn.softmax(s, axis=-1)
-    o = jnp.einsum("hqk,hkd->hqd", p.astype(BF), v, preferred_element_type=F32)
-    o = o.astype(BF).transpose(1, 0, 2).reshape(512, own)
-    mid = x + m[2] * collect(nt(o, wot))
-    n2, r2 = normalize(mid)
-    a2 = spread((n2 * (1.0 + m[4]) + m[3]).astype(BF))
-    u = nn(a2, wi)
-    g, pull = jax.vjp(gelu_tanh, u)
-    g = g.astype(BF)
-    final = (mid + m[5] * collect(nt(g, wbt))).astype(BF)
-    du = pull(nn(dm, wbt))[0].astype(BF)
-    dmid = dx + norm_back(n2, r2, collect(nt(du, wi)) * (1.0 + m[4]))
-    da = spread((m[2] * dmid).astype(BF))
-    do = nn(da, wot).astype(BF).reshape(512, heads, HEAD_DIM).transpose(1, 0, 2)
-    dp = jnp.einsum("hqd,hkd->hqk", do, v, preferred_element_type=F32)
-    ds = c * p * (dp - jnp.sum(p * dp, axis=-1, keepdims=True))
-    ds = ds.astype(BF)
-    dq = jnp.einsum("hqk,hkd->hqd", ds, k, preferred_element_type=F32)
-    dk = jnp.einsum("hqk,hqd->hkd", ds, q, preferred_element_type=F32)
-    dv = jnp.einsum("hqk,hqd->hkd", p.astype(BF), do, preferred_element_type=F32)
-    dqkv = jnp.stack([dq, dk, dv]).astype(BF).transpose(2, 0, 1, 3).reshape(512, 3 * own)
-    dlast = dmid + norm_back(n1, r1, collect(nt(dqkv, wq)) * (1.0 + m[1]))
-    grads = jnp.concatenate([tn(a1, dqkv), tn(da, o), tn(a2, du), tn(dm, g)], axis=1)
-    sums = scatter_rows((grads * scale).astype(BF).reshape(4, 384, WIDTH))
     return (
         final[None],
-        dlast[None],
+        grad_in_rows[None],
         sums[:, :1152].reshape(1, 48, 3, own),
         sums[:, 1152:1536].T[None],
         sums[:, 1536:3072][None],

time: 465 us -> 211 us (0.45)
  waiting for transfers between devices: 122 us -> 0 us
  matrix products: 81.3 us -> 0 us
  other arithmetic: 39.8 us -> 0 us
  between operations: 14.5 us -> 0.65 us
  Pallas kernels: 187 us -> 200 us
  local copies, waits for them, and re-layouts: 18.2 us -> 10 us
    dot_general x18 -> x0, matrix products: 81.3 us -> none  [the longest x4 22.9 us: nn(): return jnp.dot(a, b, preferred_element_type=F32)]
    reduce_scatter x4 -> x0, waiting for transfers between devices: 64.2 us -> none  [collect(): lax.psum_scatter(part.astype(BF), SP, scatter_dimension=0, tiled=True)]
    all_gather x4 -> x0, waiting for transfers between devices: 58.1 us -> none  [spread(): return lax.all_gather(rows, SP, axis=0, tiled=True)]
    convert_element_type x6 -> x0, other arithmetic: 24.1 us -> none  [the longest x1 14.2 us: body(): sums = scatter_rows((grads * scale).astype(BF).reshape(4, 384, WIDTH))]
    pallas_call x2 -> x1, Pallas kernels: 187 us -> 200 us  [body(): pl.pallas_call(block_kernel, out_shape=(jax.ShapeDtypeStruct((128, 1536),...]
    reduce_sum x6 -> x0, other arithmetic: 7.65 us -> none  [the longest x2 2.8 us: norm_back(): first = jnp.mean(incoming, axis=-1, keepdims=True)]
  transfers between devices with their start and end apart: 8 -> 0, of which waited for: 6 -> 0; matrix products, arithmetic and copies ran while one was open for 15% -> 0% of each run, Pallas kernels for 40% -> 0%
where the time goes in v2:
time: 211 us
  Pallas kernels  200 us (95%)
  local copies, waits for them, and re-layouts  10 us (5%)
    pallas_call x1, Pallas kernels, body(): pl.pallas_call(block_kernel, out_shape=(jax.ShapeDtypeStruct((128, 1536),...  200 us
    unnamed x10, local copies, waits for them, and re-layouts  5.54 us

profile of v2, /device:TPU:0, one launch (start us, length us, event | category | flops | bytes accessed | tf_op | source)
XLA Modules:
  0.0 211.1 jit_solution(9270799576506073779)
XLA Ops:
  0.6 1.4 copy.20
  2.0 1.0 copy.15
  3.0 0.7 copy.18
  3.6 200.4 %block.1 = (bf16[128,1536]{1,0:T(8,128)(2,1)}, f32[128,1536]{1,0:T(8,128)}, f32[48,4608]{1,0:T(8,128)}) custom-call(bf16[128,1536]{1,0:T(8,128)(2,1)} %bitcast.31, f32[6,1536]{1,0:T(8,128)} %bitcast.33, bf16[128,1536]{1,0:T(8,128)(2,1)} %bitcast.32, bf16[48,1152]{1,0:T(8,128)(2,1)} %bitcast.29, bf16[48,384]{1,0:T(8,128)(2,1)} %bitcast.36, ...), custom_call_target="tpu_custom_call" | custom-call | tf_op jit(solution)/shard_map/block/pallas_call | solution.py:704
  204.1 1.5 slice_bitcast_fusion.2
  205.6 0.9 slice.12
  206.6 1.9 slice_bitcast_fusion
  208.5 0.0 copy-start.1
  208.5 0.0 copy-start
  208.5 0.1 reshape.15
  208.6 0.7 copy.16
  209.3 0.2 copy-done.1
  209.5 0.7 copy.23
  210.2 0.0 copy-done
  210.2 0.9 copy.24
Async XLA Ops:
  208.5 1.0 copy-start.1
  208.5 1.7 copy-start

commit v3 on v2

--- a/solution.py
+++ b/solution.py
@@ -21,12 +21,191 @@
 VMEM_LIMIT = 67_000_000
 
 CHUNKS = (
-    ((0, 640), (640, 512)),
+    ((0, 256), (256, 128)),
+    ((384, 384), (768, 384)),
     ((1152, 128), (1280, 256)),
-    ((1536, 768), (2304, 768)),
-    ((3072, 768), (3840, 768)),
+    ((1536, 384), (1920, 384)),
+    ((2304, 384), (2688, 384)),
+    ((3072, 384), (3456, 384)),
+    ((3840, 384), (4224, 384)),
 )
 WIDTH = 4608
+ORDER = (
+    "load_first",
+    "ag_s1_0",
+    "load_inputs",
+    "first_norm_0",
+    "load_rest",
+    "ag_s1_2",
+    "ag_s1_1",
+    "ag_s1_3",
+    "ag_s2_0",
+    "gate_grad",
+    "ag_s1_6",
+    "ag_s2_2",
+    "first_norm_1",
+    "ag_s2b_0",
+    "a1_start_1",
+    "ag_s2b_2",
+    "ag_s2_1",
+    "a1_start_0",
+    "ag_s3_0",
+    "ag_s3_2",
+    "ag_s1_4",
+    "dm_start_0",
+    "ag_s2b_1",
+    "ag_s2_3",
+    "ag_s3b_2",
+    "ag_s3_1",
+    "ag_s2b_3",
+    "a1_relay_0",
+    "dm_start_1",
+    "ag_s3b_0",
+    "ag_done_2",
+    "ag_s3b_1",
+    "a1_relay_1",
+    "ag_s2_6",
+    "ag_s2_4",
+    "a1_own_half",
+    "ag_s1_5",
+    "a1_done",
+    "ag_done_0",
+    "project_0",
+    "ag_s3_3",
+    "attend_0",
+    "ag_done_1",
+    "dm_relay_0",
+    "dm_relay_1",
+    "project_1",
+    "attend_other",
+    "dm_release",
+    "att_mm_other",
+    "ag_s2b_4",
+    "ag_s2_5",
+    "dm_own_half",
+    "ag_s2b_6",
+    "att_other",
+    "attend_own",
+    "att_mm_own",
+    "att_own",
+    "att_send",
+    "ag_s3_4",
+    "ag_s2b_5",
+    "att_wait_0",
+    "ag_s3b_3",
+    "second_norm_0",
+    "ag_s3b_4",
+    "a2_start_0",
+    "att_wait_1",
+    "ag_s3_5",
+    "second_norm_1",
+    "att_release",
+    "ag_s3_6",
+    "a2_relay_0",
+    "a2_start_1",
+    "a2_relay_1",
+    "ag_s3b_5",
+    "a2_done",
+    "a2_own_half",
+    "ag_done_4",
+    "ag_done_3",
+    "hidden_other_1",
+    "hidden_other_0",
+    "dm_done",
+    "hidden_own_0",
+    "hidden_own_1",
+    "ag_s3b_6",
+    "grad_back_1",
+    "rs_r1_6",
+    "grad_back_0",
+    "ag_done_5",
+    "rs_r1_5",
+    "hidden_grad_0",
+    "ag_done_6",
+    "hidden_grad_1",
+    "da2_mm_other",
+    "da2_other",
+    "rs_r1b_6",
+    "da2_mm_own",
+    "da2_send",
+    "grad_in_1",
+    "grad_in_0",
+    "da2_own",
+    "rs_r1b_5",
+    "da2_wait_0",
+    "rs_r1_4",
+    "mid_grad_0",
+    "ffn_mm_own",
+    "rs_r1_3",
+    "da_start_0",
+    "da2_wait_1",
+    "mid_grad_1",
+    "da_start_1",
+    "rs_r2_6",
+    "rs_r2_5",
+    "rs_r1b_4",
+    "da_own_half",
+    "da_relay_0",
+    "ffn_mm_other",
+    "ffn_other",
+    "da2_release",
+    "ffn_own",
+    "da_relay_1",
+    "ffn_send",
+    "heads_own",
+    "rs_r1b_3",
+    "da_done",
+    "heads_other",
+    "attend_back_0",
+    "attend_back_1",
+    "da1_mm_own",
+    "ffn_wait_0",
+    "grad_q_1",
+    "rs_r2_4",
+    "rs_r1_1",
+    "da1_own",
+    "da1_mm_other",
+    "da1_other",
+    "rs_r2b_5",
+    "grad_out",
+    "rs_r2_3",
+    "rs_r2b_6",
+    "rs_r1b_1",
+    "rs_r1_2",
+    "da1_send",
+    "ffn_wait_1",
+    "rs_r3_5",
+    "grad_q_0",
+    "rs_r2b_3",
+    "rs_r1_0",
+    "rs_r2b_4",
+    "rs_r2_1",
+    "last_out",
+    "rs_r1b_0",
+    "rs_r3_3",
+    "da1_wait_0",
+    "rs_r1b_2",
+    "rs_r2b_1",
+    "da1_wait_1",
+    "rs_r3_6",
+    "rs_r3_4",
+    "rs_r2_0",
+    "rs_r2_2",
+    "rs_done_6",
+    "rs_r3_1",
+    "rs_r2b_0",
+    "rs_done_3",
+    "rs_r2b_2",
+    "rs_r3_0",
+    "rs_r3_2",
+    "first_grad",
+    "rs_done_5",
+    "rs_done_4",
+    "rs_done_0",
+    "rs_done_1",
+    "rs_done_2",
+    "finish",
+)
 
 
 def turn(axis, step, size):
@@ -263,7 +442,13 @@
         self.copies[k, 5][0].wait_recv()
         cols = pl.ds(a0, an + bn)
         own = self.g[self.z, rows_of(96 * self.y + 48 * self.xh, 48), cols]
-        self.out[:, cols] = own.astype(F32) + self.last[:, cols].astype(F32)
+        total = own.astype(F32) + self.last[:, cols].astype(F32)
+        if a0 >= 1152:
+            self.out[:, cols] = total
+            return
+        for at in range(0, an + bn, 128):
+            head, which = (a0 + at) // 384, (a0 + at) % 384 // 128
+            self.out[:, pl.ds(384 * which + 128 * head, 128)] = total[:, at : at + 128]
 
 
 def scatter_buffers():
@@ -315,32 +500,33 @@
     def __init__(self, wires, buf):
         self.wires, self.buf = wires, buf
         self.xl, self.c = (lax.axis_index(a) for a in SP)
+        self.far, self.near, self.relays = {}, {}, {}
 
     def block(self, xl, c, start=0, count=128):
         return self.buf.at[rows_of(256 * xl + 128 * c + start, count), :]
 
-    def start(self):
-        own = self.block(self.xl, self.c)
-        go = self.wires.go
-        self.far = []
-        for i in range(2):
-            part = self.block(self.xl, self.c, 64 * i, 64)
-            self.far.append(go(part, part, turn("xl", 1, 2)))
-        self.near = go(own, own, turn("c", 1, 2))
-
-    def relay(self):
-        self.relays = []
-        for i in range(2):
-            self.far[i].wait_recv()
-            part = self.block(1 - self.xl, self.c, 64 * i, 64)
-            self.relays.append(self.wires.go(part, part, turn("c", 1, 2)))
+    def start(self, i):
+        part = self.block(self.xl, self.c, 64 * i, 64)
+        self.far[i] = self.wires.go(part, part, turn("xl", 1, 2))
+        self.near[i] = self.wires.go(part, part, turn("c", 1, 2))
+
+    def relay(self, i):
+        self.far[i].wait_recv()
+        part = self.block(1 - self.xl, self.c, 64 * i, 64)
+        self.relays[i] = self.wires.go(part, part, turn("c", 1, 2))
 
     def own_half(self):
-        self.near.wait_recv()
+        for copy in self.near.values():
+            copy.wait_recv()
 
     def done(self):
-        for copy in self.relays:
+        for copy in self.relays.values():
             copy.wait_recv()
+
+    def release(self):
+        for group in (self.far, self.near, self.relays):
+            for copy in group.values():
+                self.wires.sent(copy)
 
 
 class Collect:
@@ -356,21 +542,23 @@
 
     def send(self):
         self.first.wait_recv()
-        mine = self.block(1 - self.xl, self.c)
+        self.third = []
         for i in range(2):
             rows = pl.ds(64 * i, 64)
-            add2(mine.at[rows, :], self.pair.at[0, rows, :])
-        self.third = self.wires.go(mine, self.cross, turn("xl", 1, 2))
+            mine = self.block(1 - self.xl, self.c).at[rows, :]
+            add2(mine, self.pair.at[0, rows, :])
+            self.third.append(self.wires.go(mine, self.cross.at[rows, :], turn("xl", 1, 2)))
 
     def own(self):
         self.second = self.wires.go(self.block(self.xl, 1 - self.c), self.pair.at[1], turn("c", 1, 2))
 
-    def wait(self):
-        self.second.wait_recv()
-        self.third.wait_recv()
+    def wait(self, i):
+        if i == 0:
+            self.second.wait_recv()
+        self.third[i].wait_recv()
 
     def release(self):
-        for copy in (self.first, self.second, self.third):
+        for copy in (self.first, self.second, *self.third):
             self.wires.sent(copy)
 
     def rows(self, start, count):
@@ -405,28 +593,43 @@
 ROOT = math.sqrt(2.0 / math.pi)
 
 
-def by_rows(fn):
-    @pl.loop(0, 128 // BLOCK)
+def by_rows(fn, start=0, count=128):
+    @pl.loop(start // BLOCK, (start + count) // BLOCK)
     def _(i):
         fn(pl.multiple_of(i * BLOCK, BLOCK))
 
 
 def block_kernel(
-    x_ref, m_ref, og_ref, wq_ref, wo_ref, wi_ref, wb_ref,
-    final_ref, ig_ref, sums_ref,
-    w, g, last, a1, dm, a2, da, qkv, o, do, gp, act, part0, part1, pair0, cross0, pair1, cross1,
-    mid, dmid, acck, accv, send, recv, local_sem, *bufs,
+    x_in, m_in, og_in, wq_ref, wo_ref, wi_ref, wb_ref,
+    final_out, ig_out, sums_out,
+    x_ref, m_ref, og_ref, final_ref, ig_ref, sums_ref,
+    w, g, last, a1, dm, a2, da, qkv, o, do, gp, act, part, probs, dv, pair0, cross0, pair1, cross1,
+    mid, dmid, send, recv, local_sem, *bufs,
 ):
     z, y, xh, xl, c = (lax.axis_index(a) for a in FSDP + SP)
     shard_rows = rows_of(96 * y + 48 * xh, 48)
-    loads = []
-    for i, (ref, at, count) in enumerate(
-        ((wq_ref, 0, 1152), (wo_ref, 1152, 384), (wi_ref, 1536, 1536), (wb_ref, 3072, 1536))
-    ):
-        load = pltpu.make_async_copy(ref, w.at[z, shard_rows, pl.ds(at, count)], local_sem.at[i])
+    pieces = [(wq_ref, 384 * which + 128 * h, 384 * h + 128 * which, 128) for h in range(3) for which in range(3)]
+    pieces += [(wo_ref, 0, 1152, 384), (wi_ref, 0, 1536, 1536), (wb_ref, 0, 3072, 1536)]
+    loads = [
+        pltpu.make_async_copy(
+            ref.at[:, pl.ds(at, count)], w.at[z, shard_rows, pl.ds(to, count)], local_sem.at[i]
+        )
+        for i, (ref, at, to, count) in enumerate(pieces)
+    ]
+    inputs = [
+        pltpu.make_async_copy(a, b, local_sem.at[12 + i])
+        for i, (a, b) in enumerate(((x_in, x_ref), (m_in, m_ref), (og_in, og_ref)))
+    ]
+    outputs = {
+        name: pltpu.make_async_copy(a, b, local_sem.at[15 + i])
+        for i, (name, a, b) in enumerate(
+            (("final", final_ref, final_out), ("ig", ig_ref, ig_out), ("sums", sums_ref, sums_out))
+        )
+    }
+    for load in loads[:3] + inputs[:2] + loads[3:] + inputs[2:]:
         load.start()
-        loads.append(load)
-    greet(sp=True)
+    with jax.named_scope("greet"):
+        greet(sp=True)
     wires = Wires(send, recv)
     ag = Gather(wires, w)
     rs = make_scatter(wires, g, bufs, last, sums_ref)
@@ -434,6 +637,11 @@
     own_start, other_start = 256 * xl, 256 * (1 - xl)
     scale = 1.0 / math.sqrt(32 * 512)
     factor = temper / math.sqrt(HEAD_DIM)
+    steps = {}
+
+    def step(fn):
+        steps[fn.__name__] = fn
+        return fn
 
     def mod(i):
         return m_ref[pl.ds(i, 1), :]
@@ -444,74 +652,108 @@
     def weights(start, count):
         return w[:, :, pl.ds(start, count)].reshape(1536, count)
 
-    loads[0].wait()
-    ag.s1(0)
+    for k in range(len(CHUNKS)):
+        for name in ("s1", "s2", "s2b", "s3", "s3b", "done"):
+            steps[f"ag_{name}_{k}"] = functools.partial(getattr(ag, name), k)
+        for name in ("r1", "r1b", "r2", "r2b", "r3", "done"):
+            steps[f"rs_{name}_{k}"] = functools.partial(getattr(rs, name), k)
+    for key, buf in (("a1", a1), ("dm", dm), ("a2", a2), ("da", da)):
+        spread = Spread(wires, buf)
+        for i in range(2):
+            steps[f"{key}_start_{i}"] = functools.partial(spread.start, i)
+            steps[f"{key}_relay_{i}"] = functools.partial(spread.relay, i)
+        steps[f"{key}_own_half"] = spread.own_half
+        steps[f"{key}_done"] = spread.done
+        steps[f"{key}_release"] = spread.release
+    reds = {
+        "att": Collect(wires, part, pair0, cross0),
+        "da2": Collect(wires, part, pair0, cross0),
+        "da1": Collect(wires, part, pair0, cross0),
+        "ffn": Collect(wires, dm, pair1, cross1),
+    }
+    for key, red in reds.items():
+        for name in ("other", "own", "send", "release"):
+            steps[f"{key}_{name}"] = getattr(red, name)
+        for i in range(2):
+            steps[f"{key}_wait_{i}"] = functools.partial(red.wait, i)
+
+    @step
+    def load_first():
+        for load in loads[:3]:
+            load.wait()
+
+    @step
+    def load_inputs():
+        inputs[0].wait()
+        inputs[1].wait()
+
+    @step
+    def load_rest():
+        for load in loads[3:]:
+            load.wait()
+        inputs[2].wait()
 
     def first_norm(r):
         n1, _ = normalize(x_ref[pl.ds(r, BLOCK), :].astype(F32))
         a1[own(r)] = (n1 * (1.0 + mod(1)) + mod(0)).astype(BF)
 
-    by_rows(first_norm)
-    sp1 = Spread(wires, a1)
-    sp1.start()
-    for load in loads[1:]:
-        load.wait()
-    ag.s1(1)
-    ag.s1(2)
-    ag.s2(0)
-
-    def gate_grad(r):
-        dm[own(r)] = (mod(5) * og_ref[pl.ds(r, BLOCK), :].astype(F32)).astype(BF)
-
-    by_rows(gate_grad)
-    ag.s2b(0)
-    ag.s3(0)
-    ag.s2(1)
-    ag.s1(3)
-    sp1.relay()
-    spm = Spread(wires, dm)
-    spm.start()
-    ag.s2b(1)
-    ag.s2(2)
-    ag.s3b(0)
-    ag.s3(1)
-    ag.s2b(2)
-    ag.s2(3)
-    sp1.own_half()
-    sp1.done()
-    ag.done(0)
-
-    def project_qkv(start, count):
+    def second_norm(r):
+        rows = pl.ds(r, BLOCK)
+        value = x_ref[rows, :].astype(F32) + mod(2) * reds["att"].rows(r, BLOCK)
+        mid[rows, :] = value
+        n2, _ = normalize(value)
+        a2[own(r)] = (n2 * (1.0 + mod(4)) + mod(3)).astype(BF)
+
+    def mid_grad(r):
+        rows = pl.ds(r, BLOCK)
+        n2, r2 = normalize(mid[rows, :])
+        inner = norm_back(n2, r2, reds["da2"].rows(r, BLOCK) * (1.0 + mod(4)))
+        value = og_ref[rows, :].astype(F32) + inner
+        dmid[rows, :] = value
+        da[own(r)] = (mod(2) * value).astype(BF)
+
+    for i in range(2):
+        for fn in (first_norm, second_norm, mid_grad):
+            steps[f"{fn.__name__}_{i}"] = functools.partial(by_rows, fn, 64 * i, 64)
+
+    @step
+    def gate_grad():
+        def rows(r):
+            dm[own(r)] = (mod(5) * og_ref[pl.ds(r, BLOCK), :].astype(F32)).astype(BF)
+
+        by_rows(rows)
+
+    def lanes(h, which):
+        return pl.ds(384 * h + 128 * which, 128)
+
+    def project(start, count):
         qkv[:, pl.ds(start, count)] = nn(a1[...], weights(start, count)).astype(BF)
 
-    @pl.loop(0, 4)
-    def _(j):
-        project_qkv(pl.multiple_of(j * 256, 256), 256)
-
-    project_qkv(1024, 128)
-    ag.s3b(1)
-    ag.s3(2)
-    ag.s2b(3)
-
-    def probs(q, k):
-        s = nt(q, k) * factor
-        e = jnp.exp(s - jnp.max(s, axis=-1, keepdims=True))
-        return e, 1.0 / jnp.sum(e, axis=-1, keepdims=True)
-
-    def lanes(h, which):
-        return pl.ds(pl.multiple_of(384 * which + 128 * h, 128), 128)
-
-    @pl.loop(0, 3)
-    def _(h):
-        k, v = qkv[:, lanes(h, 1)], qkv[:, lanes(h, 2)]
-
-        @pl.loop(0, 4)
+    @step
+    def project_0():
+        project(0, 256)
+        project(256, 128)
+
+    @step
+    def project_1():
+        @pl.loop(0, 3)
+        def _(j):
+            project(pl.multiple_of(384 + j * 256, 128), 256)
+
+    def attend(heads, start, blocks):
+        @pl.loop(0, blocks)
         def _(i):
-            rows = pl.ds(pl.multiple_of(i * 128, 128), 128)
-            e, inv = probs(qkv[rows, lanes(h, 0)], k)
-            o[rows, lanes(h, 0)] = (nn(e.astype(BF), v) * inv).astype(BF)
-
-    ag.done(1)
+            rows = rows_of(start + i * 128, 128)
+            for h in heads:
+                s = nt(qkv[rows, lanes(h, 0)], qkv[:, lanes(h, 1)]) * factor
+                e = jnp.exp(s - jnp.max(s, axis=-1, keepdims=True))
+                p = (e * (1.0 / jnp.sum(e, axis=-1, keepdims=True))).astype(BF)
+                probs[h, rows, :] = p
+                o[rows, pl.ds(128 * h, 128)] = nn(p, qkv[:, lanes(h, 2)]).astype(BF)
+
+    steps["attend_0"] = functools.partial(attend, (0,), 0, 4)
+    steps["attend_other"] = functools.partial(attend, (1, 2), other_start, 2)
+    steps["attend_own"] = functools.partial(attend, (1, 2), own_start, 2)
 
     def back_half(dst, lhs, start, at, count):
         rows = rows_of(start, 256)
@@ -521,38 +763,19 @@
             rhs = w[pl.ds(2 * j, 2), :, pl.ds(at, count)].reshape(768, count)
             dst[rows, pl.ds(pl.multiple_of(768 * j, 128), 768)] = nt(lhs[rows, :], rhs).astype(BF)
 
-    def collect(red, dst, lhs, at, count):
-        back_half(dst, lhs, other_start, at, count)
-        red.other()
-        back_half(dst, lhs, own_start, at, count)
-        red.own()
-        red.send()
-
-    red1 = Collect(wires, part0, pair0, cross0)
-    collect(red1, part0, o, 1152, 384)
-    spm.relay()
-    red1.wait()
-
-    def second_norm(r):
-        rows = pl.ds(r, BLOCK)
-        value = x_ref[rows, :].astype(F32) + mod(2) * red1.rows(r, BLOCK)
-        mid[rows, :] = value
-        n2, _ = normalize(value)
-        a2[own(r)] = (n2 * (1.0 + mod(4)) + mod(3)).astype(BF)
-
-    by_rows(second_norm)
-    sp2 = Spread(wires, a2)
-    sp2.start()
-    ag.s3b(2)
-    ag.s3(3)
-    sp2.relay()
-    sp2.own_half()
-    ag.done(2)
-
-    def hidden(start):
+    for key, dst, lhs, at, count in (
+        ("att", part, o, 1152, 384),
+        ("da2", part, gp, 1536, 1536),
+        ("da1", part, qkv, 0, 1152),
+        ("ffn", dm, act, 3072, 1536),
+    ):
+        steps[f"{key}_mm_other"] = functools.partial(back_half, dst, lhs, other_start, at, count)
+        steps[f"{key}_mm_own"] = functools.partial(back_half, dst, lhs, own_start, at, count)
+
+    def hidden(start, half):
         rows = rows_of(start, 256)
 
-        @pl.loop(0, 6)
+        @pl.loop(3 * half, 3 * half + 3)
         def _(j):
             at = pl.multiple_of(j * 256, 256)
             u = nn(a2[rows, :], weights(pl.multiple_of(1536 + at, 256), 256))
@@ -563,11 +786,13 @@
             slope = half + (0.5 * ROOT) * u * (1.0 - t * t) * (1.0 + (3 * 0.044715) * sq)
             gp[rows, pl.ds(at, 256)] = slope.astype(BF)
 
-    hidden(own_start)
-    sp2.done()
-    hidden(other_start)
-    spm.own_half()
-    spm.done()
+    def hidden_grad(half):
+        @pl.loop(3 * half, 3 * half + 3)
+        def _(j):
+            at = pl.multiple_of(j * 256, 256)
+            cols = pl.ds(at, 256)
+            dg = nn(dm[...], weights(pl.multiple_of(3072 + at, 256), 256))
+            gp[:, cols] = (gp[:, cols].astype(F32) * dg).astype(BF)
 
     def grad(left, right, right_at, at, count):
         @pl.loop(0, 4)
@@ -576,130 +801,81 @@
             value = tn(lhs, right[:, pl.ds(right_at, count)]) * scale
             g[j, :, pl.ds(at, count)] = value.astype(BF)
 
-    grad(dm, act, 0, 3072, 768)
-    grad(dm, act, 768, 3840, 768)
-    rs.r1(3)
-    ag.s3b(3)
-    ag.done(3)
-
-    @pl.loop(0, 6)
-    def _(j):
-        at = pl.multiple_of(j * 256, 256)
-        cols = pl.ds(at, 256)
-        dg = nn(dm[...], weights(pl.multiple_of(3072 + at, 256), 256))
-        gp[:, cols] = (gp[:, cols].astype(F32) * dg).astype(BF)
-
-    du = gp
-    red1.release()
-    red2 = Collect(wires, part0, pair0, cross0)
-    collect(red2, part0, du, 1536, 1536)
-    rs.r1b(3)
-    grad(a2, du, 0, 1536, 768)
-    grad(a2, du, 768, 2304, 768)
-    rs.r1(2)
-    red2.wait()
-
-    def mid_grad(r):
-        rows = pl.ds(r, BLOCK)
-        n2, r2 = normalize(mid[rows, :])
-        value = og_ref[rows, :].astype(F32) + norm_back(n2, r2, red2.rows(r, BLOCK) * (1.0 + mod(4)))
-        dmid[rows, :] = value
-        da[own(r)] = (mod(2) * value).astype(BF)
-
-    by_rows(mid_grad)
-    spa = Spread(wires, da)
-    spa.start()
-    rs.r2(3)
-    back_half(part1, act, other_start, 3072, 1536)
-    back_half(part1, act, own_start, 3072, 1536)
-    spa.relay()
-    rs.r1b(2)
-    redf = Collect(wires, part1, pair1, cross1)
-    redf.other()
-    redf.own()
-    redf.send()
-    spa.own_half()
+    for i in range(2):
+        steps[f"hidden_own_{i}"] = functools.partial(hidden, own_start, i)
+        steps[f"hidden_other_{i}"] = functools.partial(hidden, other_start, i)
+        steps[f"hidden_grad_{i}"] = functools.partial(hidden_grad, i)
+        steps[f"grad_in_{i}"] = functools.partial(grad, a2, gp, 768 * i, 1536 + 768 * i, 768)
+        steps[f"grad_back_{i}"] = functools.partial(grad, dm, act, 768 * i, 3072 + 768 * i, 768)
+    steps["grad_out"] = functools.partial(grad, da, o, 0, 1152, 384)
+    steps["grad_q_0"] = functools.partial(grad, a1, qkv, 0, 0, 384)
+    steps["grad_q_1"] = functools.partial(grad, a1, qkv, 384, 384, 768)
 
     def head_grads(start):
         rows = rows_of(start, 256)
         do[rows, :] = nn(da[rows, :], weights(1152, 384)).astype(BF)
 
-    head_grads(own_start)
-    spa.done()
-    head_grads(other_start)
-    grad(da, o, 0, 1152, 128)
-    grad(da, o, 128, 1280, 256)
-    rs.r1(1)
-    rs.r2b(3)
-
-    @pl.loop(0, 3)
-    def _(h):
-        k, v = qkv[:, lanes(h, 1)], qkv[:, lanes(h, 2)]
-        acck[...] = jnp.zeros_like(acck)
-        accv[...] = jnp.zeros_like(accv)
+    steps["heads_own"] = functools.partial(head_grads, own_start)
+    steps["heads_other"] = functools.partial(head_grads, other_start)
+
+    def attend_back(heads):
+        for n, h in enumerate(heads):
+            dv[n] = tn(probs[h], do[:, pl.ds(128 * h, 128)]).astype(BF)
 
         @pl.loop(0, 4)
         def _(i):
             rows = pl.ds(pl.multiple_of(i * 128, 128), 128)
-            q = qkv[rows, lanes(h, 0)]
-            up = do[rows, lanes(h, 0)]
-            e, inv = probs(q, k)
-            p = e * inv
-            dp = nt(up, v)
-            ds = factor * p * (dp - jnp.sum(p * dp, axis=-1, keepdims=True))
-            ds = ds.astype(BF)
-            qkv[rows, lanes(h, 0)] = nn(ds, k).astype(BF)
-            acck[...] += tn(ds, q)
-            accv[...] += tn(p.astype(BF), up)
-
-        qkv[:, lanes(h, 1)] = acck[...].astype(BF)
-        qkv[:, lanes(h, 2)] = accv[...].astype(BF)
-
-    grad(a1, qkv, 0, 0, 640)
-    grad(a1, qkv, 640, 640, 512)
-    rs.r1(0)
-    red2.release()
-    red3 = Collect(wires, part0, pair0, cross0)
-    collect(red3, part0, qkv, 0, 1152)
-    rs.r2(2)
-    rs.r1b(1)
-    rs.r3(3)
-    rs.r1b(0)
-    rs.r2b(2)
-    rs.r2(1)
-    redf.wait()
-
-    def last_out(r):
-        rows = pl.ds(r, BLOCK)
-        final_ref[rows, :] = (mid[rows, :] + mod(5) * redf.rows(r, BLOCK)).astype(BF)
-
-    by_rows(last_out)
-    rs.done(3)
-    red3.wait()
-
-    def first_grad(r):
-        rows = pl.ds(r, BLOCK)
-        n1, r1 = normalize(x_ref[rows, :].astype(F32))
-        ig_ref[rows, :] = dmid[rows, :] + norm_back(n1, r1, red3.rows(r, BLOCK) * (1.0 + mod(1)))
-
-    by_rows(first_grad)
-    rs.r3(2)
-    rs.r2b(1)
-    rs.r2(0)
-    rs.done(2)
-    rs.r3(1)
-    rs.r2b(0)
-    rs.done(1)
-    rs.r3(0)
-    rs.done(0)
-    wires.drain()
+            for h in heads:
+                dp = nt(do[rows, pl.ds(128 * h, 128)], qkv[:, lanes(h, 2)])
+                p = probs[h, rows, :].astype(F32)
+                ds = factor * p * (dp - jnp.sum(p * dp, axis=-1, keepdims=True))
+                probs[h, rows, :] = ds.astype(BF)
+
+        for n, h in enumerate(heads):
+            dk = tn(probs[h], qkv[:, lanes(h, 0)]).astype(BF)
+            qkv[:, lanes(h, 0)] = nn(probs[h], qkv[:, lanes(h, 1)]).astype(BF)
+            qkv[:, lanes(h, 1)] = dk
+            qkv[:, lanes(h, 2)] = dv[n]
+
+    steps["attend_back_0"] = functools.partial(attend_back, (0,))
+    steps["attend_back_1"] = functools.partial(attend_back, (1, 2))
+
+    @step
+    def last_out():
+        def each(r):
+            rows = pl.ds(r, BLOCK)
+            final_ref[rows, :] = (mid[rows, :] + mod(5) * reds["ffn"].rows(r, BLOCK)).astype(BF)
+
+        by_rows(each)
+        outputs["final"].start()
+
+    @step
+    def first_grad():
+        def each(r):
+            rows = pl.ds(r, BLOCK)
+            n1, r1 = normalize(x_ref[rows, :].astype(F32))
+            inner = norm_back(n1, r1, reds["da1"].rows(r, BLOCK) * (1.0 + mod(1)))
+            ig_ref[rows, :] = dmid[rows, :] + inner
+
+        by_rows(each)
+        outputs["ig"].start()
+
+    @step
+    def finish():
+        outputs["sums"].start()
+        wires.drain()
+        for copy in outputs.values():
+            copy.wait()
+
+    for name in ORDER:
+        with jax.named_scope(name):
+            steps[name]()
 
 
 def body(tokens, modulation, w_qkv, w_out, w_in, w_back, out_grad):
     own = w_qkv.shape[3]
-    vmem = pl.BlockSpec(memory_space=pltpu.VMEM)
     far = pl.BlockSpec(memory_space=pl.ANY)
-    copies = 34 * len(CHUNKS) + 32
+    copies = 34 * len(CHUNKS) + 40
     rows = lambda n, dtype=BF: pltpu.VMEM((512, n), dtype)
     final, grad_in_rows, sums = pl.pallas_call(
         block_kernel,
@@ -708,25 +884,32 @@
             jax.ShapeDtypeStruct((128, 1536), F32),
             jax.ShapeDtypeStruct((48, WIDTH), F32),
         ),
-        in_specs=[vmem, vmem, vmem, far, far, far, far],
-        out_specs=(vmem, vmem, vmem),
+        in_specs=[far] * 7,
+        out_specs=(far, far, far),
         scratch_shapes=[
+            pltpu.VMEM((128, 1536), BF),
+            pltpu.VMEM((6, 1536), F32),
+            pltpu.VMEM((128, 1536), BF),
+            pltpu.VMEM((128, 1536), BF),
+            pltpu.VMEM((128, 1536), F32),
+            pltpu.VMEM((48, WIDTH), F32),
             pltpu.VMEM((4, 384, WIDTH), BF),
             pltpu.VMEM((4, 384, WIDTH), BF),
             pltpu.VMEM((48, WIDTH), BF),
             rows(1536), rows(1536), rows(1536), rows(1536),
             rows(1152), rows(384), rows(384),
-            rows(1536), rows(1536), rows(1536), rows(1536),
+            rows(1536), rows(1536), rows(1536),
+            pltpu.VMEM((3, 512, 512), BF),
+            pltpu.VMEM((2, 512, 128), BF),
             pltpu.VMEM((2, 128, 1536), BF),
             pltpu.VMEM((128, 1536), BF),
             pltpu.VMEM((2, 128, 1536), BF),
             pltpu.VMEM((128, 1536), BF),
             pltpu.VMEM((128, 1536), F32),
             pltpu.VMEM((128, 1536), F32),
-            rows(128, F32), rows(128, F32),
             pltpu.SemaphoreType.DMA((copies,)),
             pltpu.SemaphoreType.DMA((copies,)),
-            pltpu.SemaphoreType.DMA((4,)),
+            pltpu.SemaphoreType.DMA((18,)),
             *scatter_buffers(),
         ],
         compiler_params=pltpu.CompilerParams(

time: 211 us -> 184 us (0.87)
  Pallas kernels: 200 us -> 173 us
    pallas_call x1, Pallas kernels: 200 us -> 173 us  [body(): pl.pallas_call(block_kernel, out_shape=(jax.ShapeDtypeStruct((128, 1536),...]
where the time goes in v3:
time: 184 us; the launch traced here: 183 us
  Pallas kernels  173 us (94%)
  local copies, waits for them, and re-layouts  10 us (5%)
    pallas_call x1, Pallas kernels, body(): pl.pallas_call(block_kernel, out_shape=(jax.ShapeDtypeStruct((128, 1536),...  173 us
    unnamed x10, local copies, waits for them, and re-layouts  5.54 us

profile of v3, /device:TPU:0, one launch (start us, length us, event | category | flops | bytes accessed | tf_op | source)
XLA Modules:
  0.0 183.4 jit_solution(3949451187072030525)
XLA Ops:
  0.6 1.4 copy.20
  2.0 1.0 copy.15
  3.0 0.7 copy.18
  3.6 172.7 %block.1 = (bf16[128,1536]{1,0:T(8,128)(2,1)}, f32[128,1536]{1,0:T(8,128)}, f32[48,4608]{1,0:T(8,128)}) custom-call(bf16[128,1536]{1,0:T(8,128)(2,1)} %bitcast.31, f32[6,1536]{1,0:T(8,128)} %bitcast.33, bf16[128,1536]{1,0:T(8,128)(2,1)} %bitcast.32, bf16[48,1152]{1,0:T(8,128)(2,1)} %bitcast.29, bf16[48,384]{1,0:T(8,128)(2,1)} %bitcast.36, ...), custom_call_target="tpu_custom_call" | custom-call | tf_op jit(solution)/shard_map/block/pallas_call | solution.py:880
  176.4 1.5 slice_bitcast_fusion.2
  177.9 0.9 slice.12
  178.9 1.9 %slice_bitcast_fusion = (f32[1,1536,48]{1,2,0:T(8,128)}, f32[1,48,1536]{2,1,0:T(8,128)}) fusion(f32[48,4608]{1,0:T(8,128)} %get-tuple-element.11), kind=kLoop, calls=%fused_computation | loop fusion | bytes 1179648 | tf_op jit(solution)/shard_map/broadcast_in_dim | solution.py:934
  180.8 0.0 copy-start.1
  180.8 0.0 copy-start
  180.8 0.1 reshape.15
  180.9 0.7 copy.16
  181.6 0.2 copy-done.1
  181.8 0.7 copy.23
  182.5 0.0 copy-done
  182.5 0.9 copy.24
Async XLA Ops:
  180.8 1.0 copy-start.1
  180.8 1.7 copy-start

commit v4 on v3

--- a/solution.py
+++ b/solution.py
@@ -20,190 +20,242 @@
 temper = 2.5
 VMEM_LIMIT = 67_000_000
 
-CHUNKS = (
-    ((0, 256), (256, 128)),
-    ((384, 384), (768, 384)),
-    ((1152, 128), (1280, 256)),
-    ((1536, 384), (1920, 384)),
-    ((2304, 384), (2688, 384)),
-    ((3072, 384), (3456, 384)),
-    ((3840, 384), (4224, 384)),
-)
+TILES = ((2, 1, 0), (3, 2, 1), (1, 2, 0), (2, 3, 1), (3, 2, 1), (2, 3, 1), (3, 2, 1))
+
+
+def split_chunks():
+    chunks, at = [], 0
+    for tiles in TILES:
+        parts = []
+        for count in tiles:
+            parts.append((at, 128 * count))
+            at += 128 * count
+        chunks.append(tuple(parts))
+    return tuple(chunks)
+
+
+CHUNKS = split_chunks()
 WIDTH = 4608
 ORDER = (
     "load_first",
+    "met",
+    "load_rest",
+    "ag_c1_1",
+    "ag_c1_4",
     "ag_s1_0",
+    "ag_s1_4",
+    "ag_s1_1",
     "load_inputs",
+    "ag_s1_2",
+    "ag_c2_1",
+    "ag_s1_3",
+    "ag_c1_5",
+    "ag_c2_4",
     "first_norm_0",
-    "load_rest",
-    "ag_s1_2",
-    "ag_s1_1",
-    "ag_s1_3",
+    "a1_start_0",
     "ag_s2_0",
     "gate_grad",
-    "ag_s1_6",
+    "ag_s2_4",
+    "ag_s2_1",
+    "ag_c1_3",
+    "first_norm_1",
     "ag_s2_2",
-    "first_norm_1",
+    "dm_start_1",
     "ag_s2b_0",
-    "a1_start_1",
-    "ag_s2b_2",
-    "ag_s2_1",
-    "a1_start_0",
-    "ag_s3_0",
-    "ag_s3_2",
-    "ag_s1_4",
+    "ag_s2b_4",
     "dm_start_0",
     "ag_s2b_1",
+    "ag_s2b_2",
+    "ag_c2b_1",
+    "ag_c1_6",
+    "ag_s1_5",
+    "ag_c2_5",
+    "ag_s3_0",
+    "ag_c2_6",
+    "a1_relay_0",
+    "ag_s1_6",
+    "ag_s3_1",
+    "a1_start_1",
+    "ag_c2_3",
+    "ag_c3_1",
     "ag_s2_3",
-    "ag_s3b_2",
-    "ag_s3_1",
-    "ag_s2b_3",
-    "a1_relay_0",
-    "dm_start_1",
     "ag_s3b_0",
-    "ag_done_2",
+    "dm_own_half",
+    "ag_c2b_4",
+    "ag_s3_2",
+    "ag_c2b_3",
     "ag_s3b_1",
+    "dm_relay_0",
+    "ag_c3_4",
     "a1_relay_1",
-    "ag_s2_6",
-    "ag_s2_4",
-    "a1_own_half",
-    "ag_s1_5",
     "a1_done",
     "ag_done_0",
+    "ag_s2b_3",
+    "ag_s3b_2",
+    "a1_own_half",
     "project_0",
+    "ag_s2_5",
+    "ag_s3_4",
+    "dm_relay_1",
+    "attend_0",
+    "ag_c2b_6",
+    "ag_done_1",
+    "ag_s2_6",
+    "project_1",
+    "ag_c3_3",
+    "ag_done_2",
+    "attend_other",
+    "att_mm_other",
+    "att_other",
     "ag_s3_3",
-    "attend_0",
-    "ag_done_1",
-    "dm_relay_0",
-    "dm_relay_1",
-    "project_1",
-    "attend_other",
-    "dm_release",
-    "att_mm_other",
-    "ag_s2b_4",
-    "ag_s2_5",
-    "dm_own_half",
-    "ag_s2b_6",
-    "att_other",
     "attend_own",
+    "att_send",
+    "dm_done",
+    "ag_c2b_5",
+    "ag_s3b_4",
+    "ag_s2b_5",
     "att_mm_own",
     "att_own",
-    "att_send",
-    "ag_s3_4",
-    "ag_s2b_5",
     "att_wait_0",
+    "second_norm_0",
+    "a2_start_0",
+    "ag_s2b_6",
     "ag_s3b_3",
-    "second_norm_0",
-    "ag_s3b_4",
-    "a2_start_0",
     "att_wait_1",
+    "second_norm_1",
+    "a2_start_1",
+    "ag_s3_6",
+    "ag_c3_6",
+    "a2_own_half",
     "ag_s3_5",
-    "second_norm_1",
+    "a2_relay_0",
+    "a2_relay_1",
+    "ag_done_3",
+    "ag_done_4",
+    "hidden_own_1",
+    "hidden_own_0",
+    "ag_c3_5",
     "att_release",
-    "ag_s3_6",
-    "a2_relay_0",
-    "a2_start_1",
-    "a2_relay_1",
-    "ag_s3b_5",
     "a2_done",
-    "a2_own_half",
-    "ag_done_4",
-    "ag_done_3",
+    "dm_release",
+    "ag_s3b_6",
     "hidden_other_1",
     "hidden_other_0",
-    "dm_done",
-    "hidden_own_0",
-    "hidden_own_1",
-    "ag_s3b_6",
     "grad_back_1",
+    "rs_c1_6",
+    "ag_s3b_5",
+    "grad_back_0",
+    "ag_done_6",
+    "rs_c1_5",
     "rs_r1_6",
-    "grad_back_0",
+    "rs_r1_5",
+    "hidden_grad_1",
+    "grad_in_1",
+    "rs_r1_4",
     "ag_done_5",
-    "rs_r1_5",
     "hidden_grad_0",
-    "ag_done_6",
-    "hidden_grad_1",
+    "rs_c1_4",
+    "rs_r1b_6",
     "da2_mm_other",
     "da2_other",
-    "rs_r1b_6",
+    "da2_send",
     "da2_mm_own",
-    "da2_send",
-    "grad_in_1",
+    "rs_r1b_5",
+    "da2_own",
+    "ffn_mm_other",
+    "rs_c2_5",
     "grad_in_0",
-    "da2_own",
-    "rs_r1b_5",
     "da2_wait_0",
-    "rs_r1_4",
     "mid_grad_0",
-    "ffn_mm_own",
-    "rs_r1_3",
+    "rs_c2_6",
+    "rs_c2_4",
     "da_start_0",
+    "rs_r1b_4",
+    "rs_c2b_6",
+    "rs_c2b_5",
+    "rs_r2_5",
+    "rs_c2b_4",
     "da2_wait_1",
     "mid_grad_1",
     "da_start_1",
+    "da_own_half",
     "rs_r2_6",
-    "rs_r2_5",
-    "rs_r1b_4",
-    "da_own_half",
+    "da2_release",
     "da_relay_0",
-    "ffn_mm_other",
+    "heads_own",
+    "rs_r1_3",
     "ffn_other",
-    "da2_release",
+    "rs_c1_3",
+    "rs_r2b_5",
+    "da_relay_1",
+    "ffn_mm_own",
+    "rs_r2b_6",
+    "da_done",
+    "rs_c3_5",
+    "grad_out",
+    "heads_other",
+    "rs_r1_2",
+    "ffn_send",
+    "rs_r1b_3",
+    "rs_c3_6",
+    "attend_back_1",
+    "grad_q_1",
+    "rs_r3_6",
+    "rs_c4_5",
+    "rs_r1b_2",
+    "rs_r1_1",
+    "attend_back_0",
     "ffn_own",
-    "da_relay_1",
-    "ffn_send",
-    "heads_own",
-    "rs_r1b_3",
-    "da_done",
-    "heads_other",
-    "attend_back_0",
-    "attend_back_1",
+    "da1_mm_other",
+    "rs_c1_1",
+    "rs_r3_5",
+    "ffn_wait_0",
+    "rs_r2_4",
+    "grad_q_0",
+    "rs_r1_0",
+    "da1_other",
+    "da1_send",
+    "rs_r2_3",
+    "rs_c3_4",
+    "rs_done_6",
+    "rs_r1b_1",
     "da1_mm_own",
-    "ffn_wait_0",
-    "grad_q_1",
-    "rs_r2_4",
-    "rs_r1_1",
     "da1_own",
-    "da1_mm_other",
-    "da1_other",
-    "rs_r2b_5",
-    "grad_out",
-    "rs_r2_3",
-    "rs_r2b_6",
-    "rs_r1b_1",
-    "rs_r1_2",
-    "da1_send",
+    "rs_c2_3",
+    "rs_r1b_0",
+    "rs_r2b_3",
+    "da1_wait_0",
+    "rs_r2_1",
+    "rs_c4_6",
+    "rs_r2_2",
+    "rs_r2b_4",
+    "da1_wait_1",
+    "first_grad",
+    "rs_r2_0",
+    "rs_r2b_1",
+    "rs_r2b_2",
     "ffn_wait_1",
-    "rs_r3_5",
-    "grad_q_0",
-    "rs_r2b_3",
-    "rs_r1_0",
-    "rs_r2b_4",
-    "rs_r2_1",
+    "rs_r3_3",
+    "rs_c2_1",
+    "rs_r3_4",
+    "rs_r2b_0",
+    "rs_c2b_3",
+    "rs_r3_1",
+    "rs_c2b_1",
+    "rs_done_3",
+    "rs_c4_4",
+    "rs_r3_2",
+    "rs_done_5",
+    "rs_r3_0",
+    "rs_c3_3",
+    "rs_done_4",
+    "rs_c3_1",
+    "rs_done_1",
     "last_out",
-    "rs_r1b_0",
-    "rs_r3_3",
-    "da1_wait_0",
-    "rs_r1b_2",
-    "rs_r2b_1",
-    "da1_wait_1",
-    "rs_r3_6",
-    "rs_r3_4",
-    "rs_r2_0",
-    "rs_r2_2",
-    "rs_done_6",
-    "rs_r3_1",
-    "rs_r2b_0",
-    "rs_done_3",
-    "rs_r2b_2",
-    "rs_r3_0",
-    "rs_r3_2",
-    "first_grad",
-    "rs_done_5",
-    "rs_done_4",
+    "rs_c4_3",
+    "rs_done_2",
     "rs_done_0",
-    "rs_done_1",
-    "rs_done_2",
+    "rs_c4_1",
     "finish",
 )
 
@@ -245,14 +297,21 @@
         self.open = []
 
 
-def greet(sp=False):
-    barrier = pltpu.get_barrier_semaphore()
-    targets = [turn("z", 1, 4), turn("z", -1, 4), turn("y", 1, 4), turn("y", -1, 4), turn("xh", 1, 2)]
-    if sp:
-        targets += [turn("xl", 1, 2), turn("c", 1, 2)]
-    for device in targets:
-        pl.semaphore_signal(barrier, inc=1, device_id=device, device_id_type=MESH)
-    pl.semaphore_wait(barrier, len(targets))
+def partners():
+    return [turn("z", 1, 4), turn("z", -1, 4), turn("z", 2, 4), turn("y", 1, 4), turn("y", -1, 4)] + [
+        turn(axis, 1, 2) for axis in ("xh", "xl", "c")
+    ]
+
+
+def greet():
+    for device in partners():
+        pl.semaphore_signal(
+            pltpu.get_barrier_semaphore(), inc=1, device_id=device, device_id_type=MESH
+        )
+
+
+def met():
+    pl.semaphore_wait(pltpu.get_barrier_semaphore(), len(partners()))
 
 
 def rows_of(start, count):
@@ -267,19 +326,19 @@
     def __init__(self, wires, w):
         self.wires, self.w = wires, w
         self.z, self.y, self.xh = (lax.axis_index(a) for a in FSDP)
-        self.one, self.two, self.relay2, self.three, self.relay3 = {}, {}, {}, {}, {}
+        self.one, self.two, self.relay2, self.three, self.relay3, self.third = {}, {}, {}, {}, {}, {}
 
     def same(self, part, device):
         return self.wires.go(part, part, device)
 
     def s1(self, k):
-        (a0, an), (b0, bn) = CHUNKS[k]
+        (a0, an), (b0, bn), _ = CHUNKS[k]
         part = self.w.at[self.z, rows_of(96 * self.y + 48 * self.xh, 48), pl.ds(a0, an + bn)]
         self.one[k] = self.same(part, turn("xh", 1, 2))
 
     def s2(self, k):
         self.one[k].wait_recv()
-        ca, cb = map(cols_of, CHUNKS[k])
+        ca, cb, _ = map(cols_of, CHUNKS[k])
         pa = self.w.at[self.z, rows_of(96 * self.y, 96), ca]
         pb = self.w.at[self.z, rows_of(96 * self.y, 96), cb]
         self.two[k] = [
@@ -290,7 +349,7 @@
         ]
 
     def s2b(self, k):
-        ca, cb = map(cols_of, CHUNKS[k])
+        ca, cb, _ = map(cols_of, CHUNKS[k])
         for copy in self.two[k]:
             copy.wait_recv()
         w, z, y = self.w, self.z, self.y
@@ -302,7 +361,7 @@
         ]
 
     def s3(self, k):
-        ca, cb = map(cols_of, CHUNKS[k])
+        ca, cb, _ = map(cols_of, CHUNKS[k])
         for copy in self.relay2[k]:
             copy.wait_recv()
         pa = self.w.at[self.z, :, ca]
@@ -315,7 +374,7 @@
         ]
 
     def s3b(self, k):
-        ca, cb = map(cols_of, CHUNKS[k])
+        ca, cb, _ = map(cols_of, CHUNKS[k])
         for copy in self.three[k]:
             copy.wait_recv()
         w = self.w
@@ -326,8 +385,36 @@
             self.same(w.at[:, rows_of(96 * near("y", 1) + 48, 48), cb], turn("y", -1, 4)),
         ]
 
+    def c1(self, k):
+        part = self.w.at[self.z, rows_of(96 * self.y + 48 * self.xh, 48), cols_of(CHUNKS[k][2])]
+        self.third[k, 1] = [self.same(part, turn("z", step, 4)) for step in (1, -1, 2)]
+
+    def column(self, y, planes, k):
+        return self.w.at[planes, rows_of(96 * y + 48 * self.xh, 48), cols_of(CHUNKS[k][2])]
+
+    def c2(self, k):
+        for copy in self.third[k, 1]:
+            copy.wait_recv()
+        part = self.column(self.y, pl.ds(0, 4), k)
+        self.third[k, 2] = [self.same(part, turn("y", step, 4)) for step in (1, -1)]
+
+    def c2b(self, k):
+        for copy in self.third[k, 2]:
+            copy.wait_recv()
+        self.third[k, 3] = [
+            self.same(self.column(near("y", -1), pl.ds(0, 2), k), turn("y", 1, 4)),
+            self.same(self.column(near("y", 1), pl.ds(2, 2), k), turn("y", -1, 4)),
+        ]
+
+    def c3(self, k):
+        for copy in self.third[k, 3]:
+            copy.wait_recv()
+        self.third[k, 4] = [
+            self.same(self.column(y, pl.ds(0, 4), k), turn("xh", 1, 2)) for y in range(4)
+        ]
+
     def done(self, k):
-        for copy in self.relay3[k]:
+        for copy in self.relay3[k] + self.third.get((k, 4), []):
             copy.wait_recv()
 
 
@@ -344,8 +431,8 @@
 
 
 class Scatter:
-    def __init__(self, wires, g, half_a, full_a, half_b, full_b, half2, full2, last, out):
-        self.wires, self.g, self.out = wires, g, out
+    def __init__(self, wires, g, half_a, full_a, half_b, full_b, half2, full2, third, last, out):
+        self.wires, self.g, self.out, self.third = wires, g, out, third
         self.half_a, self.full_a, self.half_b, self.full_b = half_a, full_a, half_b, full_b
         self.half2, self.full2, self.last = half2, full2, last
         self.z, self.y, self.xh = (lax.axis_index(a) for a in FSDP)
@@ -364,7 +451,7 @@
         return self.g.at[pl.ds(near("z", step), 1), rows_of(96 * self.y + start, count), cols]
 
     def r1(self, k):
-        ca, cb = map(cols_of, CHUNKS[k])
+        ca, cb, _ = map(cols_of, CHUNKS[k])
         go = self.wires.go
         self.copies[k, 1] = [
             go(self.block_a(2, 0, 192, ca), self.half_a[k].at[pl.ds(0, 1)], turn("z", 1, 4)),
@@ -374,7 +461,7 @@
         ]
 
     def r1b(self, k):
-        ca, cb = map(cols_of, CHUNKS[k])
+        ca, cb, _ = map(cols_of, CHUNKS[k])
         go, copies = self.wires.go, self.copies[k, 1]
         sent = []
         copies[0].wait_recv()
@@ -392,7 +479,7 @@
         self.copies[k, 2] = sent
 
     def r2(self, k):
-        ca, cb = map(cols_of, CHUNKS[k])
+        ca, cb, _ = map(cols_of, CHUNKS[k])
         go, copies = self.wires.go, self.copies[k, 2]
         copies[0].wait_recv()
         copies[1].wait_recv()
@@ -428,7 +515,7 @@
 
     def r3(self, k):
         go, copies = self.wires.go, self.copies[k, 4]
-        (a0, an), (b0, bn) = CHUNKS[k]
+        (a0, an), (b0, bn), _ = CHUNKS[k]
         for colour, sub in enumerate((self.sub_a, self.sub_b)):
             cols, full = cols_of(CHUNKS[k][colour]), self.full2[k][colour]
             copies[2 * colour].wait_recv()
@@ -438,22 +525,75 @@
         self.copies[k, 5] = [go(part, self.last.at[:, pl.ds(a0, an + bn)], turn("xh", 1, 2))]
 
     def done(self, k):
-        (a0, an), (b0, bn) = CHUNKS[k]
+        (a0, an), (b0, bn), _ = CHUNKS[k]
         self.copies[k, 5][0].wait_recv()
         cols = pl.ds(a0, an + bn)
         own = self.g[self.z, rows_of(96 * self.y + 48 * self.xh, 48), cols]
-        total = own.astype(F32) + self.last[:, cols].astype(F32)
-        if a0 >= 1152:
-            self.out[:, cols] = total
+        self.store(a0, own.astype(F32) + self.last[:, cols].astype(F32))
+
+    def store(self, start, total):
+        if start >= 1152:
+            self.out[:, pl.ds(start, total.shape[1])] = total
             return
-        for at in range(0, an + bn, 128):
-            head, which = (a0 + at) // 384, (a0 + at) % 384 // 128
+        for at in range(0, total.shape[1], 128):
+            head, which = (start + at) // 384, (start + at) % 384 // 128
             self.out[:, pl.ds(384 * which + 128 * head, 128)] = total[:, at : at + 128]
+
+    def column(self, y, xh, planes, k):
+        return self.g.at[planes, rows_of(96 * y + 48 * xh, 48), cols_of(CHUNKS[k][2])]
+
+    def c1(self, k):
+        self.copies[k, 6] = [
+            self.wires.go(
+                self.column(y, 1 - self.xh, pl.ds(0, 4), k), self.third[k][0].at[y], turn("xh", 1, 2)
+            )
+            for y in range(4)
+        ]
+
+    def c2(self, k):
+        for y, copy in enumerate(self.copies[k, 6]):
+            copy.wait_recv()
+            add_into(self.column(y, self.xh, pl.ds(0, 4), k), self.third[k][0].at[y])
+        half, far = self.third[k][1], near("y", 2)
+        self.copies[k, 7] = [
+            self.wires.go(self.column(far, self.xh, pl.ds(0, 2), k), half.at[0], turn("y", 1, 4)),
+            self.wires.go(self.column(far, self.xh, pl.ds(2, 2), k), half.at[1], turn("y", -1, 4)),
+        ]
+
+    def c2b(self, k):
+        half, full = self.third[k][1], self.third[k][2]
+        sent = []
+        for i, step in enumerate((1, -1)):
+            self.copies[k, 7][i].wait_recv()
+            add_into(self.column(near("y", step), self.xh, pl.ds(2 * i, 2), k), half.at[i])
+            part = self.column(near("y", step), self.xh, pl.ds(0, 4), k)
+            sent.append(self.wires.go(part, full.at[i], turn("y", step, 4)))
+        self.copies[k, 8] = sent
+
+    def c3(self, k):
+        for copy in self.copies[k, 8]:
+            copy.wait_recv()
+        full, pieces = self.third[k][2], self.third[k][3]
+        add_into(self.column(self.y, self.xh, pl.ds(0, 4), k), full.at[0], full.at[1])
+        self.copies[k, 9] = [
+            self.wires.go(
+                self.column(self.y, self.xh, near("z", step), k), pieces.at[i], turn("z", step, 4)
+            )
+            for i, step in enumerate((1, -1, 2))
+        ]
+
+    def c4(self, k):
+        start, count = CHUNKS[k][2]
+        total = self.g[self.z, rows_of(96 * self.y + 48 * self.xh, 48), pl.ds(start, count)].astype(F32)
+        for i, copy in enumerate(self.copies[k, 9]):
+            copy.wait_recv()
+            total = total + self.third[k][3][i].astype(F32)
+        self.store(start, total)
 
 
 def scatter_buffers():
     shapes = []
-    for (a0, an), (b0, bn) in CHUNKS:
+    for (_, an), (_, bn), (_, cn) in CHUNKS:
         shapes += [
             pltpu.VMEM((2, 192, an), BF),
             pltpu.VMEM((2, 384, an), BF),
@@ -464,12 +604,22 @@
             pltpu.VMEM((2, 48, bn), BF),
             pltpu.VMEM((2, 96, bn), BF),
         ]
+        if cn:
+            shapes += [
+                pltpu.VMEM((4, 4, 48, cn), BF),
+                pltpu.VMEM((2, 2, 48, cn), BF),
+                pltpu.VMEM((2, 4, 48, cn), BF),
+                pltpu.VMEM((3, 48, cn), BF),
+            ]
     return shapes
 
 
 def make_scatter(wires, g, bufs, last, out):
-    n = len(CHUNKS)
-    groups = [bufs[8 * k : 8 * k + 8] for k in range(n)]
+    groups, bufs = [], list(bufs)
+    for chunk in CHUNKS:
+        count = 12 if chunk[2][1] else 8
+        groups.append(bufs[:count])
+        bufs = bufs[count:]
     return Scatter(
         wires,
         g,
@@ -479,6 +629,7 @@
         [b[3] for b in groups],
         [(b[4], b[6]) for b in groups],
         [(b[5], b[7]) for b in groups],
+        [b[8:] for b in groups],
         last,
         out,
     )
@@ -608,13 +759,15 @@
 ):
     z, y, xh, xl, c = (lax.axis_index(a) for a in FSDP + SP)
     shard_rows = rows_of(96 * y + 48 * xh, 48)
-    pieces = [(wq_ref, 384 * which + 128 * h, 384 * h + 128 * which, 128) for h in range(3) for which in range(3)]
-    pieces += [(wo_ref, 0, 1152, 384), (wi_ref, 0, 1536, 1536), (wb_ref, 0, 3072, 1536)]
+    pieces = [
+        (wq_ref.at[which, :, pl.ds(128 * h, 128)], 384 * h + 128 * which, 128)
+        for h in range(3)
+        for which in range(3)
+    ]
+    pieces += [(wo_ref, 1152, 384), (wi_ref, 1536, 1536), (wb_ref, 3072, 1536)]
     loads = [
-        pltpu.make_async_copy(
-            ref.at[:, pl.ds(at, count)], w.at[z, shard_rows, pl.ds(to, count)], local_sem.at[i]
-        )
-        for i, (ref, at, to, count) in enumerate(pieces)
+        pltpu.make_async_copy(part, w.at[z, shard_rows, pl.ds(at, count)], local_sem.at[i])
+        for i, (part, at, count) in enumerate(pieces)
     ]
     inputs = [
         pltpu.make_async_copy(a, b, local_sem.at[12 + i])
@@ -626,10 +779,9 @@
             (("final", final_ref, final_out), ("ig", ig_ref, ig_out), ("sums", sums_ref, sums_out))
         )
     }
+    greet()
     for load in loads[:3] + inputs[:2] + loads[3:] + inputs[2:]:
         load.start()
-    with jax.named_scope("greet"):
-        greet(sp=True)
     wires = Wires(send, recv)
     ag = Gather(wires, w)
     rs = make_scatter(wires, g, bufs, last, sums_ref)
@@ -653,9 +805,10 @@
         return w[:, :, pl.ds(start, count)].reshape(1536, count)
 
     for k in range(len(CHUNKS)):
-        for name in ("s1", "s2", "s2b", "s3", "s3b", "done"):
+        third = ("c1", "c2", "c2b", "c3") if CHUNKS[k][2][1] else ()
+        for name in ("s1", "s2", "s2b", "s3", "s3b", "done", *third):
             steps[f"ag_{name}_{k}"] = functools.partial(getattr(ag, name), k)
-        for name in ("r1", "r1b", "r2", "r2b", "r3", "done"):
+        for name in ("r1", "r1b", "r2", "r2b", "r3", "done", *third, *(("c4",) if third else ())):
             steps[f"rs_{name}_{k}"] = functools.partial(getattr(rs, name), k)
     for key, buf in (("a1", a1), ("dm", dm), ("a2", a2), ("da", da)):
         spread = Spread(wires, buf)
@@ -682,6 +835,8 @@
         for load in loads[:3]:
             load.wait()
 
+    steps["met"] = met
+
     @step
     def load_inputs():
         inputs[0].wait()
@@ -872,10 +1027,30 @@
             steps[name]()
 
 
+def finish_kernel(
+    final_in, ig_in, sums_in, final_out, ig_out, gq_out, go_out, gi_out, gb_out, final, ig, sums, sem
+):
+    cuts = [(384 * which, 384, gq_out.at[which]) for which in range(3)]
+    cuts += [(1152, 384, go_out), (1536, 1536, gi_out), (3072, 1536, gb_out)]
+    pairs = [(sums_in.at[:, pl.ds(at, n)], sums.at[:, pl.ds(at, n)], out) for at, n, out in cuts]
+    pairs += [(ig_in, ig, ig_out), (final_in, final, final_out)]
+    loads, stores = [], []
+    for i, (source, held, out) in enumerate(pairs):
+        loads.append(pltpu.make_async_copy(source, held, sem.at[0, i]))
+        stores.append(pltpu.make_async_copy(held, out, sem.at[1, i]))
+    for load in loads:
+        load.start()
+    for load, store in zip(loads, stores):
+        load.wait()
+        store.start()
+    for store in stores:
+        store.wait()
+
+
 def body(tokens, modulation, w_qkv, w_out, w_in, w_back, out_grad):
     own = w_qkv.shape[3]
     far = pl.BlockSpec(memory_space=pl.ANY)
-    copies = 34 * len(CHUNKS) + 40
+    copies = 54 * len(CHUNKS) + 40
     rows = lambda n, dtype=BF: pltpu.VMEM((512, n), dtype)
     final, grad_in_rows, sums = pl.pallas_call(
         block_kernel,
@@ -920,19 +1095,33 @@
         tokens[0],
         modulation[0, 0],
         out_grad[0],
-        w_qkv[0].reshape(48, 3 * own),
+        w_qkv[0].transpose(1, 0, 2),
         w_out[0].T,
         w_in[0],
         w_back[0].T,
     )
-    return (
-        final[None],
-        grad_in_rows[None],
-        sums[:, :1152].reshape(1, 48, 3, own),
-        sums[:, 1152:1536].T[None],
-        sums[:, 1536:3072][None],
-        sums[:, 3072:].T[None],
-    )
+    outs = pl.pallas_call(
+        finish_kernel,
+        out_shape=(
+            jax.ShapeDtypeStruct((128, 1536), BF),
+            jax.ShapeDtypeStruct((128, 1536), F32),
+            jax.ShapeDtypeStruct((3, 48, own), F32),
+            jax.ShapeDtypeStruct((48, own), F32),
+            jax.ShapeDtypeStruct((48, 4 * own), F32),
+            jax.ShapeDtypeStruct((48, 4 * own), F32),
+        ),
+        in_specs=[far] * 3,
+        out_specs=(far,) * 6,
+        scratch_shapes=[
+            pltpu.VMEM((128, 1536), BF),
+            pltpu.VMEM((128, 1536), F32),
+            pltpu.VMEM((48, WIDTH), F32),
+            pltpu.SemaphoreType.DMA((2, 8)),
+        ],
+        name="finish",
+    )(final, grad_in_rows, sums)
+    final, grad_in_rows, gq, go, gi, gb = outs
+    return (final[None], grad_in_rows[None], gq.transpose(1, 0, 2)[None], go.T[None], gi[None], gb.T[None])
 
 
 def solution(mesh):

time: 184 us -> 167 us (0.908)
  local copies, waits for them, and re-layouts: 10 us -> 1.39 us
  Pallas kernels: 173 us -> 165 us
    pallas_call x1, Pallas kernels: 173 us -> 162 us  [body(): pl.pallas_call(block_kernel, out_shape=(jax.ShapeDtypeStruct((128, 1536),...]
    unnamed x10 -> x1, local copies, waits for them, and re-layouts: 5.54 us -> 1.39 us
    broadcast_in_dim x2 -> x0, local copies, waits for them, and re-layouts: 3.42 us -> none  [the longest x1 1.9 us: body(): sums[:, 3072:].T[None]]
    pallas_call x0 -> x1, Pallas kernels: none -> 2.62 us  [body(): pl.pallas_call(finish_kernel, out_shape=(jax.ShapeDtypeStruct((128, 1536)...]
where the time goes in v4:
time: 167 us
  Pallas kernels  165 us (99%)
    pallas_call x1, Pallas kernels, body(): pl.pallas_call(block_kernel, out_shape=(jax.ShapeDtypeStruct((128, 1536),...  162 us

profile of v4, /device:TPU:0, one launch (start us, length us, event | category | flops | bytes accessed | tf_op | source)
XLA Modules:
  0.0 166.7 jit_solution(174420498931087966)
XLA Ops:
  0.6 1.4 copy.15
  2.0 161.9 %block.1 = (bf16[128,1536]{1,0:T(8,128)(2,1)}, f32[128,1536]{1,0:T(8,128)}, f32[48,4608]{1,0:T(8,128)}) custom-call(bf16[128,1536]{1,0:T(8,128)(2,1)} %bitcast.27, f32[6,1536]{1,0:T(8,128)} %bitcast.29, bf16[128,1536]{1,0:T(8,128)(2,1)} %bitcast.28, bf16[3,48,384]{2,1,0:T(8,128)(2,1)} %bitcast.32, bf16[48,384]{1,0:T(8,128)(2,1)} %bitcast.33, ...), custom_call_target="tpu_custom_call" | custom-call | tf_op jit(solution)/shard_map/block/pallas_call | solution.py:1055
  164.0 2.6 %finish.1 = (bf16[128,1536]{1,0:T(8,128)(2,1)}, f32[128,1536]{1,0:T(8,128)}, f32[3,48,384]{2,1,0:T(8,128)}, f32[48,384]{1,0:T(8,128)}, f32[48,1536]{1,0:T(8,128)}, /*index=5*/f32[48,1536]{1,0:T(8,128)}) custom-call(bf16[128,1536]{1,0:T(8,128)(2,1)} %get-tuple-element.15.final_in, f32[128,1536]{1,0:T(8,128)} %get-tuple-element.16.ig_in, ...), custom_call_target="tpu_custom_call" | custom-call | tf_op jit(solution)/shard_map/finish/pallas_call | solution.py:1103

commit v5 on v4

--- a/solution.py
+++ b/solution.py
@@ -20,7 +20,7 @@
 temper = 2.5
 VMEM_LIMIT = 67_000_000
 
-TILES = ((2, 1, 0), (3, 2, 1), (1, 2, 0), (2, 3, 1), (3, 2, 1), (2, 3, 1), (3, 2, 1))
+TILES = ((2, 1, 0), (3, 2, 1), (1, 1, 1), (2, 3, 1), (3, 2, 1), (2, 3, 1), (3, 2, 1))
 
 
 def split_chunks():
@@ -40,222 +40,231 @@
     "load_first",
     "met",
     "load_rest",
+    "ag_s1_2",
+    "ag_c1_2",
+    "ag_s1_0",
+    "load_inputs",
+    "ag_s1_1",
     "ag_c1_1",
-    "ag_c1_4",
-    "ag_s1_0",
     "ag_s1_4",
-    "ag_s1_1",
-    "load_inputs",
-    "ag_s1_2",
-    "ag_c2_1",
     "ag_s1_3",
-    "ag_c1_5",
-    "ag_c2_4",
+    "ag_c1_3",
+    "ag_s1_5",
+    "first_norm_1",
+    "ag_c1_6",
+    "ag_s2_2",
+    "ag_c2_2",
+    "ag_s2_0",
+    "gate_grad",
     "first_norm_0",
     "a1_start_0",
-    "ag_s2_0",
-    "gate_grad",
+    "dm_start_1",
+    "ag_s1_6",
+    "ag_s2_1",
+    "ag_c2_3",
+    "ag_c1_5",
+    "ag_c1_4",
     "ag_s2_4",
-    "ag_s2_1",
-    "ag_c1_3",
-    "first_norm_1",
-    "ag_s2_2",
-    "dm_start_1",
     "ag_s2b_0",
+    "ag_s2b_2",
+    "ag_c2_1",
+    "ag_s2_3",
+    "a1_start_1",
+    "ag_c2_4",
+    "ag_c2_6",
+    "ag_s2b_1",
+    "ag_s3_0",
+    "ag_c2b_1",
+    "ag_s3_2",
+    "a1_relay_0",
+    "ag_c2b_3",
+    "ag_c2b_2",
     "ag_s2b_4",
+    "ag_s3b_0",
+    "ag_c2_5",
     "dm_start_0",
-    "ag_s2b_1",
-    "ag_s2b_2",
-    "ag_c2b_1",
-    "ag_c1_6",
-    "ag_s1_5",
-    "ag_c2_5",
-    "ag_s3_0",
-    "ag_c2_6",
-    "a1_relay_0",
-    "ag_s1_6",
     "ag_s3_1",
-    "a1_start_1",
-    "ag_c2_3",
+    "ag_c2b_4",
     "ag_c3_1",
-    "ag_s2_3",
-    "ag_s3b_0",
+    "ag_c2b_6",
+    "dm_relay_0",
+    "a1_relay_1",
+    "ag_s2_6",
+    "dm_relay_1",
+    "a1_done",
+    "ag_s2b_3",
+    "ag_done_0",
+    "ag_c3_2",
+    "ag_s3b_1",
     "dm_own_half",
-    "ag_c2b_4",
-    "ag_s3_2",
-    "ag_c2b_3",
-    "ag_s3b_1",
-    "dm_relay_0",
-    "ag_c3_4",
-    "a1_relay_1",
-    "a1_done",
-    "ag_done_0",
-    "ag_s2b_3",
-    "ag_s3b_2",
+    "ag_s2_5",
+    "dm_release",
+    "ag_c3_3",
     "a1_own_half",
     "project_0",
-    "ag_s2_5",
+    "ag_c3_4",
+    "attend_0",
+    "ag_s3b_2",
+    "ag_done_1",
     "ag_s3_4",
-    "dm_relay_1",
-    "attend_0",
-    "ag_c2b_6",
-    "ag_done_1",
-    "ag_s2_6",
     "project_1",
-    "ag_c3_3",
+    "attend_other",
+    "ag_c2b_5",
     "ag_done_2",
-    "attend_other",
     "att_mm_other",
     "att_other",
     "ag_s3_3",
+    "dm_done",
+    "att_send",
     "attend_own",
-    "att_send",
-    "dm_done",
-    "ag_c2b_5",
-    "ag_s3b_4",
-    "ag_s2b_5",
     "att_mm_own",
     "att_own",
+    "att_release",
+    "ag_s2b_6",
+    "ag_s2b_5",
     "att_wait_0",
+    "ag_s3b_4",
     "second_norm_0",
+    "ag_s3b_3",
     "a2_start_0",
-    "ag_s2b_6",
-    "ag_s3b_3",
+    "ag_done_4",
+    "ag_s3_5",
     "att_wait_1",
+    "ag_s3_6",
     "second_norm_1",
     "a2_start_1",
-    "ag_s3_6",
+    "ag_done_3",
+    "a2_relay_0",
+    "a2_own_half",
+    "hidden_own_1",
+    "a2_relay_1",
+    "ag_c3_5",
     "ag_c3_6",
-    "a2_own_half",
-    "ag_s3_5",
-    "a2_relay_0",
-    "a2_relay_1",
-    "ag_done_3",
-    "ag_done_4",
-    "hidden_own_1",
     "hidden_own_0",
-    "ag_c3_5",
-    "att_release",
     "a2_done",
-    "dm_release",
+    "hidden_other_0",
+    "ag_s3b_5",
+    "hidden_other_1",
+    "grad_back_1",
     "ag_s3b_6",
-    "hidden_other_1",
-    "hidden_other_0",
-    "grad_back_1",
-    "rs_c1_6",
-    "ag_s3b_5",
+    "rs_r1_6",
     "grad_back_0",
+    "rs_r1_5",
+    "ag_done_5",
+    "rs_c1_5",
+    "hidden_grad_0",
+    "grad_in_0",
+    "rs_r1_3",
     "ag_done_6",
-    "rs_c1_5",
-    "rs_r1_6",
-    "rs_r1_5",
+    "rs_c1_3",
     "hidden_grad_1",
-    "grad_in_1",
-    "rs_r1_4",
-    "ag_done_5",
-    "hidden_grad_0",
-    "rs_c1_4",
-    "rs_r1b_6",
     "da2_mm_other",
     "da2_other",
+    "rs_r1b_5",
     "da2_send",
+    "ffn_mm_other",
     "da2_mm_own",
-    "rs_r1b_5",
+    "rs_r1b_3",
+    "grad_in_1",
+    "rs_c2_3",
     "da2_own",
-    "ffn_mm_other",
-    "rs_c2_5",
-    "grad_in_0",
+    "rs_r1_4",
     "da2_wait_0",
+    "ffn_other",
     "mid_grad_0",
-    "rs_c2_6",
-    "rs_c2_4",
     "da_start_0",
-    "rs_r1b_4",
-    "rs_c2b_6",
-    "rs_c2b_5",
     "rs_r2_5",
-    "rs_c2b_4",
+    "rs_r1b_6",
     "da2_wait_1",
     "mid_grad_1",
+    "ffn_mm_own",
     "da_start_1",
+    "rs_r1b_4",
+    "rs_c1_6",
+    "da_relay_0",
     "da_own_half",
+    "rs_r2_3",
+    "rs_c2_5",
+    "da_relay_1",
+    "ffn_own",
+    "heads_own",
+    "rs_c2b_3",
+    "da_done",
+    "rs_c1_4",
+    "heads_other",
+    "rs_r2b_5",
     "rs_r2_6",
-    "da2_release",
-    "da_relay_0",
-    "heads_own",
-    "rs_r1_3",
-    "ffn_other",
-    "rs_c1_3",
-    "rs_r2b_5",
-    "da_relay_1",
-    "ffn_mm_own",
-    "rs_r2b_6",
-    "da_done",
-    "rs_c3_5",
-    "grad_out",
-    "heads_other",
-    "rs_r1_2",
     "ffn_send",
-    "rs_r1b_3",
-    "rs_c3_6",
     "attend_back_1",
     "grad_q_1",
+    "rs_r1_1",
+    "rs_c2b_5",
+    "attend_back_0",
+    "rs_r2_4",
+    "rs_c1_1",
+    "grad_q_0",
+    "rs_c2_4",
+    "rs_r1_0",
+    "rs_r2b_3",
+    "grad_out",
+    "rs_c2b_4",
+    "rs_r3_5",
+    "rs_c1_2",
+    "rs_r1_2",
+    "rs_c2_6",
+    "da2_release",
+    "rs_r2b_4",
+    "da1_mm_own",
+    "ffn_wait_0",
+    "rs_r2b_6",
+    "rs_r3_3",
+    "rs_r1b_1",
+    "da1_mm_other",
+    "rs_c3_5",
+    "da1_other",
+    "da1_own",
+    "rs_c2b_6",
+    "rs_r1b_0",
+    "ffn_wait_1",
+    "rs_r3_4",
+    "da1_send",
+    "rs_c2_1",
+    "rs_r2_1",
+    "rs_done_5",
+    "rs_c2_2",
+    "rs_r1b_2",
+    "rs_c4_5",
+    "rs_r2_0",
+    "rs_c3_4",
     "rs_r3_6",
-    "rs_c4_5",
-    "rs_r1b_2",
-    "rs_r1_1",
-    "attend_back_0",
-    "ffn_own",
-    "da1_mm_other",
-    "rs_c1_1",
-    "rs_r3_5",
-    "ffn_wait_0",
-    "rs_r2_4",
-    "grad_q_0",
-    "rs_r1_0",
-    "da1_other",
-    "da1_send",
-    "rs_r2_3",
-    "rs_c3_4",
+    "rs_done_3",
+    "rs_r2b_1",
+    "last_out",
+    "rs_c3_6",
+    "rs_r2_2",
+    "rs_c3_3",
+    "rs_r2b_0",
+    "rs_done_4",
+    "rs_c2b_1",
+    "rs_c2b_2",
+    "rs_r2b_2",
+    "da1_wait_0",
+    "rs_r3_0",
+    "rs_r3_1",
+    "rs_c4_4",
+    "rs_c3_1",
+    "rs_c4_6",
+    "rs_c3_2",
+    "rs_r3_2",
+    "da1_wait_1",
+    "rs_c4_3",
+    "first_grad",
     "rs_done_6",
-    "rs_r1b_1",
-    "da1_mm_own",
-    "da1_own",
-    "rs_c2_3",
-    "rs_r1b_0",
-    "rs_r2b_3",
-    "da1_wait_0",
-    "rs_r2_1",
-    "rs_c4_6",
-    "rs_r2_2",
-    "rs_r2b_4",
-    "da1_wait_1",
-    "first_grad",
-    "rs_r2_0",
-    "rs_r2b_1",
-    "rs_r2b_2",
-    "ffn_wait_1",
-    "rs_r3_3",
-    "rs_c2_1",
-    "rs_r3_4",
-    "rs_r2b_0",
-    "rs_c2b_3",
-    "rs_r3_1",
-    "rs_c2b_1",
-    "rs_done_3",
-    "rs_c4_4",
-    "rs_r3_2",
-    "rs_done_5",
-    "rs_r3_0",
-    "rs_c3_3",
-    "rs_done_4",
-    "rs_c3_1",
+    "rs_done_0",
     "rs_done_1",
-    "last_out",
-    "rs_c4_3",
+    "rs_c4_2",
+    "rs_c4_1",
     "rs_done_2",
-    "rs_done_0",
-    "rs_c4_1",
     "finish",
 )
 
@@ -796,7 +805,7 @@
         return fn
 
     def mod(i):
-        return m_ref[pl.ds(i, 1), :]
+        return m_ref[i]
 
     def own(start):
         return (rows_of(own_row + start, BLOCK), slice(None))
@@ -1063,7 +1072,7 @@
         out_specs=(far, far, far),
         scratch_shapes=[
             pltpu.VMEM((128, 1536), BF),
-            pltpu.VMEM((6, 1536), F32),
+            pltpu.VMEM((6, 1, 1536), F32),
             pltpu.VMEM((128, 1536), BF),
             pltpu.VMEM((128, 1536), BF),
             pltpu.VMEM((128, 1536), F32),
@@ -1093,7 +1102,7 @@
         name="block",
     )(
         tokens[0],
-        modulation[0, 0],
+        modulation[0].transpose(1, 0, 2),
         out_grad[0],
         w_qkv[0].transpose(1, 0, 2),
         w_out[0].T,

time: 167 us -> 169 us (1.012)
  Pallas kernels: 165 us -> 168 us
    pallas_call x1, Pallas kernels: 162 us -> 165 us  [body(): pl.pallas_call(block_kernel, out_shape=(jax.ShapeDtypeStruct((128, 1536),...]
where the time goes in v5:
time: 169 us
  Pallas kernels  168 us (99%)
    pallas_call x1, Pallas kernels, body(): pl.pallas_call(block_kernel, out_shape=(jax.ShapeDtypeStruct((128, 1536),...  165 us

profile of v5, /device:TPU:0, one launch (start us, length us, event | category | flops | bytes accessed | tf_op | source)
XLA Modules:
  0.0 168.9 jit_solution(11131172036685236323)
XLA Ops:
  0.6 165.4 %block.1 = (bf16[128,1536]{1,0:T(8,128)(2,1)}, f32[128,1536]{1,0:T(8,128)}, f32[48,4608]{1,0:T(8,128)}) custom-call(bf16[128,1536]{1,0:T(8,128)(2,1)} %bitcast.25, f32[6,1,1536]{2,1,0:T(1,128)} %bitcast.30, bf16[128,1536]{1,0:T(8,128)(2,1)} %bitcast.26, bf16[3,48,384]{2,1,0:T(8,128)(2,1)} %bitcast.29, bf16[48,384]{1,0:T(8,128)(2,1)} %bitcast.31, ...), custom_call_target="tpu_custom_call" | custom-call | tf_op jit(solution)/shard_map/block/pallas_call | solution.py:1064
  166.1 2.6 %finish.1 = (bf16[128,1536]{1,0:T(8,128)(2,1)}, f32[128,1536]{1,0:T(8,128)}, f32[3,48,384]{2,1,0:T(8,128)}, f32[48,384]{1,0:T(8,128)}, f32[48,1536]{1,0:T(8,128)}, /*index=5*/f32[48,1536]{1,0:T(8,128)}) custom-call(bf16[128,1536]{1,0:T(8,128)(2,1)} %get-tuple-element.15.final_in, f32[128,1536]{1,0:T(8,128)} %get-tuple-element.16.ig_in, ...), custom_call_target="tpu_custom_call" | custom-call | tf_op jit(solution)/shard_map/finish/pallas_call | solution.py:1112

commit v6 on v3

--- a/solution.py
+++ b/solution.py
@@ -20,190 +20,194 @@
 temper = 2.5
 VMEM_LIMIT = 67_000_000
 
-CHUNKS = (
-    ((0, 256), (256, 128)),
-    ((384, 384), (768, 384)),
-    ((1152, 128), (1280, 256)),
-    ((1536, 384), (1920, 384)),
-    ((2304, 384), (2688, 384)),
-    ((3072, 384), (3456, 384)),
-    ((3840, 384), (4224, 384)),
-)
+TILES = ((2, 1), (3, 3), (1, 2), (3, 3), (3, 3))
+
+
+def split_chunks():
+    chunks, at = [], 0
+    for tiles in TILES:
+        parts = []
+        for count in tiles:
+            parts.append((at, 128 * count))
+            at += 128 * count
+        chunks.append(tuple(parts))
+    return tuple(chunks)
+
+
+CHUNKS = split_chunks()
+HELD = 3072
+STEPS = {"own": 0, "next": 1, "prev": -1, "far": 2}
 WIDTH = 4608
 ORDER = (
     "load_first",
+    "load_inputs",
+    "met",
     "ag_s1_0",
-    "load_inputs",
     "first_norm_0",
     "load_rest",
+    "gate_grad",
     "ag_s1_2",
     "ag_s1_1",
-    "ag_s1_3",
     "ag_s2_0",
-    "gate_grad",
-    "ag_s1_6",
+    "first_norm_1",
+    "a1_start_0",
     "ag_s2_2",
-    "first_norm_1",
     "ag_s2b_0",
+    "ag_s2_1",
+    "ag_s2b_2",
     "a1_start_1",
-    "ag_s2b_2",
-    "ag_s2_1",
-    "a1_start_0",
     "ag_s3_0",
-    "ag_s3_2",
+    "ag_s2b_1",
     "ag_s1_4",
     "dm_start_0",
-    "ag_s2b_1",
+    "ag_s3_2",
+    "a1_relay_0",
+    "ag_s1_3",
+    "ag_s3_1",
+    "a1_own_half",
+    "ag_s3b_0",
+    "dm_start_1",
+    "a1_relay_1",
+    "ag_s3b_1",
+    "a1_done",
+    "ag_s3b_2",
+    "dm_relay_0",
     "ag_s2_3",
-    "ag_s3b_2",
-    "ag_s3_1",
-    "ag_s2b_3",
-    "a1_relay_0",
-    "dm_start_1",
-    "ag_s3b_0",
-    "ag_done_2",
-    "ag_s3b_1",
-    "a1_relay_1",
-    "ag_s2_6",
-    "ag_s2_4",
-    "a1_own_half",
-    "ag_s1_5",
-    "a1_done",
     "ag_done_0",
     "project_0",
-    "ag_s3_3",
     "attend_0",
     "ag_done_1",
-    "dm_relay_0",
-    "dm_relay_1",
     "project_1",
+    "ag_s2_4",
+    "ag_done_2",
     "attend_other",
-    "dm_release",
     "att_mm_other",
+    "ag_s2b_3",
+    "att_other",
     "ag_s2b_4",
-    "ag_s2_5",
-    "dm_own_half",
-    "ag_s2b_6",
-    "att_other",
+    "att_send",
+    "ag_s3_3",
     "attend_own",
+    "dm_relay_far",
     "att_mm_own",
     "att_own",
-    "att_send",
+    "dm_relay_1",
+    "dm_own_half",
+    "dm_done",
+    "att_wait_0",
+    "second_norm_0",
     "ag_s3_4",
-    "ag_s2b_5",
-    "att_wait_0",
-    "ag_s3b_3",
-    "second_norm_0",
-    "ag_s3b_4",
     "a2_start_0",
     "att_wait_1",
-    "ag_s3_5",
     "second_norm_1",
+    "ag_s3b_3",
+    "a2_start_1",
+    "a2_own_half",
+    "ag_s3b_4",
+    "a2_relay_0",
+    "a2_relay_1",
+    "ag_done_3",
+    "hidden_own",
+    "a2_done",
+    "hidden_next",
+    "dm_done_far",
+    "ag_done_4",
+    "hgrad_next",
+    "a2_relay_far",
+    "da2_mm_next",
+    "a2_done_far",
+    "da2_give_next",
+    "hidden_far",
+    "hgrad_far",
+    "da2_mm_far",
+    "da2_give_far",
+    "hidden_prev",
+    "da2_take_far",
+    "hgrad_prev",
+    "da2_mm_prev",
+    "da2_take_next",
+    "da2_give_prev",
+    "grad_back_1",
+    "da2_take_prev",
+    "grad_back_0",
+    "hgrad_own",
+    "rs_r1_4",
+    "da2_pass_on",
+    "grad_in_0",
+    "dm_release",
     "att_release",
-    "ag_s3_6",
-    "a2_relay_0",
-    "a2_start_1",
-    "a2_relay_1",
-    "ag_s3b_5",
-    "a2_done",
-    "a2_own_half",
-    "ag_done_4",
-    "ag_done_3",
-    "hidden_other_1",
-    "hidden_other_0",
-    "dm_done",
-    "hidden_own_0",
-    "hidden_own_1",
-    "ag_s3b_6",
-    "grad_back_1",
-    "rs_r1_6",
-    "grad_back_0",
-    "ag_done_5",
-    "rs_r1_5",
-    "hidden_grad_0",
-    "ag_done_6",
-    "hidden_grad_1",
-    "da2_mm_other",
-    "da2_other",
-    "rs_r1b_6",
+    "grad_in_1",
+    "rs_r1_3",
     "da2_mm_own",
-    "da2_send",
-    "grad_in_1",
-    "grad_in_0",
-    "da2_own",
-    "rs_r1b_5",
-    "da2_wait_0",
-    "rs_r1_4",
+    "da2_give_own",
+    "rs_r1b_4",
+    "ffn_mm_prev",
+    "da2_take_own",
+    "da2_wait",
     "mid_grad_0",
+    "da_start_0",
+    "mid_grad_1",
+    "ffn_give_prev",
+    "da_start_1",
     "ffn_mm_own",
-    "rs_r1_3",
-    "da_start_0",
-    "da2_wait_1",
-    "mid_grad_1",
-    "da_start_1",
-    "rs_r2_6",
-    "rs_r2_5",
-    "rs_r1b_4",
+    "ffn_mm_far",
+    "ffn_give_far",
+    "ffn_mm_next",
+    "ffn_take_far",
     "da_own_half",
+    "rs_r1b_3",
     "da_relay_0",
-    "ffn_mm_other",
-    "ffn_other",
-    "da2_release",
-    "ffn_own",
+    "rs_r2_4",
+    "heads_own",
+    "ffn_give_next",
     "da_relay_1",
-    "ffn_send",
-    "heads_own",
-    "rs_r1b_3",
     "da_done",
+    "grad_out",
+    "rs_r1_2",
+    "ffn_give_own",
     "heads_other",
+    "rs_r2_3",
+    "rs_r2b_4",
+    "attend_back_1",
+    "rs_r1b_2",
+    "rs_r2b_3",
+    "grad_q_1",
+    "rs_r1_1",
     "attend_back_0",
-    "attend_back_1",
+    "ffn_take_next",
+    "grad_q_0",
+    "rs_r1_0",
+    "da1_mm_other",
+    "ffn_take_own",
+    "ffn_take_prev",
+    "rs_r3_3",
+    "rs_r2_2",
+    "rs_r3_4",
+    "da1_other",
+    "rs_r1b_1",
+    "rs_r1b_0",
+    "ffn_pass_on",
+    "da1_send",
+    "rs_done_3",
+    "rs_r2_1",
     "da1_mm_own",
-    "ffn_wait_0",
-    "grad_q_1",
-    "rs_r2_4",
-    "rs_r1_1",
     "da1_own",
-    "da1_mm_other",
-    "da1_other",
-    "rs_r2b_5",
-    "grad_out",
-    "rs_r2_3",
-    "rs_r2b_6",
-    "rs_r1b_1",
-    "rs_r1_2",
-    "da1_send",
-    "ffn_wait_1",
-    "rs_r3_5",
-    "grad_q_0",
-    "rs_r2b_3",
-    "rs_r1_0",
-    "rs_r2b_4",
-    "rs_r2_1",
+    "rs_r2b_2",
+    "rs_r2_0",
+    "rs_r2b_1",
+    "rs_r2b_0",
+    "rs_r3_2",
+    "rs_r3_1",
+    "rs_done_4",
+    "da1_wait_0",
+    "ffn_wait",
     "last_out",
-    "rs_r1b_0",
-    "rs_r3_3",
-    "da1_wait_0",
-    "rs_r1b_2",
-    "rs_r2b_1",
+    "rs_r3_0",
+    "rs_done_2",
     "da1_wait_1",
-    "rs_r3_6",
-    "rs_r3_4",
-    "rs_r2_0",
-    "rs_r2_2",
-    "rs_done_6",
-    "rs_r3_1",
-    "rs_r2b_0",
-    "rs_done_3",
-    "rs_r2b_2",
-    "rs_r3_0",
-    "rs_r3_2",
     "first_grad",
-    "rs_done_5",
-    "rs_done_4",
+    "rs_done_1",
     "rs_done_0",
-    "rs_done_1",
-    "rs_done_2",
     "finish",
 )
 
@@ -245,14 +249,35 @@
         self.open = []
 
 
-def greet(sp=False):
-    barrier = pltpu.get_barrier_semaphore()
-    targets = [turn("z", 1, 4), turn("z", -1, 4), turn("y", 1, 4), turn("y", -1, 4), turn("xh", 1, 2)]
-    if sp:
-        targets += [turn("xl", 1, 2), turn("c", 1, 2)]
-    for device in targets:
-        pl.semaphore_signal(barrier, inc=1, device_id=device, device_id_type=MESH)
-    pl.semaphore_wait(barrier, len(targets))
+def chip(step):
+    xh, xl = lax.axis_index("xh"), lax.axis_index("xl")
+    if step == 0:
+        return xh, xl
+    if step == 2:
+        return 1 - xh, xl
+    return lax.rem(xh + xl + (0 if step == 1 else 1), 2), 1 - xl
+
+
+def along(step):
+    xh, xl = chip(step)
+    return {"xh": xh, "xl": xl}
+
+
+def partners():
+    return [turn("z", 1, 4), turn("z", -1, 4), turn("y", 1, 4), turn("y", -1, 4)] + [
+        turn("xh", 1, 2), turn("c", 1, 2), along(1), along(-1)
+    ]
+
+
+def greet():
+    for device in partners():
+        pl.semaphore_signal(
+            pltpu.get_barrier_semaphore(), inc=1, device_id=device, device_id_type=MESH
+        )
+
+
+def met():
+    pl.semaphore_wait(pltpu.get_barrier_semaphore(), len(partners()))
 
 
 def rows_of(start, count):
@@ -264,8 +289,8 @@
 
 
 class Gather:
-    def __init__(self, wires, w):
-        self.wires, self.w = wires, w
+    def __init__(self, wires, w, stage):
+        self.wires, self.w, self.stage = wires, w, stage
         self.z, self.y, self.xh = (lax.axis_index(a) for a in FSDP)
         self.one, self.two, self.relay2, self.three, self.relay3 = {}, {}, {}, {}, {}
 
@@ -275,7 +300,8 @@
     def s1(self, k):
         (a0, an), (b0, bn) = CHUNKS[k]
         part = self.w.at[self.z, rows_of(96 * self.y + 48 * self.xh, 48), pl.ds(a0, an + bn)]
-        self.one[k] = self.same(part, turn("xh", 1, 2))
+        source = part if k < 3 else self.stage.at[:, pl.ds(a0 - 1536, an + bn)]
+        self.one[k] = self.wires.go(source, part, turn("xh", 1, 2))
 
     def s2(self, k):
         self.one[k].wait_recv()
@@ -441,9 +467,15 @@
         (a0, an), (b0, bn) = CHUNKS[k]
         self.copies[k, 5][0].wait_recv()
         cols = pl.ds(a0, an + bn)
-        own = self.g[self.z, rows_of(96 * self.y + 48 * self.xh, 48), cols]
-        total = own.astype(F32) + self.last[:, cols].astype(F32)
-        if a0 >= 1152:
+        own = self.g[self.z, rows_of(96 * self.y + 48 * self.xh, 48), cols].astype(F32)
+        came = self.last[:, cols].astype(F32)
+        if k >= 3:
+            base = 1536 * (k - 2)
+            self.out[:, pl.ds(pl.multiple_of(base + 768 * self.xh, 128), 768)] = own
+            self.out[:, pl.ds(pl.multiple_of(base + 768 * (1 - self.xh), 128), 768)] = came
+            return
+        total = own + came
+        if k == 2:
             self.out[:, cols] = total
             return
         for at in range(0, an + bn, 128):
@@ -453,7 +485,7 @@
 
 def scatter_buffers():
     shapes = []
-    for (a0, an), (b0, bn) in CHUNKS:
+    for (_, an), (_, bn) in CHUNKS:
         shapes += [
             pltpu.VMEM((2, 192, an), BF),
             pltpu.VMEM((2, 384, an), BF),
@@ -468,8 +500,7 @@
 
 
 def make_scatter(wires, g, bufs, last, out):
-    n = len(CHUNKS)
-    groups = [bufs[8 * k : 8 * k + 8] for k in range(n)]
+    groups = [bufs[8 * k : 8 * k + 8] for k in range(len(CHUNKS))]
     return Scatter(
         wires,
         g,
@@ -567,6 +598,113 @@
         return total + self.cross[pl.ds(start, count), :].astype(F32)
 
 
+class RingSpread:
+    def __init__(self, wires, buf):
+        self.wires, self.buf, self.c = wires, buf, lax.axis_index("c")
+        self.sent = {}
+
+    def part(self, step, i):
+        xh, xl = chip(step)
+        return self.buf.at[rows_of(512 * xh + 256 * xl + 128 * self.c + 64 * i, 64), :]
+
+    def go(self, key, step, i, device):
+        self.sent[key] = self.wires.go(self.part(step, i), self.part(step, i), device)
+
+    def start(self, i):
+        self.go(("next", i), 0, i, along(1))
+        self.go(("prev", i), 0, i, along(-1))
+        self.go(("own", i), 0, i, turn("c", 1, 2))
+
+    def side(self, name, step, i):
+        self.sent[name, i].wait_recv()
+        if (name, i) in (("next", 0), ("prev", 1)):
+            self.go(("far", i), step, i, along(-step))
+        self.go(("core", step, i), step, i, turn("c", 1, 2))
+
+    def relay(self, i):
+        if i == 0:
+            self.side("next", -1, 0)
+            self.side("prev", 1, 1)
+        else:
+            self.side("next", -1, 1)
+            self.side("prev", 1, 0)
+
+    def relay_far(self):
+        for i in range(2):
+            self.sent["far", i].wait_recv()
+            self.go(("core", 2, i), 2, i, turn("c", 1, 2))
+
+    def own_half(self):
+        for i in range(2):
+            self.sent["own", i].wait_recv()
+
+    def done(self):
+        for step in (1, -1):
+            for i in range(2):
+                self.sent["core", step, i].wait_recv()
+
+    def done_far(self):
+        for i in range(2):
+            self.sent["core", 2, i].wait_recv()
+
+    def release(self):
+        for copy in self.sent.values():
+            self.wires.sent(copy)
+
+
+class RingCollect:
+    def __init__(self, wires, part, pair, half, full):
+        self.wires, self.part, self.pair, self.half, self.full = wires, part, pair, half, full
+        self.c = lax.axis_index("c")
+        self.sent = {}
+
+    def block(self, step, c, start=0, count=128):
+        xh, xl = chip(step)
+        return self.part.at[rows_of(512 * xh + 256 * xl + 128 * c + start, count), :]
+
+    def give(self, name):
+        step = STEPS[name]
+        self.sent[name] = self.wires.go(self.block(step, 1 - self.c), self.pair.at[step % 4], turn("c", 1, 2))
+
+    def take(self, name):
+        step = STEPS[name]
+        self.sent[name].wait_recv()
+        if step == 0:
+            return
+        add2(self.block(step, self.c), self.pair.at[step % 4])
+        if step == 2:
+            for i, way in enumerate((1, -1)):
+                self.sent["half", way] = self.wires.go(
+                    self.block(2, self.c, 64 * i, 64), self.half.at[i], along(way)
+                )
+            return
+        i = 1 if step == 1 else 0
+        self.sent["early", step] = self.wires.go(
+            self.block(step, self.c, 64 * i, 64), self.full.at[1 - i, pl.ds(64 * i, 64), :], along(step)
+        )
+
+    def pass_on(self):
+        for i, step in enumerate((1, -1)):
+            self.sent["half", step].wait_recv()
+            block = self.block(step, self.c, 64 * i, 64)
+            add2(block, self.half.at[i])
+            self.sent["late", step] = self.wires.go(
+                block, self.full.at[i, pl.ds(64 * i, 64), :], along(step)
+            )
+
+    def wait(self):
+        for step in (1, -1):
+            self.sent["early", step].wait_recv()
+            self.sent["late", step].wait_recv()
+
+    def rows(self, start, count):
+        xh, xl = chip(0)
+        total = self.part[rows_of(512 * xh + 256 * xl + 128 * self.c + start, count), :].astype(F32)
+        for ref in (self.pair.at[0], self.full.at[0], self.full.at[1]):
+            total = total + ref[pl.ds(start, count), :].astype(F32)
+        return total
+
+
 def add2(dst, src):
     rows = dst.shape[0]
 
@@ -603,18 +741,26 @@
     x_in, m_in, og_in, wq_ref, wo_ref, wi_ref, wb_ref,
     final_out, ig_out, sums_out,
     x_ref, m_ref, og_ref, final_ref, ig_ref, sums_ref,
-    w, g, last, a1, dm, a2, da, qkv, o, do, gp, act, part, probs, dv, pair0, cross0, pair1, cross1,
-    mid, dmid, send, recv, local_sem, *bufs,
+    w, g, last, stage, a1, dm, a2, da, qkv, o, do, gp, act, part, ring_part, probs, dv, pair, cross,
+    pair0, half0, full0, pair1, half1, full1, mid, dmid, send, recv, local_sem, *bufs,
 ):
     z, y, xh, xl, c = (lax.axis_index(a) for a in FSDP + SP)
     shard_rows = rows_of(96 * y + 48 * xh, 48)
-    pieces = [(wq_ref, 384 * which + 128 * h, 384 * h + 128 * which, 128) for h in range(3) for which in range(3)]
-    pieces += [(wo_ref, 0, 1152, 384), (wi_ref, 0, 1536, 1536), (wb_ref, 0, 3072, 1536)]
+    pieces = [
+        (wq_ref.at[which, :, pl.ds(128 * h, 128)], 384 * h + 128 * which, 128)
+        for h in range(3)
+        for which in range(3)
+    ]
+    mine = pl.ds(pl.multiple_of(768 * xh, 128), 768)
+    theirs = pl.ds(pl.multiple_of(768 * (1 - xh), 128), 768)
+    pieces += [(wo_ref, 1152, 384), (wi_ref.at[:, mine], 1536, 768), (wb_ref.at[:, mine], 2304, 768)]
     loads = [
-        pltpu.make_async_copy(
-            ref.at[:, pl.ds(at, count)], w.at[z, shard_rows, pl.ds(to, count)], local_sem.at[i]
-        )
-        for i, (ref, at, to, count) in enumerate(pieces)
+        pltpu.make_async_copy(source, w.at[z, shard_rows, pl.ds(at, count)], local_sem.at[i])
+        for i, (source, at, count) in enumerate(pieces)
+    ]
+    loads += [
+        pltpu.make_async_copy(ref.at[:, theirs], stage.at[:, pl.ds(768 * i, 768)], local_sem.at[18 + i])
+        for i, ref in enumerate((wi_ref, wb_ref))
     ]
     inputs = [
         pltpu.make_async_copy(a, b, local_sem.at[12 + i])
@@ -626,12 +772,11 @@
             (("final", final_ref, final_out), ("ig", ig_ref, ig_out), ("sums", sums_ref, sums_out))
         )
     }
+    greet()
     for load in loads[:3] + inputs[:2] + loads[3:] + inputs[2:]:
         load.start()
-    with jax.named_scope("greet"):
-        greet(sp=True)
     wires = Wires(send, recv)
-    ag = Gather(wires, w)
+    ag = Gather(wires, w, stage)
     rs = make_scatter(wires, g, bufs, last, sums_ref)
     own_row = 256 * xl + 128 * c
     own_start, other_start = 256 * xl, 256 * (1 - xl)
@@ -644,10 +789,13 @@
         return fn
 
     def mod(i):
-        return m_ref[pl.ds(i, 1), :]
+        return m_ref[i]
 
     def own(start):
         return (rows_of(own_row + start, BLOCK), slice(None))
+
+    def ring_own(start):
+        return (rows_of(512 * xh + own_row + start, BLOCK), slice(None))
 
     def weights(start, count):
         return w[:, :, pl.ds(start, count)].reshape(1536, count)
@@ -657,30 +805,42 @@
             steps[f"ag_{name}_{k}"] = functools.partial(getattr(ag, name), k)
         for name in ("r1", "r1b", "r2", "r2b", "r3", "done"):
             steps[f"rs_{name}_{k}"] = functools.partial(getattr(rs, name), k)
-    for key, buf in (("a1", a1), ("dm", dm), ("a2", a2), ("da", da)):
+    for key, buf in (("a1", a1), ("da", da)):
         spread = Spread(wires, buf)
         for i in range(2):
             steps[f"{key}_start_{i}"] = functools.partial(spread.start, i)
             steps[f"{key}_relay_{i}"] = functools.partial(spread.relay, i)
         steps[f"{key}_own_half"] = spread.own_half
         steps[f"{key}_done"] = spread.done
-        steps[f"{key}_release"] = spread.release
-    reds = {
-        "att": Collect(wires, part, pair0, cross0),
-        "da2": Collect(wires, part, pair0, cross0),
-        "da1": Collect(wires, part, pair0, cross0),
-        "ffn": Collect(wires, dm, pair1, cross1),
-    }
+    for key, buf in (("dm", dm), ("a2", a2)):
+        spread = RingSpread(wires, buf)
+        for i in range(2):
+            steps[f"{key}_start_{i}"] = functools.partial(spread.start, i)
+            steps[f"{key}_relay_{i}"] = functools.partial(spread.relay, i)
+        for name in ("relay_far", "own_half", "done", "done_far", "release"):
+            steps[f"{key}_{name}"] = getattr(spread, name)
+    reds = {"att": Collect(wires, part, pair, cross), "da1": Collect(wires, part, pair, cross)}
     for key, red in reds.items():
         for name in ("other", "own", "send", "release"):
             steps[f"{key}_{name}"] = getattr(red, name)
         for i in range(2):
             steps[f"{key}_wait_{i}"] = functools.partial(red.wait, i)
+    reds["da2"] = RingCollect(wires, ring_part, pair0, half0, full0)
+    reds["ffn"] = RingCollect(wires, dm, pair1, half1, full1)
+    for key in ("da2", "ffn"):
+        red = reds[key]
+        for name in STEPS:
+            steps[f"{key}_give_{name}"] = functools.partial(red.give, name)
+            steps[f"{key}_take_{name}"] = functools.partial(red.take, name)
+        steps[f"{key}_pass_on"] = red.pass_on
+        steps[f"{key}_wait"] = red.wait
 
     @step
     def load_first():
         for load in loads[:3]:
             load.wait()
+
+    steps["met"] = met
 
     @step
     def load_inputs():
@@ -702,7 +862,7 @@
         value = x_ref[rows, :].astype(F32) + mod(2) * reds["att"].rows(r, BLOCK)
         mid[rows, :] = value
         n2, _ = normalize(value)
-        a2[own(r)] = (n2 * (1.0 + mod(4)) + mod(3)).astype(BF)
+        a2[ring_own(r)] = (n2 * (1.0 + mod(4)) + mod(3)).astype(BF)
 
     def mid_grad(r):
         rows = pl.ds(r, BLOCK)
@@ -719,7 +879,7 @@
     @step
     def gate_grad():
         def rows(r):
-            dm[own(r)] = (mod(5) * og_ref[pl.ds(r, BLOCK), :].astype(F32)).astype(BF)
+            dm[ring_own(r)] = (mod(5) * og_ref[pl.ds(r, BLOCK), :].astype(F32)).astype(BF)
 
         by_rows(rows)
 
@@ -763,19 +923,18 @@
             rhs = w[pl.ds(2 * j, 2), :, pl.ds(at, count)].reshape(768, count)
             dst[rows, pl.ds(pl.multiple_of(768 * j, 128), 768)] = nt(lhs[rows, :], rhs).astype(BF)
 
-    for key, dst, lhs, at, count in (
-        ("att", part, o, 1152, 384),
-        ("da2", part, gp, 1536, 1536),
-        ("da1", part, qkv, 0, 1152),
-        ("ffn", dm, act, 3072, 1536),
-    ):
+    for key, dst, lhs, at, count in (("att", part, o, 1152, 384), ("da1", part, qkv, 0, 1152)):
         steps[f"{key}_mm_other"] = functools.partial(back_half, dst, lhs, other_start, at, count)
         steps[f"{key}_mm_own"] = functools.partial(back_half, dst, lhs, own_start, at, count)
 
-    def hidden(start, half):
-        rows = rows_of(start, 256)
-
-        @pl.loop(3 * half, 3 * half + 3)
+    def quarter(name):
+        at_xh, at_xl = chip(STEPS[name])
+        return 512 * at_xh + 256 * at_xl
+
+    def hidden(name):
+        rows = rows_of(quarter(name), 256)
+
+        @pl.loop(0, 3)
         def _(j):
             at = pl.multiple_of(j * 256, 256)
             u = nn(a2[rows, :], weights(pl.multiple_of(1536 + at, 256), 256))
@@ -786,27 +945,32 @@
             slope = half + (0.5 * ROOT) * u * (1.0 - t * t) * (1.0 + (3 * 0.044715) * sq)
             gp[rows, pl.ds(at, 256)] = slope.astype(BF)
 
-    def hidden_grad(half):
-        @pl.loop(3 * half, 3 * half + 3)
+    def hidden_grad(name):
+        rows = rows_of(quarter(name), 256)
+
+        @pl.loop(0, 3)
         def _(j):
             at = pl.multiple_of(j * 256, 256)
             cols = pl.ds(at, 256)
-            dg = nn(dm[...], weights(pl.multiple_of(3072 + at, 256), 256))
-            gp[:, cols] = (gp[:, cols].astype(F32) * dg).astype(BF)
-
-    def grad(left, right, right_at, at, count):
-        @pl.loop(0, 4)
+            dg = nn(dm[rows, :], weights(pl.multiple_of(2304 + at, 256), 256))
+            gp[rows, cols] = (gp[rows, cols].astype(F32) * dg).astype(BF)
+
+    for name in STEPS:
+        steps[f"hidden_{name}"] = functools.partial(hidden, name)
+        steps[f"hgrad_{name}"] = functools.partial(hidden_grad, name)
+        steps[f"da2_mm_{name}"] = functools.partial(back_half, ring_part, gp, quarter(name), 1536, 768)
+        steps[f"ffn_mm_{name}"] = functools.partial(back_half, dm, act, quarter(name), 2304, 768)
+
+    def grad(left, right, right_at, at, count, planes=(0, 4)):
+        @pl.loop(*planes)
         def _(j):
             lhs = left[:, pl.ds(pl.multiple_of(384 * j, 128), 384)]
             value = tn(lhs, right[:, pl.ds(right_at, count)]) * scale
             g[j, :, pl.ds(at, count)] = value.astype(BF)
 
     for i in range(2):
-        steps[f"hidden_own_{i}"] = functools.partial(hidden, own_start, i)
-        steps[f"hidden_other_{i}"] = functools.partial(hidden, other_start, i)
-        steps[f"hidden_grad_{i}"] = functools.partial(hidden_grad, i)
-        steps[f"grad_in_{i}"] = functools.partial(grad, a2, gp, 768 * i, 1536 + 768 * i, 768)
-        steps[f"grad_back_{i}"] = functools.partial(grad, dm, act, 768 * i, 3072 + 768 * i, 768)
+        steps[f"grad_in_{i}"] = functools.partial(grad, a2, gp, 0, 1536, 768, (2 * i, 2 * i + 2))
+        steps[f"grad_back_{i}"] = functools.partial(grad, dm, act, 0, 2304, 768, (2 * i, 2 * i + 2))
     steps["grad_out"] = functools.partial(grad, da, o, 0, 1152, 384)
     steps["grad_q_0"] = functools.partial(grad, a1, qkv, 0, 0, 384)
     steps["grad_q_1"] = functools.partial(grad, a1, qkv, 384, 384, 768)
@@ -872,11 +1036,31 @@
             steps[name]()
 
 
+def finish_kernel(
+    final_in, ig_in, sums_in, final_out, ig_out, gq_out, go_out, gi_out, gb_out, final, ig, sums, sem
+):
+    cuts = [(384 * which, 384, gq_out.at[which]) for which in range(3)]
+    cuts += [(1152, 384, go_out), (1536, 1536, gi_out), (3072, 1536, gb_out)]
+    pairs = [(sums_in.at[:, pl.ds(at, n)], sums.at[:, pl.ds(at, n)], out) for at, n, out in cuts]
+    pairs += [(ig_in, ig, ig_out), (final_in, final, final_out)]
+    loads, stores = [], []
+    for i, (source, held, out) in enumerate(pairs):
+        loads.append(pltpu.make_async_copy(source, held, sem.at[0, i]))
+        stores.append(pltpu.make_async_copy(held, out, sem.at[1, i]))
+    for load in loads:
+        load.start()
+    for load, store in zip(loads, stores):
+        load.wait()
+        store.start()
+    for store in stores:
+        store.wait()
+
+
 def body(tokens, modulation, w_qkv, w_out, w_in, w_back, out_grad):
     own = w_qkv.shape[3]
     far = pl.BlockSpec(memory_space=pl.ANY)
-    copies = 34 * len(CHUNKS) + 40
-    rows = lambda n, dtype=BF: pltpu.VMEM((512, n), dtype)
+    copies = 34 * len(CHUNKS) + 2 * 6 + 2 * 4 + 2 * 14 + 2 * 10
+    rows = lambda n, count=512: pltpu.VMEM((count, n), BF)
     final, grad_in_rows, sums = pl.pallas_call(
         block_kernel,
         out_shape=(
@@ -888,28 +1072,33 @@
         out_specs=(far, far, far),
         scratch_shapes=[
             pltpu.VMEM((128, 1536), BF),
-            pltpu.VMEM((6, 1536), F32),
+            pltpu.VMEM((6, 1, 1536), F32),
             pltpu.VMEM((128, 1536), BF),
             pltpu.VMEM((128, 1536), BF),
             pltpu.VMEM((128, 1536), F32),
             pltpu.VMEM((48, WIDTH), F32),
-            pltpu.VMEM((4, 384, WIDTH), BF),
-            pltpu.VMEM((4, 384, WIDTH), BF),
-            pltpu.VMEM((48, WIDTH), BF),
-            rows(1536), rows(1536), rows(1536), rows(1536),
+            pltpu.VMEM((4, 384, HELD), BF),
+            pltpu.VMEM((4, 384, HELD), BF),
+            pltpu.VMEM((48, HELD), BF),
+            pltpu.VMEM((48, 1536), BF),
+            rows(1536), rows(1536, 1024), rows(1536, 1024), rows(1536),
             rows(1152), rows(384), rows(384),
-            rows(1536), rows(1536), rows(1536),
+            rows(768, 1024), rows(768, 1024), rows(1536), rows(1536, 1024),
             pltpu.VMEM((3, 512, 512), BF),
             pltpu.VMEM((2, 512, 128), BF),
             pltpu.VMEM((2, 128, 1536), BF),
             pltpu.VMEM((128, 1536), BF),
+            pltpu.VMEM((4, 128, 1536), BF),
+            pltpu.VMEM((2, 64, 1536), BF),
             pltpu.VMEM((2, 128, 1536), BF),
-            pltpu.VMEM((128, 1536), BF),
+            pltpu.VMEM((4, 128, 1536), BF),
+            pltpu.VMEM((2, 64, 1536), BF),
+            pltpu.VMEM((2, 128, 1536), BF),
             pltpu.VMEM((128, 1536), F32),
             pltpu.VMEM((128, 1536), F32),
             pltpu.SemaphoreType.DMA((copies,)),
             pltpu.SemaphoreType.DMA((copies,)),
-            pltpu.SemaphoreType.DMA((18,)),
+            pltpu.SemaphoreType.DMA((20,)),
             *scatter_buffers(),
         ],
         compiler_params=pltpu.CompilerParams(
@@ -918,21 +1107,35 @@
         name="block",
     )(
         tokens[0],
-        modulation[0, 0],
+        modulation[0].transpose(1, 0, 2),
         out_grad[0],
-        w_qkv[0].reshape(48, 3 * own),
+        w_qkv[0].transpose(1, 0, 2),
         w_out[0].T,
         w_in[0],
         w_back[0].T,
     )
-    return (
-        final[None],
-        grad_in_rows[None],
-        sums[:, :1152].reshape(1, 48, 3, own),
-        sums[:, 1152:1536].T[None],
-        sums[:, 1536:3072][None],
-        sums[:, 3072:].T[None],
-    )
+    outs = pl.pallas_call(
+        finish_kernel,
+        out_shape=(
+            jax.ShapeDtypeStruct((128, 1536), BF),
+            jax.ShapeDtypeStruct((128, 1536), F32),
+            jax.ShapeDtypeStruct((3, 48, own), F32),
+            jax.ShapeDtypeStruct((48, own), F32),
+            jax.ShapeDtypeStruct((48, 4 * own), F32),
+            jax.ShapeDtypeStruct((48, 4 * own), F32),
+        ),
+        in_specs=[far] * 3,
+        out_specs=(far,) * 6,
+        scratch_shapes=[
+            pltpu.VMEM((128, 1536), BF),
+            pltpu.VMEM((128, 1536), F32),
+            pltpu.VMEM((48, WIDTH), F32),
+            pltpu.SemaphoreType.DMA((2, 8)),
+        ],
+        name="finish",
+    )(final, grad_in_rows, sums)
+    final, grad_in_rows, gq, go, gi, gb = outs
+    return (final[None], grad_in_rows[None], gq.transpose(1, 0, 2)[None], go.T[None], gi[None], gb.T[None])
 
 
 def solution(mesh):

time: 184 us -> 155 us (0.84)
  Pallas kernels: 173 us -> 154 us
  local copies, waits for them, and re-layouts: 10 us -> 0 us
    pallas_call x1, Pallas kernels: 173 us -> 151 us  [body(): pl.pallas_call(block_kernel, out_shape=(jax.ShapeDtypeStruct((128, 1536),...]
    unnamed x10 -> x0, local copies, waits for them, and re-layouts: 5.54 us -> none
    broadcast_in_dim x2 -> x0, local copies, waits for them, and re-layouts: 3.42 us -> none  [the longest x1 1.9 us: body(): sums[:, 3072:].T[None]]
    pallas_call x0 -> x1, Pallas kernels: none -> 2.62 us  [body(): pl.pallas_call(finish_kernel, out_shape=(jax.ShapeDtypeStruct((128, 1536)...]
where the time goes in v6:
time: 155 us; the launch traced here: 154 us
  Pallas kernels  154 us (99%)
    pallas_call x1, Pallas kernels, body(): pl.pallas_call(block_kernel, out_shape=(jax.ShapeDtypeStruct((128, 1536),...  151 us

profile of v6, /device:TPU:0, one launch (start us, length us, event | category | flops | bytes accessed | tf_op | source)
XLA Modules:
  0.0 154.4 jit_solution(5821601375374057591)
XLA Ops:
  0.6 151.0 %block.1 = (bf16[128,1536]{1,0:T(8,128)(2,1)}, f32[128,1536]{1,0:T(8,128)}, f32[48,4608]{1,0:T(8,128)}) custom-call(bf16[128,1536]{1,0:T(8,128)(2,1)} %bitcast.25, f32[6,1,1536]{2,1,0:T(1,128)} %bitcast.30, bf16[128,1536]{1,0:T(8,128)(2,1)} %bitcast.26, bf16[3,48,384]{2,1,0:T(8,128)(2,1)} %bitcast.29, bf16[48,384]{1,0:T(8,128)(2,1)} %bitcast.31, ...), custom_call_target="tpu_custom_call" | custom-call | tf_op jit(solution)/shard_map/block/pallas_call | solution.py:1064
  151.6 2.6 %finish.1 = (bf16[128,1536]{1,0:T(8,128)(2,1)}, f32[128,1536]{1,0:T(8,128)}, f32[3,48,384]{2,1,0:T(8,128)}, f32[48,384]{1,0:T(8,128)}, f32[48,1536]{1,0:T(8,128)}, /*index=5*/f32[48,1536]{1,0:T(8,128)}) custom-call(bf16[128,1536]{1,0:T(8,128)(2,1)} %get-tuple-element.15.final_in, f32[128,1536]{1,0:T(8,128)} %get-tuple-element.16.ig_in, ...), custom_call_target="tpu_custom_call" | custom-call | tf_op jit(solution)/shard_map/finish/pallas_call | solution.py:1117

commit v7 on v6

--- a/solution.py
+++ b/solution.py
@@ -20,7 +20,8 @@
 temper = 2.5
 VMEM_LIMIT = 67_000_000
 
-TILES = ((2, 1), (3, 3), (1, 2), (3, 3), (3, 3))
+TILES = ((2, 1), (1, 2), (2, 1), (1, 2), (3, 3), (3, 3))
+OUT, IN, BACK = 3, 4, 5
 
 
 def split_chunks():
@@ -40,174 +41,192 @@
 WIDTH = 4608
 ORDER = (
     "load_first",
+    "load_rest",
     "load_inputs",
+    "first_norm_0",
+    "gate_grad",
     "met",
+    "ag_s1_1",
+    "ag_s1_2",
     "ag_s1_0",
-    "first_norm_0",
-    "load_rest",
-    "gate_grad",
-    "ag_s1_2",
-    "ag_s1_1",
+    "ag_s1_3",
+    "a1_start_0",
+    "first_norm_1",
+    "ag_s1_5",
+    "ag_s2_1",
+    "a1_start_1",
+    "ag_s2_2",
     "ag_s2_0",
-    "first_norm_1",
-    "a1_start_0",
-    "ag_s2_2",
+    "ag_s2_3",
+    "ag_s2b_1",
+    "ag_s2b_2",
     "ag_s2b_0",
-    "ag_s2_1",
-    "ag_s2b_2",
-    "a1_start_1",
+    "ag_s2b_3",
+    "ag_s3_1",
     "ag_s3_0",
-    "ag_s2b_1",
+    "ag_s3_2",
+    "dm_start_1",
+    "a1_relay_0",
+    "dm_start_0",
+    "a1_relay_1",
     "ag_s1_4",
-    "dm_start_0",
-    "ag_s3_2",
-    "a1_relay_0",
-    "ag_s1_3",
-    "ag_s3_1",
-    "a1_own_half",
-    "ag_s3b_0",
-    "dm_start_1",
-    "a1_relay_1",
     "ag_s3b_1",
     "a1_done",
+    "ag_s3_3",
+    "ag_s3b_0",
+    "dm_own_half",
+    "a1_own_half",
+    "dm_relay_0",
     "ag_s3b_2",
-    "dm_relay_0",
-    "ag_s2_3",
+    "ag_done_1",
+    "project_1",
+    "ag_s3b_3",
+    "attend_1_other",
+    "ag_s2_4",
+    "ag_s2_5",
     "ag_done_0",
     "project_0",
-    "attend_0",
-    "ag_done_1",
-    "project_1",
-    "ag_s2_4",
+    "attend_0_other",
+    "attend_0_own",
     "ag_done_2",
-    "attend_other",
+    "project_2",
+    "attend_2_other",
+    "ag_done_3",
     "att_mm_other",
-    "ag_s2b_3",
     "att_other",
+    "dm_relay_far",
     "ag_s2b_4",
+    "attend_1_own",
+    "attend_2_own",
     "att_send",
-    "ag_s3_3",
-    "attend_own",
-    "dm_relay_far",
+    "ag_s2b_5",
     "att_mm_own",
+    "ag_s3_4",
+    "dm_relay_1",
     "att_own",
-    "dm_relay_1",
-    "dm_own_half",
-    "dm_done",
+    "ag_s3_5",
+    "att_release",
     "att_wait_0",
     "second_norm_0",
-    "ag_s3_4",
     "a2_start_0",
     "att_wait_1",
     "second_norm_1",
-    "ag_s3b_3",
+    "ag_s3b_4",
     "a2_start_1",
+    "dm_done",
+    "dm_release",
+    "a2_relay_0",
+    "ag_s3b_5",
     "a2_own_half",
-    "ag_s3b_4",
-    "a2_relay_0",
+    "dm_done_far",
     "a2_relay_1",
-    "ag_done_3",
+    "ag_done_4",
     "hidden_own",
     "a2_done",
     "hidden_next",
-    "dm_done_far",
-    "ag_done_4",
+    "hidden_prev",
+    "a2_relay_far",
+    "ag_done_5",
+    "hgrad_own",
     "hgrad_next",
-    "a2_relay_far",
-    "da2_mm_next",
     "a2_done_far",
-    "da2_give_next",
     "hidden_far",
     "hgrad_far",
     "da2_mm_far",
     "da2_give_far",
-    "hidden_prev",
-    "da2_take_far",
     "hgrad_prev",
     "da2_mm_prev",
+    "da2_give_prev",
+    "da2_take_far",
+    "grad_back_0",
+    "da2_mm_next",
+    "da2_give_next",
+    "grad_back_1",
+    "rs_r1_5",
+    "da2_take_prev",
     "da2_take_next",
-    "da2_give_prev",
-    "grad_back_1",
-    "da2_take_prev",
-    "grad_back_0",
-    "hgrad_own",
+    "grad_in_0",
+    "grad_in_1",
     "rs_r1_4",
     "da2_pass_on",
-    "grad_in_0",
-    "dm_release",
-    "att_release",
-    "grad_in_1",
-    "rs_r1_3",
     "da2_mm_own",
+    "ffn_mm_own",
+    "ffn_mm_prev",
+    "ffn_give_prev",
+    "rs_r1b_5",
+    "ffn_mm_far",
+    "ffn_mm_next",
     "da2_give_own",
     "rs_r1b_4",
-    "ffn_mm_prev",
     "da2_take_own",
     "da2_wait",
     "mid_grad_0",
     "da_start_0",
     "mid_grad_1",
-    "ffn_give_prev",
     "da_start_1",
-    "ffn_mm_own",
-    "ffn_mm_far",
+    "ffn_take_prev",
+    "ffn_give_next",
     "ffn_give_far",
-    "ffn_mm_next",
-    "ffn_take_far",
+    "rs_r2_5",
     "da_own_half",
-    "rs_r1b_3",
     "da_relay_0",
+    "ffn_give_own",
     "rs_r2_4",
+    "da_relay_1",
+    "ffn_take_next",
     "heads_own",
-    "ffn_give_next",
-    "da_relay_1",
+    "rs_r2b_5",
     "da_done",
     "grad_out",
-    "rs_r1_2",
-    "ffn_give_own",
+    "rs_r1_3",
     "heads_other",
-    "rs_r2_3",
     "rs_r2b_4",
-    "attend_back_1",
-    "rs_r1b_2",
-    "rs_r2b_3",
-    "grad_q_1",
-    "rs_r1_1",
     "attend_back_0",
-    "ffn_take_next",
     "grad_q_0",
     "rs_r1_0",
+    "ffn_take_far",
+    "attend_back_2",
+    "ffn_take_own",
+    "rs_r1b_3",
+    "grad_q_2",
+    "rs_r1_2",
+    "rs_r3_5",
+    "attend_back_1",
+    "grad_q_1",
     "da1_mm_other",
-    "ffn_take_own",
-    "ffn_take_prev",
+    "da1_other",
+    "rs_r3_4",
+    "rs_r1_1",
+    "rs_r1b_0",
+    "da1_mm_own",
+    "da1_send",
+    "rs_r1b_2",
+    "rs_done_5",
+    "ffn_pass_on",
+    "rs_r1b_1",
+    "rs_r2_0",
+    "da1_own",
+    "rs_r2_2",
+    "da1_wait_0",
+    "rs_r2_3",
+    "rs_r2_1",
+    "rs_r2b_0",
+    "rs_r2b_3",
+    "rs_r2b_2",
+    "rs_done_4",
+    "rs_r2b_1",
+    "rs_r3_0",
+    "da1_wait_1",
     "rs_r3_3",
-    "rs_r2_2",
-    "rs_r3_4",
-    "da1_other",
-    "rs_r1b_1",
-    "rs_r1b_0",
-    "ffn_pass_on",
-    "da1_send",
-    "rs_done_3",
-    "rs_r2_1",
-    "da1_mm_own",
-    "da1_own",
-    "rs_r2b_2",
-    "rs_r2_0",
-    "rs_r2b_1",
-    "rs_r2b_0",
+    "first_grad",
     "rs_r3_2",
-    "rs_r3_1",
-    "rs_done_4",
-    "da1_wait_0",
     "ffn_wait",
     "last_out",
-    "rs_r3_0",
+    "rs_r3_1",
     "rs_done_2",
-    "da1_wait_1",
-    "first_grad",
+    "rs_done_3",
+    "rs_done_0",
     "rs_done_1",
-    "rs_done_0",
     "finish",
 )
 
@@ -300,7 +319,7 @@
     def s1(self, k):
         (a0, an), (b0, bn) = CHUNKS[k]
         part = self.w.at[self.z, rows_of(96 * self.y + 48 * self.xh, 48), pl.ds(a0, an + bn)]
-        source = part if k < 3 else self.stage.at[:, pl.ds(a0 - 1536, an + bn)]
+        source = part if k < IN else self.stage.at[:, pl.ds(a0 - 1536, an + bn)]
         self.one[k] = self.wires.go(source, part, turn("xh", 1, 2))
 
     def s2(self, k):
@@ -469,13 +488,13 @@
         cols = pl.ds(a0, an + bn)
         own = self.g[self.z, rows_of(96 * self.y + 48 * self.xh, 48), cols].astype(F32)
         came = self.last[:, cols].astype(F32)
-        if k >= 3:
-            base = 1536 * (k - 2)
+        if k >= IN:
+            base = 1536 * (k - OUT)
             self.out[:, pl.ds(pl.multiple_of(base + 768 * self.xh, 128), 768)] = own
             self.out[:, pl.ds(pl.multiple_of(base + 768 * (1 - self.xh), 128), 768)] = came
             return
         total = own + came
-        if k == 2:
+        if k == OUT:
             self.out[:, cols] = total
             return
         for at in range(0, an + bn, 128):
@@ -732,9 +751,8 @@
 
 
 def by_rows(fn, start=0, count=128):
-    @pl.loop(start // BLOCK, (start + count) // BLOCK)
-    def _(i):
-        fn(pl.multiple_of(i * BLOCK, BLOCK))
+    for r in range(start, start + count, BLOCK):
+        fn(r)
 
 
 def block_kernel(
@@ -889,39 +907,31 @@
     def project(start, count):
         qkv[:, pl.ds(start, count)] = nn(a1[...], weights(start, count)).astype(BF)
 
-    @step
-    def project_0():
-        project(0, 256)
-        project(256, 128)
-
-    @step
-    def project_1():
-        @pl.loop(0, 3)
-        def _(j):
-            project(pl.multiple_of(384 + j * 256, 128), 256)
-
-    def attend(heads, start, blocks):
-        @pl.loop(0, blocks)
-        def _(i):
-            rows = rows_of(start + i * 128, 128)
-            for h in heads:
-                s = nt(qkv[rows, lanes(h, 0)], qkv[:, lanes(h, 1)]) * factor
-                e = jnp.exp(s - jnp.max(s, axis=-1, keepdims=True))
-                p = (e * (1.0 / jnp.sum(e, axis=-1, keepdims=True))).astype(BF)
-                probs[h, rows, :] = p
-                o[rows, pl.ds(128 * h, 128)] = nn(p, qkv[:, lanes(h, 2)]).astype(BF)
-
-    steps["attend_0"] = functools.partial(attend, (0,), 0, 4)
-    steps["attend_other"] = functools.partial(attend, (1, 2), other_start, 2)
-    steps["attend_own"] = functools.partial(attend, (1, 2), own_start, 2)
+    for h in range(3):
+
+        def project_head(h=h):
+            project(384 * h, 384)
+
+        steps[f"project_{h}"] = project_head
+
+    def attend(h, start):
+        rows = rows_of(start, 256)
+        s = nt(qkv[rows, lanes(h, 0)], qkv[:, lanes(h, 1)])
+        e = jnp.exp(factor * (s - jnp.max(s, axis=-1, keepdims=True)))
+        p = (e * (1.0 / jnp.sum(e, axis=-1, keepdims=True))).astype(BF)
+        probs[h, rows, :] = p
+        o[rows, pl.ds(128 * h, 128)] = nn(p, qkv[:, lanes(h, 2)]).astype(BF)
+
+    for h in range(3):
+        steps[f"attend_{h}_other"] = functools.partial(attend, h, other_start)
+        steps[f"attend_{h}_own"] = functools.partial(attend, h, own_start)
 
     def back_half(dst, lhs, start, at, count):
         rows = rows_of(start, 256)
 
-        @pl.loop(0, 2)
-        def _(j):
-            rhs = w[pl.ds(2 * j, 2), :, pl.ds(at, count)].reshape(768, count)
-            dst[rows, pl.ds(pl.multiple_of(768 * j, 128), 768)] = nt(lhs[rows, :], rhs).astype(BF)
+        for j in range(2):
+            rhs = w[2 * j : 2 * j + 2, :, pl.ds(at, count)].reshape(768, count)
+            dst[rows, pl.ds(768 * j, 768)] = nt(lhs[rows, :], rhs).astype(BF)
 
     for key, dst, lhs, at, count in (("att", part, o, 1152, 384), ("da1", part, qkv, 0, 1152)):
         steps[f"{key}_mm_other"] = functools.partial(back_half, dst, lhs, other_start, at, count)
@@ -934,25 +944,21 @@
     def hidden(name):
         rows = rows_of(quarter(name), 256)
 
-        @pl.loop(0, 3)
-        def _(j):
-            at = pl.multiple_of(j * 256, 256)
-            u = nn(a2[rows, :], weights(pl.multiple_of(1536 + at, 256), 256))
+        for at in range(0, 768, 256):
+            u = nn(a2[rows, :], weights(1536 + at, 256))
             sq = u * u
-            t = jnp.tanh(ROOT * u * (1.0 + 0.044715 * sq))
-            half = 0.5 * (1.0 + t)
+            t = jnp.tanh(u * (ROOT + (ROOT * 0.044715) * sq))
+            half = 0.5 + 0.5 * t
             act[rows, pl.ds(at, 256)] = (u * half).astype(BF)
-            slope = half + (0.5 * ROOT) * u * (1.0 - t * t) * (1.0 + (3 * 0.044715) * sq)
-            gp[rows, pl.ds(at, 256)] = slope.astype(BF)
+            inner = (0.5 * ROOT) + (1.5 * ROOT * 0.044715) * sq
+            gp[rows, pl.ds(at, 256)] = (half + u * inner * (1.0 - t * t)).astype(BF)
 
     def hidden_grad(name):
         rows = rows_of(quarter(name), 256)
 
-        @pl.loop(0, 3)
-        def _(j):
-            at = pl.multiple_of(j * 256, 256)
+        for at in range(0, 768, 256):
             cols = pl.ds(at, 256)
-            dg = nn(dm[rows, :], weights(pl.multiple_of(2304 + at, 256), 256))
+            dg = nn(dm[rows, :], weights(2304 + at, 256))
             gp[rows, cols] = (gp[rows, cols].astype(F32) * dg).astype(BF)
 
     for name in STEPS:
@@ -962,9 +968,8 @@
         steps[f"ffn_mm_{name}"] = functools.partial(back_half, dm, act, quarter(name), 2304, 768)
 
     def grad(left, right, right_at, at, count, planes=(0, 4)):
-        @pl.loop(*planes)
-        def _(j):
-            lhs = left[:, pl.ds(pl.multiple_of(384 * j, 128), 384)]
+        for j in range(*planes):
+            lhs = left[:, pl.ds(384 * j, 384)]
             value = tn(lhs, right[:, pl.ds(right_at, count)]) * scale
             g[j, :, pl.ds(at, count)] = value.astype(BF)
 
@@ -972,8 +977,8 @@
         steps[f"grad_in_{i}"] = functools.partial(grad, a2, gp, 0, 1536, 768, (2 * i, 2 * i + 2))
         steps[f"grad_back_{i}"] = functools.partial(grad, dm, act, 0, 2304, 768, (2 * i, 2 * i + 2))
     steps["grad_out"] = functools.partial(grad, da, o, 0, 1152, 384)
-    steps["grad_q_0"] = functools.partial(grad, a1, qkv, 0, 0, 384)
-    steps["grad_q_1"] = functools.partial(grad, a1, qkv, 384, 384, 768)
+    for h in range(3):
+        steps[f"grad_q_{h}"] = functools.partial(grad, a1, qkv, 384 * h, 384 * h, 384)
 
     def head_grads(start):
         rows = rows_of(start, 256)
@@ -982,27 +987,21 @@
     steps["heads_own"] = functools.partial(head_grads, own_start)
     steps["heads_other"] = functools.partial(head_grads, other_start)
 
-    def attend_back(heads):
-        for n, h in enumerate(heads):
-            dv[n] = tn(probs[h], do[:, pl.ds(128 * h, 128)]).astype(BF)
-
-        @pl.loop(0, 4)
-        def _(i):
-            rows = pl.ds(pl.multiple_of(i * 128, 128), 128)
-            for h in heads:
-                dp = nt(do[rows, pl.ds(128 * h, 128)], qkv[:, lanes(h, 2)])
-                p = probs[h, rows, :].astype(F32)
-                ds = factor * p * (dp - jnp.sum(p * dp, axis=-1, keepdims=True))
-                probs[h, rows, :] = ds.astype(BF)
-
-        for n, h in enumerate(heads):
-            dk = tn(probs[h], qkv[:, lanes(h, 0)]).astype(BF)
-            qkv[:, lanes(h, 0)] = nn(probs[h], qkv[:, lanes(h, 1)]).astype(BF)
-            qkv[:, lanes(h, 1)] = dk
-            qkv[:, lanes(h, 2)] = dv[n]
-
-    steps["attend_back_0"] = functools.partial(attend_back, (0,))
-    steps["attend_back_1"] = functools.partial(attend_back, (1, 2))
+    def attend_back(h):
+        dv[...] = tn(probs[h], do[:, pl.ds(128 * h, 128)]).astype(BF)
+        for i in range(4):
+            rows = pl.ds(i * 128, 128)
+            dp = nt(do[rows, pl.ds(128 * h, 128)], qkv[:, lanes(h, 2)])
+            p = probs[h, rows, :].astype(F32)
+            ds = factor * p * (dp - jnp.sum(p * dp, axis=-1, keepdims=True))
+            probs[h, rows, :] = ds.astype(BF)
+        dk = tn(probs[h], qkv[:, lanes(h, 0)]).astype(BF)
+        qkv[:, lanes(h, 0)] = nn(probs[h], qkv[:, lanes(h, 1)]).astype(BF)
+        qkv[:, lanes(h, 1)] = dk
+        qkv[:, lanes(h, 2)] = dv[...]
+
+    for h in range(3):
+        steps[f"attend_back_{h}"] = functools.partial(attend_back, h)
 
     @step
     def last_out():
@@ -1085,7 +1084,7 @@
             rows(1152), rows(384), rows(384),
             rows(768, 1024), rows(768, 1024), rows(1536), rows(1536, 1024),
             pltpu.VMEM((3, 512, 512), BF),
-            pltpu.VMEM((2, 512, 128), BF),
+            pltpu.VMEM((512, 128), BF),
             pltpu.VMEM((2, 128, 1536), BF),
             pltpu.VMEM((128, 1536), BF),
             pltpu.VMEM((4, 128, 1536), BF),

time: 155 us -> 147 us (0.948)
  Pallas kernels: 154 us -> 146 us
    pallas_call x1, Pallas kernels: 151 us -> 144 us  [body(): pl.pallas_call(block_kernel, out_shape=(jax.ShapeDtypeStruct((128, 1536),...]
where the time goes in v7:
time: 147 us
  Pallas kernels  146 us (99%)
    pallas_call x1, Pallas kernels, body(): pl.pallas_call(block_kernel, out_shape=(jax.ShapeDtypeStruct((128, 1536),...  144 us

profile of v7, /device:TPU:0, one launch (start us, length us, event | category | flops | bytes accessed | tf_op | source)
XLA Modules:
  0.0 147.3 jit_solution(13855684731790605830)
XLA Ops:
  0.6 143.8 %block.1 = (bf16[128,1536]{1,0:T(8,128)(2,1)}, f32[128,1536]{1,0:T(8,128)}, f32[48,4608]{1,0:T(8,128)}) custom-call(bf16[128,1536]{1,0:T(8,128)(2,1)} %bitcast.25, f32[6,1,1536]{2,1,0:T(1,128)} %bitcast.30, bf16[128,1536]{1,0:T(8,128)(2,1)} %bitcast.26, bf16[3,48,384]{2,1,0:T(8,128)(2,1)} %bitcast.29, bf16[48,384]{1,0:T(8,128)(2,1)} %bitcast.31, ...), custom_call_target="tpu_custom_call" | custom-call | tf_op jit(solution)/shard_map/block/pallas_call | solution.py:1063
  144.4 2.6 %finish.1 = (bf16[128,1536]{1,0:T(8,128)(2,1)}, f32[128,1536]{1,0:T(8,128)}, f32[3,48,384]{2,1,0:T(8,128)}, f32[48,384]{1,0:T(8,128)}, f32[48,1536]{1,0:T(8,128)}, /*index=5*/f32[48,1536]{1,0:T(8,128)}) custom-call(bf16[128,1536]{1,0:T(8,128)(2,1)} %get-tuple-element.15.final_in, f32[128,1536]{1,0:T(8,128)} %get-tuple-element.16.ig_in, ...), custom_call_target="tpu_custom_call" | custom-call | tf_op jit(solution)/shard_map/finish/pallas_call | solution.py:1116

commit v8 on v7

--- a/solution.py
+++ b/solution.py
@@ -18,7 +18,7 @@
 
 ln_eps = 1e-06
 temper = 2.5
-VMEM_LIMIT = 67_000_000
+VMEM_LIMIT = 64_500_000
 
 TILES = ((2, 1), (1, 2), (2, 1), (1, 2), (3, 3), (3, 3))
 OUT, IN, BACK = 3, 4, 5
@@ -40,194 +40,38 @@
 STEPS = {"own": 0, "next": 1, "prev": -1, "far": 2}
 WIDTH = 4608
 ORDER = (
-    "load_first",
-    "load_rest",
-    "load_inputs",
-    "first_norm_0",
-    "gate_grad",
-    "met",
-    "ag_s1_1",
-    "ag_s1_2",
-    "ag_s1_0",
-    "ag_s1_3",
-    "a1_start_0",
-    "first_norm_1",
-    "ag_s1_5",
-    "ag_s2_1",
-    "a1_start_1",
-    "ag_s2_2",
-    "ag_s2_0",
-    "ag_s2_3",
-    "ag_s2b_1",
-    "ag_s2b_2",
-    "ag_s2b_0",
-    "ag_s2b_3",
-    "ag_s3_1",
-    "ag_s3_0",
-    "ag_s3_2",
-    "dm_start_1",
-    "a1_relay_0",
-    "dm_start_0",
-    "a1_relay_1",
-    "ag_s1_4",
-    "ag_s3b_1",
-    "a1_done",
-    "ag_s3_3",
-    "ag_s3b_0",
-    "dm_own_half",
-    "a1_own_half",
-    "dm_relay_0",
-    "ag_s3b_2",
-    "ag_done_1",
-    "project_1",
-    "ag_s3b_3",
-    "attend_1_other",
-    "ag_s2_4",
-    "ag_s2_5",
-    "ag_done_0",
-    "project_0",
-    "attend_0_other",
-    "attend_0_own",
-    "ag_done_2",
-    "project_2",
-    "attend_2_other",
-    "ag_done_3",
-    "att_mm_other",
-    "att_other",
-    "dm_relay_far",
-    "ag_s2b_4",
-    "attend_1_own",
-    "attend_2_own",
-    "att_send",
-    "ag_s2b_5",
-    "att_mm_own",
-    "ag_s3_4",
-    "dm_relay_1",
-    "att_own",
-    "ag_s3_5",
-    "att_release",
-    "att_wait_0",
-    "second_norm_0",
-    "a2_start_0",
-    "att_wait_1",
-    "second_norm_1",
-    "ag_s3b_4",
-    "a2_start_1",
-    "dm_done",
-    "dm_release",
-    "a2_relay_0",
-    "ag_s3b_5",
-    "a2_own_half",
-    "dm_done_far",
-    "a2_relay_1",
-    "ag_done_4",
-    "hidden_own",
-    "a2_done",
-    "hidden_next",
-    "hidden_prev",
-    "a2_relay_far",
-    "ag_done_5",
-    "hgrad_own",
-    "hgrad_next",
-    "a2_done_far",
-    "hidden_far",
-    "hgrad_far",
-    "da2_mm_far",
-    "da2_give_far",
-    "hgrad_prev",
-    "da2_mm_prev",
-    "da2_give_prev",
-    "da2_take_far",
-    "grad_back_0",
-    "da2_mm_next",
-    "da2_give_next",
-    "grad_back_1",
-    "rs_r1_5",
-    "da2_take_prev",
-    "da2_take_next",
-    "grad_in_0",
-    "grad_in_1",
-    "rs_r1_4",
-    "da2_pass_on",
-    "da2_mm_own",
-    "ffn_mm_own",
-    "ffn_mm_prev",
-    "ffn_give_prev",
-    "rs_r1b_5",
-    "ffn_mm_far",
-    "ffn_mm_next",
-    "da2_give_own",
-    "rs_r1b_4",
-    "da2_take_own",
-    "da2_wait",
-    "mid_grad_0",
-    "da_start_0",
-    "mid_grad_1",
-    "da_start_1",
-    "ffn_take_prev",
-    "ffn_give_next",
-    "ffn_give_far",
-    "rs_r2_5",
-    "da_own_half",
-    "da_relay_0",
-    "ffn_give_own",
-    "rs_r2_4",
-    "da_relay_1",
-    "ffn_take_next",
-    "heads_own",
-    "rs_r2b_5",
-    "da_done",
-    "grad_out",
-    "rs_r1_3",
-    "heads_other",
-    "rs_r2b_4",
-    "attend_back_0",
-    "grad_q_0",
-    "rs_r1_0",
-    "ffn_take_far",
-    "attend_back_2",
-    "ffn_take_own",
-    "rs_r1b_3",
-    "grad_q_2",
-    "rs_r1_2",
-    "rs_r3_5",
-    "attend_back_1",
-    "grad_q_1",
-    "da1_mm_other",
-    "da1_other",
-    "rs_r3_4",
-    "rs_r1_1",
-    "rs_r1b_0",
-    "da1_mm_own",
-    "da1_send",
-    "rs_r1b_2",
-    "rs_done_5",
-    "ffn_pass_on",
-    "rs_r1b_1",
-    "rs_r2_0",
-    "da1_own",
-    "rs_r2_2",
-    "da1_wait_0",
-    "rs_r2_3",
-    "rs_r2_1",
-    "rs_r2b_0",
-    "rs_r2b_3",
-    "rs_r2b_2",
-    "rs_done_4",
-    "rs_r2b_1",
-    "rs_r3_0",
-    "da1_wait_1",
-    "rs_r3_3",
-    "first_grad",
-    "rs_r3_2",
-    "ffn_wait",
-    "last_out",
-    "rs_r3_1",
-    "rs_done_2",
-    "rs_done_3",
-    "rs_done_0",
-    "rs_done_1",
-    "finish",
+    134, 137, 136, 135, 36, 24,
+    144, 12, 0, 86, 37, 141,
+    25, 13, 1, 138, 72, 74,
+    38, 26, 48, 76, 14, 2,
+    39, 15, 73, 3, 84, 75,
+    77, 60, 27, 16, 4, 28,
+    40, 49, 61, 85, 17, 146,
+    150, 5, 145, 148, 29, 147,
+    41, 152, 154, 102, 50, 89,
+    153, 149, 62, 104, 51, 151,
+    87, 63, 155, 88, 103, 106,
+    139, 93, 91, 107, 142, 95,
+    52, 90, 105, 94, 98, 64,
+    96, 53, 158, 99, 162, 166,
+    97, 65, 167, 100, 170, 171,
+    172, 120, 163, 164, 121, 168,
+    118, 116, 175, 177, 117, 66,
+    119, 159, 174, 176, 54, 122,
+    160, 114, 92, 169, 128, 67,
+    115, 161, 165, 124, 129, 126,
+    123, 140, 78, 55, 143, 80,
+    125, 127, 68, 173, 82, 130,
+    131, 79, 182, 81, 56, 83,
+    178, 42, 183, 69, 186, 181,
+    30, 184, 179, 6, 43, 185,
+    180, 18, 70, 156, 132, 31,
+    157, 7, 19, 44, 108, 32,
+    110, 8, 57, 20, 45, 109,
+    9, 112, 33, 58, 21, 46,
+    113, 10, 133, 187, 34, 22,
+    188, 59, 11, 35, 71, 47,
+    23, 189,
 )
 
 
@@ -757,8 +601,8 @@
 
 def block_kernel(
     x_in, m_in, og_in, wq_ref, wo_ref, wi_ref, wb_ref,
-    final_out, ig_out, sums_out,
-    x_ref, m_ref, og_ref, final_ref, ig_ref, sums_ref,
+    final_ref, ig_ref, sums_ref,
+    x_ref, m_ref, og_ref,
     w, g, last, stage, a1, dm, a2, da, qkv, o, do, gp, act, part, ring_part, probs, dv, pair, cross,
     pair0, half0, full0, pair1, half1, full1, mid, dmid, send, recv, local_sem, *bufs,
 ):
@@ -784,12 +628,6 @@
         pltpu.make_async_copy(a, b, local_sem.at[12 + i])
         for i, (a, b) in enumerate(((x_in, x_ref), (m_in, m_ref), (og_in, og_ref)))
     ]
-    outputs = {
-        name: pltpu.make_async_copy(a, b, local_sem.at[15 + i])
-        for i, (name, a, b) in enumerate(
-            (("final", final_ref, final_out), ("ig", ig_ref, ig_out), ("sums", sums_ref, sums_out))
-        )
-    }
     greet()
     for load in loads[:3] + inputs[:2] + loads[3:] + inputs[2:]:
         load.start()
@@ -1010,7 +848,6 @@
             final_ref[rows, :] = (mid[rows, :] + mod(5) * reds["ffn"].rows(r, BLOCK)).astype(BF)
 
         by_rows(each)
-        outputs["final"].start()
 
     @step
     def first_grad():
@@ -1021,35 +858,24 @@
             ig_ref[rows, :] = dmid[rows, :] + inner
 
         by_rows(each)
-        outputs["ig"].start()
 
     @step
     def finish():
-        outputs["sums"].start()
         wires.drain()
-        for copy in outputs.values():
-            copy.wait()
-
-    for name in ORDER:
-        with jax.named_scope(name):
-            steps[name]()
-
-
-def finish_kernel(
-    final_in, ig_in, sums_in, final_out, ig_out, gq_out, go_out, gi_out, gb_out, final, ig, sums, sem
-):
+
+    names = list(steps)
+    for at in ORDER:
+        with jax.named_scope(names[at]):
+            steps[names[at]]()
+
+
+def finish_kernel(final, ig, sums, final_out, ig_out, gq_out, go_out, gi_out, gb_out, sem):
     cuts = [(384 * which, 384, gq_out.at[which]) for which in range(3)]
     cuts += [(1152, 384, go_out), (1536, 1536, gi_out), (3072, 1536, gb_out)]
-    pairs = [(sums_in.at[:, pl.ds(at, n)], sums.at[:, pl.ds(at, n)], out) for at, n, out in cuts]
-    pairs += [(ig_in, ig, ig_out), (final_in, final, final_out)]
-    loads, stores = [], []
-    for i, (source, held, out) in enumerate(pairs):
-        loads.append(pltpu.make_async_copy(source, held, sem.at[0, i]))
-        stores.append(pltpu.make_async_copy(held, out, sem.at[1, i]))
-    for load in loads:
-        load.start()
-    for load, store in zip(loads, stores):
-        load.wait()
+    pairs = [(sums.at[:, pl.ds(at, n)], out) for at, n, out in cuts]
+    pairs += [(ig, ig_out), (final, final_out)]
+    stores = [pltpu.make_async_copy(held, out, sem.at[i]) for i, (held, out) in enumerate(pairs)]
+    for store in stores:
         store.start()
     for store in stores:
         store.wait()
@@ -1058,24 +884,22 @@
 def body(tokens, modulation, w_qkv, w_out, w_in, w_back, out_grad):
     own = w_qkv.shape[3]
     far = pl.BlockSpec(memory_space=pl.ANY)
+    near_memory = pl.BlockSpec(memory_space=pltpu.VMEM)
     copies = 34 * len(CHUNKS) + 2 * 6 + 2 * 4 + 2 * 14 + 2 * 10
     rows = lambda n, count=512: pltpu.VMEM((count, n), BF)
     final, grad_in_rows, sums = pl.pallas_call(
         block_kernel,
         out_shape=(
-            jax.ShapeDtypeStruct((128, 1536), BF),
-            jax.ShapeDtypeStruct((128, 1536), F32),
-            jax.ShapeDtypeStruct((48, WIDTH), F32),
+            pltpu.VMEM((128, 1536), BF),
+            pltpu.VMEM((128, 1536), F32),
+            pltpu.VMEM((48, WIDTH), F32),
         ),
         in_specs=[far] * 7,
-        out_specs=(far, far, far),
+        out_specs=(near_memory,) * 3,
         scratch_shapes=[
             pltpu.VMEM((128, 1536), BF),
             pltpu.VMEM((6, 1, 1536), F32),
             pltpu.VMEM((128, 1536), BF),
-            pltpu.VMEM((128, 1536), BF),
-            pltpu.VMEM((128, 1536), F32),
-            pltpu.VMEM((48, WIDTH), F32),
             pltpu.VMEM((4, 384, HELD), BF),
             pltpu.VMEM((4, 384, HELD), BF),
             pltpu.VMEM((48, HELD), BF),
@@ -1123,16 +947,11 @@
             jax.ShapeDtypeStruct((48, 4 * own), F32),
             jax.ShapeDtypeStruct((48, 4 * own), F32),
         ),
-        in_specs=[far] * 3,
+        in_specs=[near_memory] * 3,
         out_specs=(far,) * 6,
-        scratch_shapes=[
-            pltpu.VMEM((128, 1536), BF),
-            pltpu.VMEM((128, 1536), F32),
-            pltpu.VMEM((48, WIDTH), F32),
-            pltpu.SemaphoreType.DMA((2, 8)),
-        ],
+        scratch_shapes=[pltpu.SemaphoreType.DMA((8,))],
         name="finish",
-    )(final, grad_in_rows, sums)
+    )(*(pltpu.with_memory_space_constraint(held, pltpu.VMEM) for held in (final, grad_in_rows, sums)))
     final, grad_in_rows, gq, go, gi, gb = outs
     return (final[None], grad_in_rows[None], gq.transpose(1, 0, 2)[None], go.T[None], gi[None], gb.T[None])
 

time: 147 us -> 146 us (level)
  no operation moved by 1% of the time
where the time goes in v8:
time: 146 us
  Pallas kernels  145 us (99%)
    pallas_call x1, Pallas kernels, body(): pl.pallas_call(block_kernel, out_shape=(pltpu.VMEM((128, 1536), BF), pltp...  143 us

profile of v8, /device:TPU:0, one launch (start us, length us, event | category | flops | bytes accessed | tf_op | source)
XLA Modules:
  0.0 145.6 jit_solution(4430514536194281272)
XLA Ops:
  0.6 143.4 %block.1 = (bf16[128,1536]{1,0:T(8,128)(2,1)S(1)}, f32[128,1536]{1,0:T(8,128)S(1)}, f32[48,4608]{1,0:T(8,128)S(1)}) custom-call(bf16[128,1536]{1,0:T(8,128)(2,1)} %bitcast.25, f32[6,1,1536]{2,1,0:T(1,128)} %bitcast.30, bf16[128,1536]{1,0:T(8,128)(2,1)} %bitcast.26, bf16[3,48,384]{2,1,0:T(8,128)(2,1)} %bitcast.29, bf16[48,384]{1,0:T(8,128)(2,1)} %bitcast.31, ...), custom_call_target="tpu_custom_call" | custom-call | tf_op jit(solution)/shard_map/block/pallas_call | solution.py:890
  144.1 1.4 finish.1

commit v9 on v8

--- a/solution.py
+++ b/solution.py
@@ -40,38 +40,38 @@
 STEPS = {"own": 0, "next": 1, "prev": -1, "far": 2}
 WIDTH = 4608
 ORDER = (
-    134, 137, 136, 135, 36, 24,
-    144, 12, 0, 86, 37, 141,
-    25, 13, 1, 138, 72, 74,
-    38, 26, 48, 76, 14, 2,
-    39, 15, 73, 3, 84, 75,
-    77, 60, 27, 16, 4, 28,
-    40, 49, 61, 85, 17, 146,
-    150, 5, 145, 148, 29, 147,
-    41, 152, 154, 102, 50, 89,
-    153, 149, 62, 104, 51, 151,
-    87, 63, 155, 88, 103, 106,
-    139, 93, 91, 107, 142, 95,
-    52, 90, 105, 94, 98, 64,
-    96, 53, 158, 99, 162, 166,
+    134, 137, 135, 12, 0, 24,
+    136, 36, 48, 138, 72, 141,
+    144, 74, 13, 86, 84, 1,
+    25, 37, 14, 76, 89, 49,
+    60, 2, 26, 38, 15, 3,
+    73, 75, 27, 39, 4, 16,
+    28, 40, 85, 87, 50, 77,
+    61, 5, 145, 148, 17, 146,
+    150, 29, 147, 152, 41, 154,
+    102, 90, 151, 88, 62, 149,
+    104, 51, 153, 155, 91, 103,
+    63, 92, 106, 139, 93, 52,
+    107, 142, 95, 64, 94, 96,
+    53, 98, 158, 99, 166, 162,
     97, 65, 167, 100, 170, 171,
-    172, 120, 163, 164, 121, 168,
-    118, 116, 175, 177, 117, 66,
-    119, 159, 174, 176, 54, 122,
-    160, 114, 92, 169, 128, 67,
-    115, 161, 165, 124, 129, 126,
-    123, 140, 78, 55, 143, 80,
-    125, 127, 68, 173, 82, 130,
-    131, 79, 182, 81, 56, 83,
-    178, 42, 183, 69, 186, 181,
-    30, 184, 179, 6, 43, 185,
-    180, 18, 70, 156, 132, 31,
-    157, 7, 19, 44, 108, 32,
-    110, 8, 57, 20, 45, 109,
-    9, 112, 33, 58, 21, 46,
-    113, 10, 133, 187, 34, 22,
-    188, 59, 11, 35, 71, 47,
-    23, 189,
+    172, 120, 163, 164, 121, 116,
+    168, 118, 175, 177, 66, 119,
+    117, 159, 105, 176, 174, 54,
+    122, 160, 114, 67, 173, 165,
+    130, 169, 161, 124, 115, 123,
+    140, 78, 143, 80, 128, 125,
+    55, 68, 129, 82, 126, 131,
+    182, 127, 79, 81, 56, 69,
+    83, 178, 42, 183, 186, 181,
+    30, 185, 180, 18, 184, 43,
+    179, 6, 31, 156, 70, 132,
+    157, 108, 110, 19, 7, 44,
+    32, 109, 20, 133, 187, 57,
+    112, 71, 8, 33, 45, 113,
+    21, 58, 9, 188, 34, 46,
+    22, 10, 23, 35, 47, 59,
+    11, 189,
 )
 
 

time: 146 us -> 143 us (0.979)
  Pallas kernels: 145 us -> 142 us
    pallas_call x1, Pallas kernels: 143 us -> 141 us  [body(): pl.pallas_call(block_kernel, out_shape=(pltpu.VMEM((128, 1536), BF), pltp...]
where the time goes in v9:
time: 143 us
  Pallas kernels  142 us (99%)
    pallas_call x1, Pallas kernels, body(): pl.pallas_call(block_kernel, out_shape=(pltpu.VMEM((128, 1536), BF), pltp...  141 us

profile of v9, /device:TPU:0, one launch (start us, length us, event | category | flops | bytes accessed | tf_op | source)
XLA Modules:
  0.0 142.9 jit_solution(1731639073608477081)
XLA Ops:
  0.6 140.7 %block.1 = (bf16[128,1536]{1,0:T(8,128)(2,1)S(1)}, f32[128,1536]{1,0:T(8,128)S(1)}, f32[48,4608]{1,0:T(8,128)S(1)}) custom-call(bf16[128,1536]{1,0:T(8,128)(2,1)} %bitcast.25, f32[6,1,1536]{2,1,0:T(1,128)} %bitcast.30, bf16[128,1536]{1,0:T(8,128)(2,1)} %bitcast.26, bf16[3,48,384]{2,1,0:T(8,128)(2,1)} %bitcast.29, bf16[48,384]{1,0:T(8,128)(2,1)} %bitcast.31, ...), custom_call_target="tpu_custom_call" | custom-call | tf_op jit(solution)/shard_map/block/pallas_call | solution.py:890
  141.3 1.4 finish.1

commit v10 on v9

--- a/solution.py
+++ b/solution.py
@@ -40,37 +40,37 @@
 STEPS = {"own": 0, "next": 1, "prev": -1, "far": 2}
 WIDTH = 4608
 ORDER = (
-    134, 137, 135, 12, 0, 24,
-    136, 36, 48, 138, 72, 141,
-    144, 74, 13, 86, 84, 1,
-    25, 37, 14, 76, 89, 49,
-    60, 2, 26, 38, 15, 3,
-    73, 75, 27, 39, 4, 16,
-    28, 40, 85, 87, 50, 77,
-    61, 5, 145, 148, 17, 146,
-    150, 29, 147, 152, 41, 154,
-    102, 90, 151, 88, 62, 149,
-    104, 51, 153, 155, 91, 103,
-    63, 92, 106, 139, 93, 52,
-    107, 142, 95, 64, 94, 96,
-    53, 98, 158, 99, 166, 162,
-    97, 65, 167, 100, 170, 171,
-    172, 120, 163, 164, 121, 116,
-    168, 118, 175, 177, 66, 119,
-    117, 159, 105, 176, 174, 54,
-    122, 160, 114, 67, 173, 165,
-    130, 169, 161, 124, 115, 123,
-    140, 78, 143, 80, 128, 125,
-    55, 68, 129, 82, 126, 131,
-    182, 127, 79, 81, 56, 69,
-    83, 178, 42, 183, 186, 181,
+    134, 137, 136, 141, 144, 135,
+    0, 12, 36, 24, 138, 48,
+    84, 86, 72, 74, 60, 1,
+    76, 13, 37, 25, 2, 49,
+    14, 89, 38, 26, 3, 15,
+    27, 85, 87, 39, 73, 16,
+    90, 4, 28, 75, 40, 61,
+    88, 77, 50, 17, 146, 150,
+    5, 145, 148, 29, 147, 41,
+    152, 154, 102, 149, 62, 153,
+    91, 51, 104, 151, 63, 155,
+    103, 106, 139, 93, 52, 107,
+    142, 95, 98, 64, 92, 94,
+    105, 53, 96, 158, 99, 162,
+    65, 166, 97, 163, 100, 170,
+    171, 172, 120, 167, 168, 118,
+    121, 164, 116, 175, 119, 177,
+    66, 117, 159, 176, 174, 54,
+    122, 165, 126, 160, 114, 161,
+    124, 67, 173, 130, 169, 128,
+    115, 123, 140, 125, 78, 143,
+    80, 129, 127, 131, 55, 82,
+    182, 68, 79, 81, 56, 69,
+    83, 178, 183, 42, 186, 181,
     30, 185, 180, 18, 184, 43,
-    179, 6, 31, 156, 70, 132,
-    157, 108, 110, 19, 7, 44,
-    32, 109, 20, 133, 187, 57,
-    112, 71, 8, 33, 45, 113,
-    21, 58, 9, 188, 34, 46,
-    22, 10, 23, 35, 47, 59,
+    70, 179, 6, 132, 156, 108,
+    19, 31, 157, 110, 133, 71,
+    7, 44, 109, 187, 20, 32,
+    57, 8, 21, 33, 45, 112,
+    58, 9, 113, 22, 188, 34,
+    46, 10, 59, 47, 23, 35,
     11, 189,
 )
 

time: 143 us -> 144 us (level)
  no operation moved by 1% of the time
where the time goes in v10:
time: 144 us; the launch traced here: 143 us
  Pallas kernels  142 us (99%)
    pallas_call x1, Pallas kernels, body(): pl.pallas_call(block_kernel, out_shape=(pltpu.VMEM((128, 1536), BF), pltp...  141 us

profile of v10, /device:TPU:0, one launch (start us, length us, event | category | flops | bytes accessed | tf_op | source)
XLA Modules:
  0.0 142.7 jit_solution(15197512073090444566)
XLA Ops:
  0.6 140.5 %block.1 = (bf16[128,1536]{1,0:T(8,128)(2,1)S(1)}, f32[128,1536]{1,0:T(8,128)S(1)}, f32[48,4608]{1,0:T(8,128)S(1)}) custom-call(bf16[128,1536]{1,0:T(8,128)(2,1)} %bitcast.25, f32[6,1,1536]{2,1,0:T(1,128)} %bitcast.30, bf16[128,1536]{1,0:T(8,128)(2,1)} %bitcast.26, bf16[3,48,384]{2,1,0:T(8,128)(2,1)} %bitcast.29, bf16[48,384]{1,0:T(8,128)(2,1)} %bitcast.31, ...), custom_call_target="tpu_custom_call" | custom-call | tf_op jit(solution)/shard_map/block/pallas_call | solution.py:890
  141.2 1.4 finish.1
